TPU v7x, 256 devices: a whole 4x4x8 slice. The times are simulated.
256 devices in a mesh: grp: 32 (over z_hi, y, core), tp: 8 (over z_lo, x).
Axes of the slice: x: 4, y: 4, z: 8 (z_hi: 4, z_lo: 2; z = z_hi * 2 + z_lo), core: 2. Of those that a mesh axis runs over, the one named last changes fastest.
Arguments:
- tokens: bfloat16 [2048, 6144], P('grp', 'tp'), may hold values from -6 to 6
- norm_gain: float32 [6144], replicated, may hold values from 0.25 to 1.75
- router_weight: bfloat16 [6144, 8], replicated, may hold values from -0.078125 to 0.078125
- expert_ids: int32 [2048, 2], P('grp'), may hold values from 0 to 7, all different within a row; in each aligned block of 64 rows (0 to 63, 64 to 127, ...) at most 18 rows name the same one
- gate_proj: bfloat16 [6144, 65536], P(None, ('grp', 'tp')), may hold values from -0.078125 to 0.078125
- up_proj: bfloat16 [6144, 65536], P(None, ('grp', 'tp')), may hold values from -0.078125 to 0.078125
- down_proj: bfloat16 [65536, 6144], P(('grp', 'tp')), may hold values from -0.25 to 0.25
Outputs:
- mixed: bfloat16 [2048, 6144], P('grp', 'tp')
Inputs may be any that keep to these rules, and one draw needn't show every extreme that they name: `expert_ids`: each row names two different experts; within the rows of one group (aligned blocks of 64 rows) no expert is named more than 18 times, and in some group one expert is named exactly 18 times.
All inputs are finite; a program needn't handle non-finite values.
Results may differ from a plain program's by a relative error of at most 0.017.
Values may be sent and summed in bfloat16 or wider, within the bound.
No kernel may reach another device: no remote copies, remote signals or barrier semaphores. Data moves between devices by JAX's collectives and lax.ppermute only.
A program may use at most 128 MiB of HBM per device.

v0:
```python
from functools import partial

import jax
import jax.numpy as jnp
from jax import lax
from jax.sharding import Mesh
from jax.sharding import PartitionSpec as P

CAP = 18
GRP = ("grp_0", "grp_1", "grp_2")
GRP_TP = ("grp_0", "grp_1", "grp_2", "tp")


epsilon = 1e-05


def copy_for_each(x, axis):
    copies = jnp.broadcast_to(x, (lax.axis_size(axis), *x.shape))
    return lax.all_to_all(copies, axis, split_axis=0, concat_axis=0, tiled=True)


def taken_together(x, axis):
    return copy_for_each(x, axis).sum(axis=0)


def in_blocks(x, dim, size):
    lengths = x.shape
    blocks = x.reshape(*lengths[:dim], size, lengths[dim] // size, *lengths[dim + 1 :])
    return jnp.moveaxis(blocks, dim, 0)


def joined_along(blocks, dim):
    blocks = jnp.moveaxis(blocks, 0, dim)
    lengths = blocks.shape
    return blocks.reshape(*lengths[:dim], lengths[dim] * lengths[dim + 1], *lengths[dim + 2 :])


def exchange_in_order(blocks, axes, order):
    inside = blocks.shape[1:]
    out = blocks.reshape(*(lax.axis_size(a) for a in axes), *inside)
    for k in order:
        out = lax.all_to_all(out, axes[k], k, k, tiled=True)
    return out.reshape(-1, *inside)


def two_step_exchange(x, groups, order, split_dim, concat_dim):
    size = lax.axis_size(groups[0]) * lax.axis_size(groups[1])
    blocks = in_blocks(x, split_dim, size)
    return joined_along(exchange_in_order(blocks, groups, order), concat_dim)


def expert_rows(gate_proj, up_proj, down_proj, gather_first, received):
    received = lax.all_gather(received, "tp", axis=2, tiled=True)
    source_groups, slot_count, feature_width = received.shape
    row_block = received.reshape(source_groups * slot_count, feature_width)
    gate_act = jnp.dot(row_block, gate_proj, preferred_element_type=jnp.float32)
    up_act = jnp.dot(row_block, up_proj, preferred_element_type=jnp.float32)
    hidden = (jax.nn.silu(gate_act) * up_act).astype(jnp.bfloat16)
    partial_out = jnp.dot(hidden, down_proj, preferred_element_type=jnp.float32).astype(
        jnp.bfloat16
    )
    partial_out = partial_out.reshape(source_groups, slot_count, feature_width)
    own_share = (
        lax.psum_scatter(partial_out, "tp", scatter_dimension=2, tiled=True)
        .astype(jnp.float32)
        .astype(jnp.bfloat16)
    )
    return lax.all_to_all(own_share, GRP, split_axis=0, concat_axis=0, tiled=True)


def per_device(tokens, norm_gain, router_weight, expert_ids, gate_proj, up_proj, down_proj):
    tok_rows, local_width = tokens.shape
    experts = router_weight.shape[1]
    groups = lax.axis_size(GRP)
    owners = groups // experts
    capacity = CAP
    local_rows = tokens.astype(jnp.float32)
    width_all = local_width * lax.axis_size("tp")
    offset_start = lax.axis_index("tp") * local_width
    gain_part = lax.dynamic_slice_in_dim(norm_gain, offset_start, local_width, 0)
    router_part = lax.dynamic_slice_in_dim(router_weight, offset_start, local_width, 0)
    squares = taken_together(jnp.sum(local_rows * local_rows, axis=-1, keepdims=True), "tp")
    normed = (local_rows * lax.rsqrt(squares / width_all + epsilon) * gain_part).astype(
        jnp.bfloat16
    )
    logits = taken_together(jnp.dot(normed, router_part, preferred_element_type=jnp.float32), "tp")
    expert_iota = jnp.arange(experts, dtype=jnp.int32)[None, :]
    chosen_first = (expert_ids[:, 0:1] == expert_iota).astype(jnp.int32)
    chosen_second = (expert_ids[:, 1:2] == expert_iota).astype(jnp.int32)
    first_logit = jnp.sum(logits * chosen_first.astype(jnp.float32), axis=-1)
    second = jnp.sum(logits * chosen_second.astype(jnp.float32), axis=-1)
    gate_first = 1.0 / (1.0 + jnp.exp(second - first_logit))
    gate_second = 1.0 / (1.0 + jnp.exp(first_logit - second))
    gate_table = gate_first[:, None] * chosen_first.astype(jnp.float32) + gate_second[
        :, None
    ] * chosen_second.astype(jnp.float32)
    routed = chosen_first + chosen_second
    slot_index = jnp.cumsum(routed, axis=0) - 1
    slot_iota = jnp.arange(capacity, dtype=jnp.int32)
    slot_picks = (slot_index.T[:, None, :] == slot_iota[None, :, None]) & (
        routed.T[:, None, :] == 1
    )
    selector = slot_picks.astype(jnp.bfloat16)
    per_expert = jnp.einsum(
        "ect,td->ecd", selector, normed, preferred_element_type=jnp.float32
    ).astype(jnp.bfloat16)
    outgoing = jnp.repeat(per_expert, owners, axis=0)
    worker = partial(expert_rows, gate_proj, up_proj, down_proj, True)
    returned = worker(two_step_exchange(outgoing, (("grp_0", "grp_1"), "grp_2"), (1, 0), 0, 0))
    summed = (
        returned.astype(jnp.float32).reshape(experts, owners, capacity, local_width).sum(axis=1)
    )
    combine = slot_picks.astype(jnp.float32) * gate_table.T[:, None, :]
    mixed = jnp.einsum("ect,ecd->td", combine, summed)
    return mixed.astype(jnp.bfloat16)


def solution(mesh):
    split = Mesh(mesh.devices.reshape(4, 4, 2, mesh.shape["tp"]), ("grp_0", "grp_1", "grp_2", "tp"))
    placed = (
        P(GRP, "tp"),
        P(),
        P(),
        P(GRP, None),
        P(None, GRP_TP),
        P(None, GRP_TP),
        P(GRP_TP, None),
    )
    return jax.shard_map(
        per_device, mesh=split, in_specs=placed, out_specs=P(GRP, "tp"), check_vma=False
    )
```

profile of v0, /device:TPU:33, one launch (start us, length us, event | category | flops | bytes accessed | tf_op | source)
XLA Modules:
  0.0 353.8 jit_solution(12286566533400413660)
XLA Ops:
  6.5 1.2 fusion.8
  7.7 0.6 broadcast_in_dim.10
  8.3 5.2 %all-to-all-start = ((f32[8,64,1]{1,2,0:T(1,128)}), f32[8,64,1]{1,2,0:T(1,128)S(1)}, u32[]{:S(2)}, u32[]{:S(2)}) async-start(f32[8,64,1]{1,2,0:T(1,128)} %broadcast_in_dim.10), calls=%async_computation | async-start | bytes 8192 | tf_op jit(solution)/shard_map/all_to_all | solution.py:19
  13.5 0.8 slice_bitcast_fusion.1
  14.5 0.8 dynamic_slice.6
  15.3 2.0 all-to-all-done
  17.3 1.2 convolution_convert_fusion.1
  18.6 1.0 broadcast_in_dim.24
  19.6 1.9 broadcast_in_dim.25
  21.5 1.1 broadcast_in_dim.26
  22.6 6.2 %all_to_all.25 = bf16[16,2,1,18,768]{4,0,3,2,1:T(8,128)(2,1)S(1)} all-to-all(bf16[16,2,1,18,768]{4,0,3,2,1:T(8,128)(2,1)S(1)} %broadcast_in_dim.26), channel_id=1, replica_groups=mesh['grp_0'=4,'grp_1'=4,'grp_2'=2,'tp'=8] {'grp_2'}, dimensions={1} | all-to-all | bytes 1769472 | tf_op jit(solution)/shard_map/all_to_all | solution.py:42
  28.7 0.9 copy.23
  29.7 29.7 %all_to_all.26 = bf16[16,2,1,18,768]{4,1,3,2,0:T(2,128)(2,1)S(1)} all-to-all(bf16[16,2,1,18,768]{4,1,3,2,0:T(2,128)(2,1)S(1)} %copy.23), channel_id=1, replica_groups=mesh['grp_0'=4,'grp_1'=4,'grp_2'=2,'tp'=8] {'grp_0','grp_1'}, dimensions={0} | all-to-all | bytes 1769472 | tf_op jit(solution)/shard_map/all_to_all | solution.py:42
  59.4 1.8 copy.24
  61.2 3.1 reshape_reshape.3
  64.4 82.4 %all-gather.2.cloned.1.call-done = bf16[32,18,6144]{2,0,1:T(8,128)(2,1)} async-done(((bf16[32,18,768]{2,0,1:T(8,128)(2,1)}), bf16[32,18,6144]{2,0,1:T(8,128)(2,1)}) %all-gather.2.cloned.1.call-update) | async-done | bytes 7077904 | tf_op jit(solution)/shard_map/all_gather | solution.py:53
  146.8 10.7 %copy.25 = bf16[32,18,6144]{2,1,0:T(8,128)(2,1)} copy(bf16[32,18,6144]{2,0,1:T(8,128)(2,1)} %all-gather.2.cloned.1.call-done) | data formatting | bytes 14155776 | tf_op jit(solution)/shard_map/all_gather | solution.py:53
  157.5 9.6 %reshape.146 = bf16[576,6144]{1,0:T(8,128)(2,1)} reshape(bf16[32,18,6144]{2,1,0:T(8,128)(2,1)} %copy.25) | data formatting | bytes 14155776 | tf_op jit(solution)/shard_map/reshape | solution.py:55
  167.1 6.7 %fusion.37 = f32[576,256]{1,0:T(8,128)} fusion(bf16[576,6144]{1,0:T(8,128)(2,1)} %reshape.146, bf16[6144,256]{1,0:T(8,128)(2,1)} %param.11), kind=kOutput, calls=%fused_computation.59 | convolution fusion | flops 1811939328 | bytes 10813440 | tf_op jit(solution)/shard_map/dot_general | solution.py:56
  173.8 14.3 %convolution_convert_fusion = bf16[576,6144]{1,0:T(8,128)(2,1)} fusion(bf16[256,6144]{1,0:T(8,128)(2,1)S(1)} %copy-done, bf16[576,6144]{1,0:T(8,128)(2,1)} %reshape.146, bf16[6144,256]{1,0:T(8,128)(2,1)} %param.12, f32[576,256]{1,0:T(8,128)} %fusion.37), kind=kOutput, calls=%fused_computation | convolution fusion | flops 3628302336 | bytes 21037056 | tf_op jit(solution)/shard_map/dot_general | solution.py:59
  188.2 9.5 %reshape.147 = bf16[32,18,6144]{2,1,0:T(8,128)(2,1)} reshape(bf16[576,6144]{1,0:T(8,128)(2,1)} %convolution_convert_fusion) | data formatting | bytes 14155776 | tf_op jit(solution)/shard_map/reshape | solution.py:62
  197.7 0.9 copy-done.1
  198.6 0.9 fusion.23
  199.5 0.1 reshape.154
  199.6 7.5 %all_to_all.27 = f32[8,1,512]{2,1,0:T(1,128)S(1)} all-to-all(f32[8,1,512]{2,1,0:T(1,128)S(1)} %reshape.154), channel_id=1, replica_groups=mesh['grp_0'=4,'grp_1'=4,'grp_2'=2,'tp'=8] {'tp'}, dimensions={0} | all-to-all | bytes 32768 | tf_op jit(solution)/shard_map/all_to_all | solution.py:19
  207.1 94.8 %reduce-scatter.2.cloned.1.call-done = bf16[32,18,768]{2,1,0:T(8,128)(2,1)} async-done(((bf16[32,18,6144]{2,1,0:T(8,128)(2,1)}), bf16[32,18,768]{2,1,0:T(8,128)(2,1)}) %reduce-scatter.2.cloned.1.call-update) | async-done | bytes 884752 | tf_op jit(solution)/shard_map/reduce_scatter | solution.py:64
  301.9 10.4 %all-to-all-start.4 = ((bf16[32,18,768]{2,1,0:T(8,128)(2,1)}), bf16[32,18,768]{2,1,0:T(8,128)(2,1)}, u32[]{:S(2)}, u32[]{:S(2)}) async-start(bf16[32,18,768]{2,1,0:T(8,128)(2,1)} %reduce-scatter.2.cloned.1.call-done), calls=%async_computation.5 | async-start | bytes 2359296 | tf_op jit(solution)/shard_map/all_to_all | solution.py:68
  312.3 0.5 broadcast.113
  312.8 0.7 reduce.1
  313.6 30.9 %all-to-all-done.4 = bf16[32,18,768]{2,1,0:T(8,128)(2,1)} async-done(((bf16[32,18,768]{2,1,0:T(8,128)(2,1)}), bf16[32,18,768]{2,1,0:T(8,128)(2,1)}, u32[]{:S(2)}, u32[]{:S(2)}) %all-to-all-start.4) | async-done | bytes 884768 | tf_op jit(solution)/shard_map/all_to_all | solution.py:68
  344.6 1.5 convert_reduce_fusion
  346.0 0.9 fusion.1
  (22 shorter events, 0.6 us)
Async XLA Ops:
  6.5 167.3 %copy-start = (bf16[256,6144]{1,0:T(8,128)(2,1)S(1)}, bf16[256,6144]{1,0:T(8,128)(2,1)}, u32[]{:S(2)}) copy-start(bf16[256,6144]{1,0:T(8,128)(2,1)} %param.13) | copy-start | bytes 9437188
  8.3 9.0 %all-to-all-start = ((f32[8,64,1]{1,2,0:T(1,128)}), f32[8,64,1]{1,2,0:T(1,128)S(1)}, u32[]{:S(2)}, u32[]{:S(2)}) async-start(f32[8,64,1]{1,2,0:T(1,128)} %broadcast_in_dim.10), calls=%async_computation | async-start | bytes 8192 | tf_op jit(solution)/shard_map/all_to_all | solution.py:19
  13.5 133.3 %all-gather.2.cloned.1.call-start = ((), (), s32[]{:S(2)}) async-start(), calls=%async_computation.6 | async-start | bytes 7962624 | tf_op jit(solution)/shard_map/all_gather | solution.py:53
  64.4 237.5 %reduce-scatter.2.cloned.1.call-start = ((), (), s32[]{:S(2)}) async-start(), calls=%async_computation.7 | async-start | bytes 10616832 | tf_op jit(solution)/shard_map/reduce_scatter | solution.py:64
  197.7 0.9 copy-start.1
  301.9 42.7 %all-to-all-start.4 = ((bf16[32,18,768]{2,1,0:T(8,128)(2,1)}), bf16[32,18,768]{2,1,0:T(8,128)(2,1)}, u32[]{:S(2)}, u32[]{:S(2)}) async-start(bf16[32,18,768]{2,1,0:T(8,128)(2,1)} %reduce-scatter.2.cloned.1.call-done), calls=%async_computation.5 | async-start | bytes 2359296 | tf_op jit(solution)/shard_map/all_to_all | solution.py:68
Sparse Core Ops, SparseCore 0:
  64.5 82.2 all-gather.1
  197.8 104.0 reduce-scatter.1
where the time goes:
time: 355 us; the launch traced here: 354 us
  waiting for transfers between devices  210 us (59%)
  local copies, waits for them, and re-layouts  43.6 us (12%)
  blocking collectives  43.4 us (12%)
  matrix products  24 us (7%)
  starting transfers between devices  15.6 us (4%)
  between operations  13.5 us (4%)
    reduce_scatter x1, waiting for transfers between devices, expert_rows(): lax.psum_scatter(partial_out, 'tp', scatter_dimension=2, tiled=True)  94.8 us
    all_gather x1, waiting for transfers between devices, expert_rows(): received = lax.all_gather(received, 'tp', axis=2, tiled=True)  82.4 us
    all_to_all x2, blocking collectives, exchange_in_order(): out = lax.all_to_all(out, axes[k], k, k, tiled=True)  35.9 us
    all_to_all x1, waiting for transfers between devices, expert_rows(): lax.all_to_all(own_share, GRP, split_axis=0, concat_axis=0, tiled=True)  30.9 us
    dot_general x1, matrix products, expert_rows(): jnp.dot(hidden, down_proj, preferred_element_type=jnp.float32)  14.3 us
    all_gather x1, local copies, waits for them, and re-layouts, expert_rows(): received = lax.all_gather(received, 'tp', axis=2, tiled=True)  10.7 us
    all_to_all x1, starting transfers between devices, expert_rows(): lax.all_to_all(own_share, GRP, split_axis=0, concat_axis=0, tiled=True)  10.4 us
    reshape x1, local copies, waits for them, and re-layouts, expert_rows(): row_block = received.reshape(source_groups * slot_count, feature_width)  9.63 us
  transfers between devices with their start and end apart: 4, of which 4 were waited for; matrix products, arithmetic and copies ran while one was open for 1% of the time, Pallas kernels for 0%

commit v1 on v0

v1 whole, which is shorter than its diff:
```python
from functools import partial

import jax
import jax.numpy as jnp
from jax import lax
from jax.experimental import pallas as pl
from jax.experimental.pallas import tpu as pltpu
from jax.sharding import Mesh
from jax.sharding import PartitionSpec as P


AXES = ("zh", "y2", "y1", "c", "zl", "x")
SIZES = (4, 2, 2, 2, 2, 4)
GRP = ("zh", "y2", "y1", "c")
TP = ("zl", "x")
OWNER = ("y1", "c", "zl", "x")
CAP = 18
FAR = 4
KEPT = FAR * CAP
ROWS = 2 * KEPT
EXTRA = 8
BLOCK = 40
EPSILON = 1e-05
F32 = jnp.float32
BF16 = jnp.bfloat16


def place(y, z, x, step):
    if step == "x+":
        return y, z, (x + 1) % 4
    if step == "x-":
        return y, z, (x - 1) % 4
    if step == "xx":
        return y, z, (x + 2) % 4
    if step == "y":
        return 1 - y, z, x
    if step == "z":
        return y, 1 - z, x
    return 1 - y, 1 - z, x


def owner_pairs(step_core0, step_core1):
    pairs = []
    for y in range(2):
        for core, step in enumerate((step_core0, step_core1)):
            for z in range(2):
                for x in range(4):
                    y_to, z_to, x_to = place(y, z, x, step)
                    source = ((y * 2 + core) * 2 + z) * 4 + x
                    target = ((y_to * 2 + core) * 2 + z_to) * 4 + x_to
                    pairs.append((source, target))
    return pairs


def hop(value, step_core0, step_core1):
    return lax.ppermute(value, OWNER, owner_pairs(step_core0, step_core1))


def along_z(value, distance):
    return lax.ppermute(value, "zh", [(i, (i + distance) % FAR) for i in range(FAR)])


def across_y(value):
    return lax.ppermute(value, ("y2", "y1"), [(i, 3 - i) for i in range(4)])


def other_core(value):
    return lax.ppermute(value, "c", [(0, 1), (1, 0)])


def vmem(count):
    return [pl.BlockSpec(memory_space=pltpu.VMEM)] * count


def hbm(count):
    return [pl.BlockSpec(memory_space=pltpu.HBM)] * count


def small(kernel, outs, *operands):
    return pl.pallas_call(
        kernel,
        out_shape=[jax.ShapeDtypeStruct(shape, BF16) for shape in outs],
        in_specs=vmem(len(operands)),
        out_specs=vmem(len(outs)),
        compiler_params=pltpu.CompilerParams(vmem_limit_bytes=4 << 20),
    )(*operands)


def moved(shape, source_of, *blocks):
    joined = jnp.concatenate([b[...] for b in blocks], axis=0)
    row = lax.broadcasted_iota(jnp.int32, (shape[0], joined.shape[0]), 0)
    column = lax.broadcasted_iota(jnp.int32, (shape[0], joined.shape[0]), 1)
    source, valid = source_of(row)
    picks = jnp.where((source == column) & valid, 1.0, 0.0).astype(BF16)
    return jnp.dot(picks, joined, preferred_element_type=F32)


def slots_of(ids):
    tokens = ids.shape[1]
    slot = lax.broadcasted_iota(jnp.int32, (ROWS, tokens), 0)
    k = (slot * 3641) >> 16
    inside = slot - k * CAP
    zh, y2 = lax.axis_index("zh"), lax.axis_index("y2")
    expert = ((zh + k) & 3) * 2 + (y2 ^ (k >> 2))
    first, second = ids[0:1, :] == expert, ids[1:2, :] == expert
    routed = jnp.where(first | second, 1.0, 0.0).astype(BF16)
    earlier = lax.broadcasted_iota(jnp.int32, (tokens, tokens), 0) < lax.broadcasted_iota(
        jnp.int32, (tokens, tokens), 1
    )
    before = jnp.dot(
        routed, jnp.where(earlier, 1.0, 0.0).astype(BF16), preferred_element_type=F32
    )
    here = before == inside.astype(F32)
    return first & here, second & here


def select_kernel(ids_ref, tokens_ref, keep_ref, send_ref):
    first, second = slots_of(ids_ref[...])
    picks = jnp.where(first | second, 1.0, 0.0).astype(BF16)
    chosen = jnp.dot(picks, tokens_ref[...], preferred_element_type=F32).astype(BF16)
    keep_ref[...] = chosen[:KEPT]
    send_ref[...] = chosen[KEPT:]


def in_blocks(row):
    block = (row * 1639) >> 16
    inside = row - block * BLOCK
    half = jnp.where(inside < CAP, 0, 1)
    return block, inside, half


def shuffle_kernel(keep_ref, came_ref, *out_refs):
    def source_of(row):
        block, inside, half = in_blocks(row)
        return half * KEPT + block * CAP + inside - half * CAP, inside < 2 * CAP

    rows = moved((FAR * BLOCK, 0), source_of, keep_ref, came_ref)
    for k, out in enumerate(out_refs):
        out[...] = rows[k * BLOCK : (k + 1) * BLOCK].astype(BF16)


def pack_kernel(*refs):
    *blocks, sums_ref, out_ref = refs

    def source_of(row):
        block = (row * 1821) >> 16
        return block * BLOCK + row - block * 2 * CAP, row >= 0

    out_ref[:ROWS] = moved((ROWS, 0), source_of, *blocks).astype(BF16)
    out_ref[ROWS:] = sums_ref[...]


def unpack_kernel(*refs):
    terms, out_refs = refs[:FAR], refs[FAR:]
    total = sum(t[...].astype(F32) for t in terms).astype(BF16)

    def source_of(row):
        block, inside, _ = in_blocks(row)
        return block * 2 * CAP + inside, inside < 2 * CAP

    rows = moved((FAR * BLOCK, 0), source_of, total)
    for k, out in enumerate(out_refs):
        out[...] = rows[k * BLOCK : (k + 1) * BLOCK].astype(BF16)


def unshuffle_kernel(*refs):
    blocks, (keep_ref, send_ref) = refs[:FAR], refs[FAR:]

    def source_of(row):
        k = (row * 3641) >> 16
        return (k & 3) * BLOCK + (k >> 2) * CAP + row - k * CAP, row >= 0

    rows = moved((ROWS, 0), source_of, *blocks).astype(BF16)
    keep_ref[...] = rows[:KEPT]
    send_ref[...] = rows[KEPT:]


def transposed_dot(left, right):
    return lax.dot_general(left, right, (((1,), (1,)), ((), ())), preferred_element_type=F32)


def halves(value):
    high = value.astype(BF16)
    return high, (value - high.astype(F32)).astype(BF16)


def stats_kernel(tokens_ref, gain_ref, router_ref, out_ref):
    tokens, width = tokens_ref.shape
    part = lax.axis_index("zl") * 4 + lax.axis_index("x")
    here = pl.ds(pl.multiple_of(part * width, width), width)
    values = tokens_ref[...].astype(F32)
    router = router_ref[:, here]
    ones = jnp.ones_like(router)
    scaled, squares = halves(values * gain_ref[:, here]), halves(values * values)
    out_ref[...] = jnp.zeros_like(out_ref)
    for n, (left, terms) in enumerate(((router, scaled), (ones, squares))):
        for k, v in enumerate(halves(sum(transposed_dot(left, t) for t in terms))):
            start = (2 * n + k) * 128
            out_ref[:, start : start + tokens] = v


def stats_in(tile, tokens):
    parts = [tile[ROWS:, n * 128 : n * 128 + tokens].astype(F32) for n in range(4)]
    return parts[0] + parts[1], parts[2] + parts[3]


def combine_kernel(width_all, ids_ref, sums_ref, keep_ref, came_ref, out_ref):
    ids = ids_ref[...]
    sums = sums_ref[...]
    experts = sums.shape[0] // 2
    scale = lax.rsqrt(sums[experts : experts + 1] / width_all + EPSILON)
    named = lax.broadcasted_iota(jnp.int32, (experts, ids.shape[1]), 0)
    logits = [
        jnp.sum(jnp.where(named == ids[k : k + 1], sums[:experts], 0.0), axis=0, keepdims=True)
        * scale
        for k in (0, 1)
    ]
    gate_first = 1.0 / (1.0 + jnp.exp(logits[1] - logits[0]))
    gate_second = 1.0 / (1.0 + jnp.exp(logits[0] - logits[1]))
    first, second = slots_of(ids)
    weights = jnp.where(first, gate_first, 0.0) + jnp.where(second, gate_second, 0.0)
    rows = jnp.concatenate([keep_ref[...], came_ref[...]], axis=0)
    out_ref[...] = sum(
        lax.dot_general(w, rows, (((0,), (0,)), ((), ())), preferred_element_type=F32)
        for w in halves(weights)
    ).astype(BF16)


def offset_place(square, ring):
    step = jnp.where(ring == 1, 3, jnp.where(ring == 2, 1, jnp.where(ring == 3, 2, 0)))
    feature = (lax.axis_index("zl") ^ (square >> 1)) * 4 + ((lax.axis_index("x") + step) & 3)
    return square & 1, feature


def tile_place(outer, inner):
    core = lax.axis_index("c")
    return offset_place(jnp.where(core == 0, outer, inner), jnp.where(core == 0, inner, outer))


CHUNK = 16


def in_hbm(*arrays):
    return [pltpu.with_memory_space_constraint(a, pltpu.HBM) for a in arrays]


def hidden_kernel(width_all, gain_ref, *refs):
    tiles, others, owns = refs[:16], refs[16:18], refs[18:20]
    out_ref, sums_ref, x_ref, w_ref, squares_ref, sems = refs[20:]
    copies = [pltpu.make_async_copy(w, w_ref.at[n], sems.at[n]) for n, w in enumerate(owns)]
    for copy in copies:
        copy.start()
    rows, width = ROWS, tiles[0].shape[1]
    slices = w_ref.shape[2]
    experts, tokens = sums_ref.shape[0] // 2, sums_ref.shape[1]
    squares_ref[...] = jnp.zeros_like(squares_ref)
    sums_ref[...] = jnp.zeros_like(sums_ref)
    for index, tile in enumerate(tiles):
        row_class, feature = tile_place(index // 4, index % 4)
        column_at = pl.ds(pl.multiple_of(feature * width, width), width)
        gain = gain_ref[:, column_at]

        def prepare(n, _, tile=tile, row_class=row_class, column_at=column_at, gain=gain):
            row_at = pl.ds(pl.multiple_of(row_class * rows + n * CHUNK, CHUNK), CHUNK)
            values = tile[pl.ds(pl.multiple_of(n * CHUNK, CHUNK), CHUNK), :].astype(F32)
            x_ref[row_at, column_at] = (values * gain).astype(BF16)
            square = values * values
            squares_ref[row_at, :] += sum(
                square[:, j * 128 : (j + 1) * 128] for j in range(width // 128)
            )
            return 0

        lax.fori_loop(0, rows // CHUNK, prepare, 0)
        own = jnp.where(row_class == 0, 1.0, 0.0)
        logits, squares = stats_in(tile, tokens)
        sums_ref[:experts] += logits * own
        sums_ref[experts:] += squares * own
    scale = lax.rsqrt(jnp.sum(squares_ref[...], axis=1, keepdims=True) / width_all + EPSILON)

    def give(start, gate_weight, up_weight):
        gate = jnp.dot(x_ref[...], gate_weight[...], preferred_element_type=F32) * scale
        up = jnp.dot(x_ref[...], up_weight[...], preferred_element_type=F32) * scale
        out_ref[:, start : start + slices] = (gate * (1.0 / (1.0 + jnp.exp(-gate))) * up).astype(
            BF16
        )

    give(slices, *others)
    for copy in copies:
        copy.wait()
    give(0, w_ref.at[0], w_ref.at[1])


def hidden_of(gain, tiles, others, owns, sums_shape):
    rows = ROWS
    width_all, slices = owns[0].shape
    return pl.pallas_call(
        partial(hidden_kernel, width_all),
        out_shape=[
            jax.ShapeDtypeStruct((2 * rows, 2 * slices), BF16),
            jax.ShapeDtypeStruct(sums_shape, F32),
        ],
        in_specs=vmem(19) + hbm(2),
        out_specs=vmem(2),
        scratch_shapes=[
            pltpu.VMEM((2 * rows, width_all), BF16),
            pltpu.VMEM((2, width_all, slices), BF16),
            pltpu.VMEM((2 * rows, 128), F32),
            pltpu.SemaphoreType.DMA((2,)),
        ],
        compiler_params=pltpu.CompilerParams(vmem_limit_bytes=20 << 20),
        cost_estimate=pl.CostEstimate(
            flops=2 * 2 * rows * width_all * 4 * slices,
            bytes_accessed=4 * width_all * slices * 2,
            transcendentals=0,
        ),
        name="hidden",
    )(gain, *tiles, *others, *in_hbm(*owns))


def down_kernel(places, hidden_ref, own_ref, other_ref, *refs):
    out_refs, y_ref = refs[:-1], refs[-1]
    slices = own_ref.shape[0]
    rows, width = y_ref.shape[1] // 2, y_ref.shape[2]

    def step(n, _):
        _, feature = offset_place((n >> 2) * 2, n & 3)
        column_at = pl.ds(pl.multiple_of(feature * width, width), width)
        y_ref[n] = (
            jnp.dot(hidden_ref[:, :slices], own_ref[:, column_at], preferred_element_type=F32)
            + jnp.dot(hidden_ref[:, slices:], other_ref[:, column_at], preferred_element_type=F32)
        ).astype(BF16)
        return 0

    lax.fori_loop(0, 8, step, 0)
    core = lax.axis_index("c")

    def give(which):
        for n in range(8):
            for row_class in range(2):
                square, ring = (n >> 2) * 2 + row_class, n & 3
                outer, inner = (square, ring) if which == 0 else (ring, square)
                at, start = places[outer * 4 + inner]
                out_refs[at][start : start + rows, :] = y_ref[
                    n, row_class * rows : (row_class + 1) * rows, :
                ]

    @pl.when(core == 0)
    def _():
        give(0)

    @pl.when(core == 1)
    def _():
        give(1)


def down_of(shapes, places, hidden, own, other):
    slices, width_all = own.shape
    width = width_all // 8
    return pl.pallas_call(
        partial(down_kernel, places),
        out_shape=[jax.ShapeDtypeStruct((rows, width), BF16) for rows in shapes],
        in_specs=vmem(3),
        out_specs=vmem(len(shapes)),
        scratch_shapes=[pltpu.VMEM((8, hidden.shape[0], width), BF16)],
        compiler_params=pltpu.CompilerParams(vmem_limit_bytes=20 << 20),
        cost_estimate=pl.CostEstimate(
            flops=2 * hidden.shape[0] * width_all * 2 * slices,
            bytes_accessed=2 * slices * width_all * 2,
            transcendentals=0,
        ),
        name="down",
    )(hidden, own, other)


def added_kernel(starts, *refs):
    *terms, out_ref = refs
    rows = out_ref.shape[0]
    out_ref[...] = sum(t[n : n + rows, :].astype(F32) for t, n in zip(terms, starts)).astype(BF16)


def added(*terms):
    terms = [t if isinstance(t, tuple) else (t, 0) for t in terms]
    (out,) = small(
        partial(added_kernel, [n for _, n in terms]),
        [(ROWS, terms[0][0].shape[1])],
        *(t for t, _ in terms),
    )
    return out


def per_device(tokens, norm_gain, router_weight, expert_ids, gate_proj, up_proj, down_proj):
    width_all = router_weight.shape[0]
    width = tokens.shape[1]
    gain = norm_gain.reshape(1, width_all)
    ids = expert_ids.T
    kept, block = (KEPT, width), (BLOCK, width)

    keep, send = small(select_kernel, [kept, kept], ids, tokens)
    came = across_y(send)
    blocks = small(shuffle_kernel, [block] * FAR, keep, came)
    arrived = [blocks[0]] + [along_z(blocks[k], k) for k in (1, 2, 3)]
    gate_other = other_core(gate_proj)
    up_other = other_core(up_proj)
    down_other = other_core(down_proj)
    (part_sums,) = small(stats_kernel, [(EXTRA, width)], tokens, gain, router_weight.T)
    (mine,) = small(pack_kernel, [(ROWS + EXTRA, width)], *arrived, part_sums)

    inner = [mine, hop(mine, "x+", "y"), hop(mine, "x-", "z"), hop(mine, "xx", "yz")]
    outer = [inner, [], [], [None] * 4]
    for a in range(4):
        outer[1].append(hop(inner[a], "y", "x+"))
        outer[2].append(hop(inner[a], "z", "x-"))
    for a in (0, 1):
        outer[3][a] = hop(outer[1][a], "z", "x+")
    for a in (2, 3):
        outer[3][a] = hop(outer[2][a], "y", "x-")
    tiles = [outer[m][a] for m in range(4) for a in range(4)]
    sums_shape = (2 * router_weight.shape[1], tokens.shape[0])
    hidden, sums = hidden_of(
        gain, tiles, (gate_other, up_other), (gate_proj, up_proj), sums_shape
    )

    shapes = [ROWS] * 12 + [2 * ROWS] * 2
    places = {4 * 0 + a: (a, 0) for a in range(4)}
    places |= {4 * 3 + a: (4 + a, 0) for a in range(4)}
    places |= {4 * 1 + 0: (8, 0), 4 * 1 + 1: (9, 0), 4 * 2 + 2: (10, 0), 4 * 2 + 3: (11, 0)}
    places |= {4 * 1 + 2: (12, 0), 4 * 1 + 3: (12, ROWS), 4 * 2 + 0: (13, 0), 4 * 2 + 1: (13, ROWS)}
    part = down_of(shapes, places, hidden, down_proj, down_other)
    own, far, near, pairs = part[:4], part[4:8], part[8:12], part[12:]
    ways = [("z", "x-"), ("z", "x-"), ("y", "x+"), ("y", "x+")]
    far_in = [hop(far[n], *ways[n]) for n in range(4)]
    first = hop(pairs[0], "y", "x-")
    second = hop(pairs[1], "z", "x+")
    ways = [("y", "x-"), ("y", "x-"), ("z", "x+"), ("z", "x+")]
    near_in = [hop(added(near[n], far_in[n]), *ways[n]) for n in range(4)]
    in_pairs = [(second, 0), (second, ROWS), (first, 0), (first, ROWS)]
    total = [added(own[n], near_in[n], in_pairs[n]) for n in range(4)]
    terms = [
        total[0], hop(total[1], "x-", "y"), hop(total[2], "x+", "z"), hop(total[3], "xx", "yz")
    ]
    blocks = small(unpack_kernel, [block] * FAR, *terms)
    back = [blocks[0]] + [along_z(blocks[k], FAR - k) for k in (1, 2, 3)]
    keep, send = small(unshuffle_kernel, [kept, kept], *back)
    came = across_y(send)
    return pl.pallas_call(
        partial(combine_kernel, width_all),
        out_shape=jax.ShapeDtypeStruct(tokens.shape, BF16),
        in_specs=vmem(4),
        out_specs=vmem(1)[0],
        compiler_params=pltpu.CompilerParams(vmem_limit_bytes=4 << 20),
        name="combine",
    )(ids, sums, keep, came)


def solution(mesh):
    cut = Mesh(mesh.devices.reshape(SIZES), AXES)
    split = GRP + TP
    placed = (
        P(GRP, TP),
        P(),
        P(),
        P(GRP, None),
        P(None, split),
        P(None, split),
        P(split, None),
    )

    return jax.shard_map(per_device, mesh=cut, in_specs=placed, out_specs=P(GRP, TP), check_vma=False)
```

time: 355 us -> 148 us (0.42)
  the two profiles are of different devices: /device:TPU:33 before, /device:TPU:24 now
where the time goes in v1:
time: 148 us; the launch traced here: 147 us
  waiting for transfers between devices  66.1 us (45%)
  starting transfers between devices  62.7 us (42%)
  Pallas kernels  13.4 us (9%)
  local copies, waits for them, and re-layouts  4.84 us (3%)
    ppermute x28, waiting for transfers between devices, hop(): return lax.ppermute(value, OWNER, owner_pairs(step_core0, step_core1))  51.1 us
    ppermute x28, starting transfers between devices, hop(): return lax.ppermute(value, OWNER, owner_pairs(step_core0, step_core1))  37.7 us
    ppermute x6, starting transfers between devices, along_z(): lax.ppermute(value, 'zh', [(i, (i + distance) % FAR) for i in range(FAR)])  21.8 us
    ppermute x2, waiting for transfers between devices, across_y(): return lax.ppermute(value, ('y2', 'y1'), [(i, 3 - i) for i in range(4)])  10.1 us
    pallas_call x1, Pallas kernels, hidden_of(): pl.pallas_call(partial(hidden_kernel, width_all), out_shape=[jax.ShapeDty...  6.71 us
    ppermute x6, waiting for transfers between devices, along_z(): lax.ppermute(value, 'zh', [(i, (i + distance) % FAR) for i in range(FAR)])  4.87 us
    unnamed x16, local copies, waits for them, and re-layouts  4.84 us
    pallas_call x1, Pallas kernels, down_of(): pl.pallas_call(partial(down_kernel, places), out_shape=[jax.ShapeDtypeStr...  3.56 us
  transfers between devices with their start and end apart: 39, of which 22 were waited for; matrix products, arithmetic and copies ran while one was open for 0% of the time, Pallas kernels for 6%

profile of v1, /device:TPU:24, one launch (start us, length us, event | category | flops | bytes accessed | tf_op | source)
XLA Modules:
  0.0 147.2 jit_solution(12307763235725686030)
XLA Ops:
  4.4 4.8 %collective-permute-done.came_ref = bf16[72,768]{1,0:T(8,128)(2,1)S(1)} collective-permute-done((bf16[72,768]{1,0:T(8,128)(2,1)S(1)}, bf16[72,768]{1,0:T(8,128)(2,1)S(1)}, u32[]{:S(2)}, u32[]{:S(2)}) %collective-permute-start) | collective-permute-done | bytes 110624 | tf_op jit(solution)/shard_map/ppermute | solution.py:64
  9.4 3.3 %collective-permute-start.1 = (bf16[40,768]{1,0:T(8,128)(2,1)S(1)}, bf16[40,768]{1,0:T(8,128)(2,1)S(1)}, u32[]{:S(2)}, u32[]{:S(2)}) collective-permute-start(bf16[40,768]{1,0:T(8,128)(2,1)S(1)} %get-tuple-element.36), channel_id=1, source_target_pairs={{0,64},{64,128},{128,192},{192,0},{1,65},{65,129},{129,193},{193,1... | collective-permute-start | bytes 184328 | tf_op jit(solution)/shard_map/ppermute | solution.py:60
  12.8 5.4 %collective-permute-start.2 = (bf16[40,768]{1,0:T(8,128)(2,1)S(1)}, bf16[40,768]{1,0:T(8,128)(2,1)S(1)}, u32[]{:S(2)}, u32[]{:S(2)}) collective-permute-start(bf16[40,768]{1,0:T(8,128)(2,1)S(1)} %get-tuple-element.37), channel_id=1, source_target_pairs={{0,128},{64,192},{128,0},{192,64},{1,129},{65,193},{129,1},{193,65... | collective-permute-start | bytes 184328 | tf_op jit(solution)/shard_map/ppermute | solution.py:60
  18.2 3.6 %collective-permute-start.3 = (bf16[40,768]{1,0:T(8,128)(2,1)S(1)}, bf16[40,768]{1,0:T(8,128)(2,1)S(1)}, u32[]{:S(2)}, u32[]{:S(2)}) collective-permute-start(bf16[40,768]{1,0:T(8,128)(2,1)S(1)} %get-tuple-element.38), channel_id=1, source_target_pairs={{0,192},{64,0},{128,64},{192,128},{1,193},{65,1},{129,65},{193,129... | collective-permute-start | bytes 184328 | tf_op jit(solution)/shard_map/ppermute | solution.py:60
  24.7 2.6 %collective-permute-start.11 = (bf16[152,768]{1,0:T(8,128)(2,1)S(1)}, bf16[152,768]{1,0:T(8,128)(2,1)S(1)}, u32[]{:S(2)}, u32[]{:S(2)}) collective-permute-start(bf16[152,768]{1,0:T(8,128)(2,1)S(1)} %shard_map.76.refs_0_), channel_id=1, source_target_pairs={{0,4},{1,5},{2,6},{3,7},{4,0},{5,1},{6,2},{7,3},{8,11},{9,8},{10,9... | collective-permute-start | bytes 700424 | tf_op jit(solution)/shard_map/ppermute | solution.py:56
  27.3 4.5 %collective-permute-done.11.refs_8_ = bf16[152,768]{1,0:T(8,128)(2,1)S(1)} collective-permute-done((bf16[152,768]{1,0:T(8,128)(2,1)S(1)}, bf16[152,768]{1,0:T(8,128)(2,1)S(1)}, u32[]{:S(2)}, u32[]{:S(2)}) %collective-permute-start.11) | collective-permute-done | bytes 233504 | tf_op jit(solution)/shard_map/ppermute | solution.py:56
  31.8 3.3 %collective-permute-start.6 = (bf16[152,768]{1,0:T(8,128)(2,1)S(1)}, bf16[152,768]{1,0:T(8,128)(2,1)S(1)}, u32[]{:S(2)}, u32[]{:S(2)}) collective-permute-start(bf16[152,768]{1,0:T(8,128)(2,1)S(1)} %shard_map.76.refs_0_), channel_id=1, source_target_pairs={{0,2},{1,3},{2,0},{3,1},{4,6},{5,7},{6,4},{7,5},{8,28},{9,29},{10,... | collective-permute-start | bytes 700424 | tf_op jit(solution)/shard_map/ppermute | solution.py:56
  36.2 3.1 %collective-permute-done.6.refs_3_ = bf16[152,768]{1,0:T(8,128)(2,1)S(1)} collective-permute-done((bf16[152,768]{1,0:T(8,128)(2,1)S(1)}, bf16[152,768]{1,0:T(8,128)(2,1)S(1)}, u32[]{:S(2)}, u32[]{:S(2)}) %collective-permute-start.6) | collective-permute-done | bytes 233504 | tf_op jit(solution)/shard_map/ppermute | solution.py:56
  43.8 2.9 %collective-permute-done.4.refs_1_ = bf16[152,768]{1,0:T(8,128)(2,1)S(1)} collective-permute-done((bf16[152,768]{1,0:T(8,128)(2,1)S(1)}, bf16[152,768]{1,0:T(8,128)(2,1)S(1)}, u32[]{:S(2)}, u32[]{:S(2)}) %collective-permute-start.4) | collective-permute-done | bytes 233504 | tf_op jit(solution)/shard_map/ppermute | solution.py:56
  46.7 4.0 %collective-permute-start.14 = (bf16[152,768]{1,0:T(8,128)(2,1)S(1)}, bf16[152,768]{1,0:T(8,128)(2,1)S(1)}, u32[]{:S(2)}, u32[]{:S(2)}) collective-permute-start(bf16[152,768]{1,0:T(8,128)(2,1)S(1)} %collective-permute-done.6.refs_3_), channel_id=1, source_target_pairs={{0,4},{1,5},{2,6},{3,7},{4,0},{5,1},{6,2},{7,3},{8,11},{9,8},{10,9... | collective-permute-start | bytes 700424 | tf_op jit(solution)/shard_map/ppermute | solution.py:56
  50.7 4.0 %collective-permute-done.14.refs_11_ = bf16[152,768]{1,0:T(8,128)(2,1)S(1)} collective-permute-done((bf16[152,768]{1,0:T(8,128)(2,1)S(1)}, bf16[152,768]{1,0:T(8,128)(2,1)S(1)}, u32[]{:S(2)}, u32[]{:S(2)}) %collective-permute-start.14) | collective-permute-done | bytes 233504 | tf_op jit(solution)/shard_map/ppermute | solution.py:56
  54.7 2.0 %collective-permute-start.13 = (bf16[152,768]{1,0:T(8,128)(2,1)S(1)}, bf16[152,768]{1,0:T(8,128)(2,1)S(1)}, u32[]{:S(2)}, u32[]{:S(2)}) collective-permute-start(bf16[152,768]{1,0:T(8,128)(2,1)S(1)} %collective-permute-done.5.refs_2_), channel_id=1, source_target_pairs={{0,4},{1,5},{2,6},{3,7},{4,0},{5,1},{6,2},{7,3},{8,11},{9,8},{10,9... | collective-permute-start | bytes 700424 | tf_op jit(solution)/shard_map/ppermute | solution.py:56
  56.8 4.0 %collective-permute-done.13.refs_10_ = bf16[152,768]{1,0:T(8,128)(2,1)S(1)} collective-permute-done((bf16[152,768]{1,0:T(8,128)(2,1)S(1)}, bf16[152,768]{1,0:T(8,128)(2,1)S(1)}, u32[]{:S(2)}, u32[]{:S(2)}) %collective-permute-start.13) | collective-permute-done | bytes 233504 | tf_op jit(solution)/shard_map/ppermute | solution.py:56
  60.8 2.0 %collective-permute-start.12 = (bf16[152,768]{1,0:T(8,128)(2,1)S(1)}, bf16[152,768]{1,0:T(8,128)(2,1)S(1)}, u32[]{:S(2)}, u32[]{:S(2)}) collective-permute-start(bf16[152,768]{1,0:T(8,128)(2,1)S(1)} %collective-permute-done.4.refs_1_), channel_id=1, source_target_pairs={{0,4},{1,5},{2,6},{3,7},{4,0},{5,1},{6,2},{7,3},{8,11},{9,8},{10,9... | collective-permute-start | bytes 700424 | tf_op jit(solution)/shard_map/ppermute | solution.py:56
  62.8 4.0 %collective-permute-done.12.refs_9_ = bf16[152,768]{1,0:T(8,128)(2,1)S(1)} collective-permute-done((bf16[152,768]{1,0:T(8,128)(2,1)S(1)}, bf16[152,768]{1,0:T(8,128)(2,1)S(1)}, u32[]{:S(2)}, u32[]{:S(2)}) %collective-permute-start.12) | collective-permute-done | bytes 233504 | tf_op jit(solution)/shard_map/ppermute | solution.py:56
  66.9 2.0 %collective-permute-done.8.refs_5_ = bf16[152,768]{1,0:T(8,128)(2,1)S(1)} collective-permute-done((bf16[152,768]{1,0:T(8,128)(2,1)S(1)}, bf16[152,768]{1,0:T(8,128)(2,1)S(1)}, u32[]{:S(2)}, u32[]{:S(2)}) %collective-permute-start.8) | collective-permute-done | bytes 233504 | tf_op jit(solution)/shard_map/ppermute | solution.py:56
  68.9 4.0 %collective-permute-done.18.refs_15_ = bf16[152,768]{1,0:T(8,128)(2,1)S(1)} collective-permute-done((bf16[152,768]{1,0:T(8,128)(2,1)S(1)}, bf16[152,768]{1,0:T(8,128)(2,1)S(1)}, u32[]{:S(2)}, u32[]{:S(2)}) %collective-permute-start.18) | collective-permute-done | bytes 233504 | tf_op jit(solution)/shard_map/ppermute | solution.py:56
  75.4 3.6 %collective-permute-done.16.refs_13_ = bf16[152,768]{1,0:T(8,128)(2,1)S(1)} collective-permute-done((bf16[152,768]{1,0:T(8,128)(2,1)S(1)}, bf16[152,768]{1,0:T(8,128)(2,1)S(1)}, u32[]{:S(2)}, u32[]{:S(2)}) %collective-permute-start.16) | collective-permute-done | bytes 233504 | tf_op jit(solution)/shard_map/ppermute | solution.py:56
  79.8 6.7 %hidden.1 = (bf16[288,512]{1,0:T(8,128)(2,1)S(1)}, f32[16,64]{1,0:T(8,128)S(1)}) custom-call(f32[1,6144]{1,0:T(1,128)S(1)} %bitcast.4, bf16[152,768]{1,0:T(8,128)(2,1)S(1)} %shard_map.76.refs_0_, bf16[152,768]{1,0:T(8,128)(2,1)S(1)} %collective-permute-done.4.refs_1_, bf16[152,768]{1,0:T(8,128)(2,1)S(1)} %collective-permute-done.5.refs_2_, ...), custom_call_target="tpu_custom_call" | custom-call | flops 3623878656 | bytes 12582912 | tf_op jit(solution)/shard_map/hidden/pallas_call | solution.py:296
  86.5 3.6 %down.1 = (bf16[144,768]{1,0:T(8,128)(2,1)S(1)}, bf16[144,768]{1,0:T(8,128)(2,1)S(1)}, bf16[144,768]{1,0:T(8,128)(2,1)S(1)}, bf16[144,768]{1,0:T(8,128)(2,1)S(1)...) custom-call(bf16[288,512]{1,0:T(8,128)(2,1)S(1)} %get-tuple-element., ...), custom_call_target="tpu_custom_call" | custom-call | flops 1811939328 | bytes 6291456 | tf_op jit(solution)/shard_map/down/pallas_call | solution.py:359
  90.1 2.1 %collective-permute-start.25 = (bf16[144,768]{1,0:T(8,128)(2,1)S(1)}, bf16[144,768]{1,0:T(8,128)(2,1)S(1)}, u32[]{:S(2)}, u32[]{:S(2)}) collective-permute-start(bf16[144,768]{1,0:T(8,128)(2,1)S(1)} %get-tuple-element.47), channel_id=1, source_target_pairs={{0,4},{1,5},{2,6},{3,7},{4,0},{5,1},{6,2},{7,3},{8,11},{9,8},{10,9... | collective-permute-start | bytes 663560 | tf_op jit(solution)/shard_map/ppermute | solution.py:56
  100.6 2.6 %collective-permute-done.22.refs_1_ = bf16[144,768]{1,0:T(8,128)(2,1)S(1)} collective-permute-done((bf16[144,768]{1,0:T(8,128)(2,1)S(1)}, bf16[144,768]{1,0:T(8,128)(2,1)S(1)}, u32[]{:S(2)}, u32[]{:S(2)}) %collective-permute-start.22) | collective-permute-done | bytes 221216 | tf_op jit(solution)/shard_map/ppermute | solution.py:56
  105.2 4.7 %collective-permute-done.26.refs_1_ = bf16[144,768]{1,0:T(8,128)(2,1)S(1)} collective-permute-done((bf16[144,768]{1,0:T(8,128)(2,1)S(1)}, bf16[144,768]{1,0:T(8,128)(2,1)S(1)}, u32[]{:S(2)}, u32[]{:S(2)}) %collective-permute-start.26) | collective-permute-done | bytes 221216 | tf_op jit(solution)/shard_map/ppermute | solution.py:56
  110.0 3.9 %collective-permute-start.27 = (bf16[144,768]{1,0:T(8,128)(2,1)S(1)}, bf16[144,768]{1,0:T(8,128)(2,1)S(1)}, u32[]{:S(2)}, u32[]{:S(2)}) collective-permute-start(bf16[144,768]{1,0:T(8,128)(2,1)S(1)} %shard_map.80), channel_id=1, source_target_pairs={{0,3},{1,0},{2,1},{3,2},{4,7},{5,4},{6,5},{7,6},{8,24},{9,25},{10,... | collective-permute-start | bytes 663560 | tf_op jit(solution)/shard_map/ppermute | solution.py:56
  114.2 4.9 %collective-permute-start.34 = (bf16[144,768]{1,0:T(8,128)(2,1)S(1)}, bf16[144,768]{1,0:T(8,128)(2,1)S(1)}, u32[]{:S(2)}, u32[]{:S(2)}) collective-permute-start(bf16[144,768]{1,0:T(8,128)(2,1)S(1)} %shard_map.84), channel_id=1, source_target_pairs={{0,2},{1,3},{2,0},{3,1},{4,6},{5,7},{6,4},{7,5},{8,28},{9,29},{10,... | collective-permute-start | bytes 663560 | tf_op jit(solution)/shard_map/ppermute | solution.py:56
  119.3 2.2 %collective-permute-done.31.refs_2_ = bf16[144,768]{1,0:T(8,128)(2,1)S(1)} collective-permute-done((bf16[144,768]{1,0:T(8,128)(2,1)S(1)}, bf16[144,768]{1,0:T(8,128)(2,1)S(1)}, u32[]{:S(2)}, u32[]{:S(2)}) %collective-permute-start.31) | collective-permute-done | bytes 221216 | tf_op jit(solution)/shard_map/ppermute | solution.py:56
  121.4 3.8 %collective-permute-done.34.refs_3_ = bf16[144,768]{1,0:T(8,128)(2,1)S(1)} collective-permute-done((bf16[144,768]{1,0:T(8,128)(2,1)S(1)}, bf16[144,768]{1,0:T(8,128)(2,1)S(1)}, u32[]{:S(2)}, u32[]{:S(2)}) %collective-permute-start.34) | collective-permute-done | bytes 221216 | tf_op jit(solution)/shard_map/ppermute | solution.py:56
  125.6 4.1 %collective-permute-start.35 = (bf16[40,768]{1,0:T(8,128)(2,1)S(1)}, bf16[40,768]{1,0:T(8,128)(2,1)S(1)}, u32[]{:S(2)}, u32[]{:S(2)}) collective-permute-start(bf16[40,768]{1,0:T(8,128)(2,1)S(1)} %get-tuple-element.56), channel_id=1, source_target_pairs={{0,192},{64,0},{128,64},{192,128},{1,193},{65,1},{129,65},{193,129... | collective-permute-start | bytes 184328 | tf_op jit(solution)/shard_map/ppermute | solution.py:60
  129.7 3.7 %collective-permute-start.36 = (bf16[40,768]{1,0:T(8,128)(2,1)S(1)}, bf16[40,768]{1,0:T(8,128)(2,1)S(1)}, u32[]{:S(2)}, u32[]{:S(2)}) collective-permute-start(bf16[40,768]{1,0:T(8,128)(2,1)S(1)} %get-tuple-element.57), channel_id=1, source_target_pairs={{0,128},{64,192},{128,0},{192,64},{1,129},{65,193},{129,1},{193,65... | collective-permute-start | bytes 184328 | tf_op jit(solution)/shard_map/ppermute | solution.py:60
  135.0 2.8 %collective-permute-done.36.refs_2_ = bf16[40,768]{1,0:T(8,128)(2,1)S(1)} collective-permute-done((bf16[40,768]{1,0:T(8,128)(2,1)S(1)}, bf16[40,768]{1,0:T(8,128)(2,1)S(1)}, u32[]{:S(2)}, u32[]{:S(2)}) %collective-permute-start.36) | collective-permute-done | bytes 61472 | tf_op jit(solution)/shard_map/ppermute | solution.py:60
  137.9 2.0 %collective-permute-done.37.refs_3_ = bf16[40,768]{1,0:T(8,128)(2,1)S(1)} collective-permute-done((bf16[40,768]{1,0:T(8,128)(2,1)S(1)}, bf16[40,768]{1,0:T(8,128)(2,1)S(1)}, u32[]{:S(2)}, u32[]{:S(2)}) %collective-permute-start.37) | collective-permute-done | bytes 61472 | tf_op jit(solution)/shard_map/ppermute | solution.py:60
  140.8 5.3 %collective-permute-done.38.came_ref = bf16[72,768]{1,0:T(8,128)(2,1)S(1)} collective-permute-done((bf16[72,768]{1,0:T(8,128)(2,1)S(1)}, bf16[72,768]{1,0:T(8,128)(2,1)S(1)}, u32[]{:S(2)}, u32[]{:S(2)}) %collective-permute-start.38) | collective-permute-done | bytes 110624 | tf_op jit(solution)/shard_map/ppermute | solution.py:64
  (79 shorter events, 31.5 us)
Async XLA Ops:
  0.0 79.0 %collective-permute-start.19 = (bf16[6144,256]{1,0:T(8,128)(2,1)}, bf16[6144,256]{1,0:T(8,128)(2,1)S(1)}, u32[]{:S(2)}, u32[]{:S(2)}) collective-permute-start(bf16[6144,256]{1,0:T(8,128)(2,1)} %refs_18_.1), channel_id=1, source_target_pairs={{0,8},{8,0},{1,9},{9,1},{2,10},{10,2},{3,11},{11,3},{4,12},{12,4},... | collective-permute-start | bytes 9437192 | tf_op jit(solution)/shard_map/ppermute | solution.py:68
  0.0 79.0 %collective-permute-start.20 = (bf16[6144,256]{1,0:T(8,128)(2,1)}, bf16[6144,256]{1,0:T(8,128)(2,1)S(1)}, u32[]{:S(2)}, u32[]{:S(2)}) collective-permute-start(bf16[6144,256]{1,0:T(8,128)(2,1)} %refs_19_.1), channel_id=1, source_target_pairs={{0,8},{8,0},{1,9},{9,1},{2,10},{10,2},{3,11},{11,3},{4,12},{12,4},... | collective-permute-start | bytes 9437192 | tf_op jit(solution)/shard_map/ppermute | solution.py:68
  0.5 86.0 %collective-permute-start.21 = (bf16[256,6144]{1,0:T(8,128)(2,1)}, bf16[256,6144]{1,0:T(8,128)(2,1)S(1)}, u32[]{:S(2)}, u32[]{:S(2)}) collective-permute-start(bf16[256,6144]{1,0:T(8,128)(2,1)} %own_ref.1), channel_id=1, source_target_pairs={{0,8},{8,0},{1,9},{9,1},{2,10},{10,2},{3,11},{11,3},{4,12},{12,4},... | collective-permute-start | bytes 9437192 | tf_op jit(solution)/shard_map/ppermute | solution.py:68
  2.4 6.8 %collective-permute-start = (bf16[72,768]{1,0:T(8,128)(2,1)S(1)}, bf16[72,768]{1,0:T(8,128)(2,1)S(1)}, u32[]{:S(2)}, u32[]{:S(2)}) collective-permute-start(bf16[72,768]{1,0:T(8,128)(2,1)S(1)} %get-tuple-element.34), channel_id=1, source_target_pairs={{0,48},{16,32},{32,16},{48,0},{1,49},{17,33},{33,17},{49,1},{2,50}... | collective-permute-start | bytes 331784 | tf_op jit(solution)/shard_map/ppermute | solution.py:64
  9.4 8.7 %collective-permute-start.1 = (bf16[40,768]{1,0:T(8,128)(2,1)S(1)}, bf16[40,768]{1,0:T(8,128)(2,1)S(1)}, u32[]{:S(2)}, u32[]{:S(2)}) collective-permute-start(bf16[40,768]{1,0:T(8,128)(2,1)S(1)} %get-tuple-element.36), channel_id=1, source_target_pairs={{0,64},{64,128},{128,192},{192,0},{1,65},{65,129},{129,193},{193,1... | collective-permute-start | bytes 184328 | tf_op jit(solution)/shard_map/ppermute | solution.py:60
  12.8 11.7 %collective-permute-start.2 = (bf16[40,768]{1,0:T(8,128)(2,1)S(1)}, bf16[40,768]{1,0:T(8,128)(2,1)S(1)}, u32[]{:S(2)}, u32[]{:S(2)}) collective-permute-start(bf16[40,768]{1,0:T(8,128)(2,1)S(1)} %get-tuple-element.37), channel_id=1, source_target_pairs={{0,128},{64,192},{128,0},{192,64},{1,129},{65,193},{129,1},{193,65... | collective-permute-start | bytes 184328 | tf_op jit(solution)/shard_map/ppermute | solution.py:60
  18.2 6.3 %collective-permute-start.3 = (bf16[40,768]{1,0:T(8,128)(2,1)S(1)}, bf16[40,768]{1,0:T(8,128)(2,1)S(1)}, u32[]{:S(2)}, u32[]{:S(2)}) collective-permute-start(bf16[40,768]{1,0:T(8,128)(2,1)S(1)} %get-tuple-element.38), channel_id=1, source_target_pairs={{0,192},{64,0},{128,64},{192,128},{1,193},{65,1},{129,65},{193,129... | collective-permute-start | bytes 184328 | tf_op jit(solution)/shard_map/ppermute | solution.py:60
  24.7 7.0 %collective-permute-start.11 = (bf16[152,768]{1,0:T(8,128)(2,1)S(1)}, bf16[152,768]{1,0:T(8,128)(2,1)S(1)}, u32[]{:S(2)}, u32[]{:S(2)}) collective-permute-start(bf16[152,768]{1,0:T(8,128)(2,1)S(1)} %shard_map.76.refs_0_), channel_id=1, source_target_pairs={{0,4},{1,5},{2,6},{3,7},{4,0},{5,1},{6,2},{7,3},{8,11},{9,8},{10,9... | collective-permute-start | bytes 700424 | tf_op jit(solution)/shard_map/ppermute | solution.py:56
  27.3 8.6 %collective-permute-start.7 = (bf16[152,768]{1,0:T(8,128)(2,1)S(1)}, bf16[152,768]{1,0:T(8,128)(2,1)S(1)}, u32[]{:S(2)}, u32[]{:S(2)}) collective-permute-start(bf16[152,768]{1,0:T(8,128)(2,1)S(1)} %shard_map.76.refs_0_), channel_id=1, source_target_pairs={{0,16},{1,17},{2,18},{3,19},{4,20},{5,21},{6,22},{7,23},{8,9},{9,1... | collective-permute-start | bytes 700424 | tf_op jit(solution)/shard_map/ppermute | solution.py:56
  31.8 7.6 %collective-permute-start.6 = (bf16[152,768]{1,0:T(8,128)(2,1)S(1)}, bf16[152,768]{1,0:T(8,128)(2,1)S(1)}, u32[]{:S(2)}, u32[]{:S(2)}) collective-permute-start(bf16[152,768]{1,0:T(8,128)(2,1)S(1)} %shard_map.76.refs_0_), channel_id=1, source_target_pairs={{0,2},{1,3},{2,0},{3,1},{4,6},{5,7},{6,4},{7,5},{8,28},{9,29},{10,... | collective-permute-start | bytes 700424 | tf_op jit(solution)/shard_map/ppermute | solution.py:56
  39.3 7.4 %collective-permute-start.4 = (bf16[152,768]{1,0:T(8,128)(2,1)S(1)}, bf16[152,768]{1,0:T(8,128)(2,1)S(1)}, u32[]{:S(2)}, u32[]{:S(2)}) collective-permute-start(bf16[152,768]{1,0:T(8,128)(2,1)S(1)} %shard_map.76.refs_0_), channel_id=1, source_target_pairs={{0,1},{1,2},{2,3},{3,0},{4,5},{5,6},{6,7},{7,4},{8,24},{9,25},{10,... | collective-permute-start | bytes 700424 | tf_op jit(solution)/shard_map/ppermute | solution.py:56
  41.9 8.8 %collective-permute-start.15 = (bf16[152,768]{1,0:T(8,128)(2,1)S(1)}, bf16[152,768]{1,0:T(8,128)(2,1)S(1)}, u32[]{:S(2)}, u32[]{:S(2)}) collective-permute-start(bf16[152,768]{1,0:T(8,128)(2,1)S(1)} %collective-permute-done.7.refs_4_), channel_id=1, source_target_pairs={{0,4},{1,5},{2,6},{3,7},{4,0},{5,1},{6,2},{7,3},{8,9},{9,10},{10,1... | collective-permute-start | bytes 700424 | tf_op jit(solution)/shard_map/ppermute | solution.py:56
  46.7 8.0 %collective-permute-start.14 = (bf16[152,768]{1,0:T(8,128)(2,1)S(1)}, bf16[152,768]{1,0:T(8,128)(2,1)S(1)}, u32[]{:S(2)}, u32[]{:S(2)}) collective-permute-start(bf16[152,768]{1,0:T(8,128)(2,1)S(1)} %collective-permute-done.6.refs_3_), channel_id=1, source_target_pairs={{0,4},{1,5},{2,6},{3,7},{4,0},{5,1},{6,2},{7,3},{8,11},{9,8},{10,9... | collective-permute-start | bytes 700424 | tf_op jit(solution)/shard_map/ppermute | solution.py:56
  50.7 6.1 %collective-permute-start.10 = (bf16[152,768]{1,0:T(8,128)(2,1)S(1)}, bf16[152,768]{1,0:T(8,128)(2,1)S(1)}, u32[]{:S(2)}, u32[]{:S(2)}) collective-permute-start(bf16[152,768]{1,0:T(8,128)(2,1)S(1)} %collective-permute-done.6.refs_3_), channel_id=1, source_target_pairs={{0,16},{1,17},{2,18},{3,19},{4,20},{5,21},{6,22},{7,23},{8,9},{9,1... | collective-permute-start | bytes 700424 | tf_op jit(solution)/shard_map/ppermute | solution.py:56
  56.8 6.1 %collective-permute-start.9 = (bf16[152,768]{1,0:T(8,128)(2,1)S(1)}, bf16[152,768]{1,0:T(8,128)(2,1)S(1)}, u32[]{:S(2)}, u32[]{:S(2)}) collective-permute-start(bf16[152,768]{1,0:T(8,128)(2,1)S(1)} %collective-permute-done.5.refs_2_), channel_id=1, source_target_pairs={{0,16},{1,17},{2,18},{3,19},{4,20},{5,21},{6,22},{7,23},{8,9},{9,1... | collective-permute-start | bytes 700424 | tf_op jit(solution)/shard_map/ppermute | solution.py:56
  60.8 6.1 %collective-permute-start.12 = (bf16[152,768]{1,0:T(8,128)(2,1)S(1)}, bf16[152,768]{1,0:T(8,128)(2,1)S(1)}, u32[]{:S(2)}, u32[]{:S(2)}) collective-permute-start(bf16[152,768]{1,0:T(8,128)(2,1)S(1)} %collective-permute-done.4.refs_1_), channel_id=1, source_target_pairs={{0,4},{1,5},{2,6},{3,7},{4,0},{5,1},{6,2},{7,3},{8,11},{9,8},{10,9... | collective-permute-start | bytes 700424 | tf_op jit(solution)/shard_map/ppermute | solution.py:56
  62.8 6.1 %collective-permute-start.8 = (bf16[152,768]{1,0:T(8,128)(2,1)S(1)}, bf16[152,768]{1,0:T(8,128)(2,1)S(1)}, u32[]{:S(2)}, u32[]{:S(2)}) collective-permute-start(bf16[152,768]{1,0:T(8,128)(2,1)S(1)} %collective-permute-done.4.refs_1_), channel_id=1, source_target_pairs={{0,16},{1,17},{2,18},{3,19},{4,20},{5,21},{6,22},{7,23},{8,9},{9,1... | collective-permute-start | bytes 700424 | tf_op jit(solution)/shard_map/ppermute | solution.py:56
  68.9 6.5 %collective-permute-start.17 = (bf16[152,768]{1,0:T(8,128)(2,1)S(1)}, bf16[152,768]{1,0:T(8,128)(2,1)S(1)}, u32[]{:S(2)}, u32[]{:S(2)}) collective-permute-start(bf16[152,768]{1,0:T(8,128)(2,1)S(1)} %collective-permute-done.13.refs_10_), channel_id=1, source_target_pairs={{0,16},{1,17},{2,18},{3,19},{4,20},{5,21},{6,22},{7,23},{8,11},{9,... | collective-permute-start | bytes 700424 | tf_op jit(solution)/shard_map/ppermute | solution.py:56
  92.2 17.8 %collective-permute-start.24 = (bf16[288,768]{1,0:T(8,128)(2,1)S(1)}, bf16[288,768]{1,0:T(8,128)(2,1)S(1)}, u32[]{:S(2)}, u32[]{:S(2)}) collective-permute-start(bf16[288,768]{1,0:T(8,128)(2,1)S(1)} %get-tuple-element.44), channel_id=1, source_target_pairs={{0,4},{1,5},{2,6},{3,7},{4,0},{5,1},{6,2},{7,3},{8,9},{9,10},{10,1... | collective-permute-start | bytes 1327112 | tf_op jit(solution)/shard_map/ppermute | solution.py:56
  92.3 8.1 %collective-permute-start.32 = (bf16[144,768]{1,0:T(8,128)(2,1)S(1)}, bf16[144,768]{1,0:T(8,128)(2,1)S(1)}, u32[]{:S(2)}, u32[]{:S(2)}) collective-permute-start(bf16[144,768]{1,0:T(8,128)(2,1)S(1)} %get-tuple-element.54), channel_id=1, source_target_pairs={{0,16},{1,17},{2,18},{3,19},{4,20},{5,21},{6,22},{7,23},{8,9},{9,1... | collective-permute-start | bytes 663560 | tf_op jit(solution)/shard_map/ppermute | solution.py:56
  94.3 19.7 %collective-permute-start.30 = (bf16[288,768]{1,0:T(8,128)(2,1)S(1)}, bf16[288,768]{1,0:T(8,128)(2,1)S(1)}, u32[]{:S(2)}, u32[]{:S(2)}) collective-permute-start(bf16[288,768]{1,0:T(8,128)(2,1)S(1)} %get-tuple-element.51), channel_id=1, source_target_pairs={{0,16},{1,17},{2,18},{3,19},{4,20},{5,21},{6,22},{7,23},{8,11},{9,... | collective-permute-start | bytes 1327112 | tf_op jit(solution)/shard_map/ppermute | solution.py:56
  96.1 7.1 %collective-permute-start.22 = (bf16[144,768]{1,0:T(8,128)(2,1)S(1)}, bf16[144,768]{1,0:T(8,128)(2,1)S(1)}, u32[]{:S(2)}, u32[]{:S(2)}) collective-permute-start(bf16[144,768]{1,0:T(8,128)(2,1)S(1)} %get-tuple-element.43), channel_id=1, source_target_pairs={{0,4},{1,5},{2,6},{3,7},{4,0},{5,1},{6,2},{7,3},{8,11},{9,8},{10,9... | collective-permute-start | bytes 663560 | tf_op jit(solution)/shard_map/ppermute | solution.py:56
  98.1 11.8 %collective-permute-start.26 = (bf16[144,768]{1,0:T(8,128)(2,1)S(1)}, bf16[144,768]{1,0:T(8,128)(2,1)S(1)}, u32[]{:S(2)}, u32[]{:S(2)}) collective-permute-start(bf16[144,768]{1,0:T(8,128)(2,1)S(1)} %shard_map.79), channel_id=1, source_target_pairs={{0,16},{1,17},{2,18},{3,19},{4,20},{5,21},{6,22},{7,23},{8,11},{9,... | collective-permute-start | bytes 663560 | tf_op jit(solution)/shard_map/ppermute | solution.py:56
  100.4 13.5 %collective-permute-start.29 = (bf16[144,768]{1,0:T(8,128)(2,1)S(1)}, bf16[144,768]{1,0:T(8,128)(2,1)S(1)}, u32[]{:S(2)}, u32[]{:S(2)}) collective-permute-start(bf16[144,768]{1,0:T(8,128)(2,1)S(1)} %shard_map.81), channel_id=1, source_target_pairs={{0,4},{1,5},{2,6},{3,7},{4,0},{5,1},{6,2},{7,3},{8,9},{9,10},{10,1... | collective-permute-start | bytes 663560 | tf_op jit(solution)/shard_map/ppermute | solution.py:56
  103.2 10.9 %collective-permute-start.33 = (bf16[144,768]{1,0:T(8,128)(2,1)S(1)}, bf16[144,768]{1,0:T(8,128)(2,1)S(1)}, u32[]{:S(2)}, u32[]{:S(2)}) collective-permute-start(bf16[144,768]{1,0:T(8,128)(2,1)S(1)} %shard_map.83), channel_id=1, source_target_pairs={{0,4},{1,5},{2,6},{3,7},{4,0},{5,1},{6,2},{7,3},{8,9},{9,10},{10,1... | collective-permute-start | bytes 663560 | tf_op jit(solution)/shard_map/ppermute | solution.py:56
  109.9 9.2 %collective-permute-start.23 = (bf16[144,768]{1,0:T(8,128)(2,1)S(1)}, bf16[144,768]{1,0:T(8,128)(2,1)S(1)}, u32[]{:S(2)}, u32[]{:S(2)}) collective-permute-start(bf16[144,768]{1,0:T(8,128)(2,1)S(1)} %shard_map.77), channel_id=1, source_target_pairs={{0,16},{1,17},{2,18},{3,19},{4,20},{5,21},{6,22},{7,23},{8,11},{9,... | collective-permute-start | bytes 663560 | tf_op jit(solution)/shard_map/ppermute | solution.py:56
  110.0 9.2 %collective-permute-start.27 = (bf16[144,768]{1,0:T(8,128)(2,1)S(1)}, bf16[144,768]{1,0:T(8,128)(2,1)S(1)}, u32[]{:S(2)}, u32[]{:S(2)}) collective-permute-start(bf16[144,768]{1,0:T(8,128)(2,1)S(1)} %shard_map.80), channel_id=1, source_target_pairs={{0,3},{1,0},{2,1},{3,2},{4,7},{5,4},{6,5},{7,6},{8,24},{9,25},{10,... | collective-permute-start | bytes 663560 | tf_op jit(solution)/shard_map/ppermute | solution.py:56
  114.0 7.4 %collective-permute-start.31 = (bf16[144,768]{1,0:T(8,128)(2,1)S(1)}, bf16[144,768]{1,0:T(8,128)(2,1)S(1)}, u32[]{:S(2)}, u32[]{:S(2)}) collective-permute-start(bf16[144,768]{1,0:T(8,128)(2,1)S(1)} %shard_map.82), channel_id=1, source_target_pairs={{0,1},{1,2},{2,3},{3,0},{4,5},{5,6},{6,7},{7,4},{8,12},{9,13},{10,... | collective-permute-start | bytes 663560 | tf_op jit(solution)/shard_map/ppermute | solution.py:56
  114.2 11.0 %collective-permute-start.34 = (bf16[144,768]{1,0:T(8,128)(2,1)S(1)}, bf16[144,768]{1,0:T(8,128)(2,1)S(1)}, u32[]{:S(2)}, u32[]{:S(2)}) collective-permute-start(bf16[144,768]{1,0:T(8,128)(2,1)S(1)} %shard_map.84), channel_id=1, source_target_pairs={{0,2},{1,3},{2,0},{3,1},{4,6},{5,7},{6,4},{7,5},{8,28},{9,29},{10,... | collective-permute-start | bytes 663560 | tf_op jit(solution)/shard_map/ppermute | solution.py:56
  125.6 9.5 %collective-permute-start.35 = (bf16[40,768]{1,0:T(8,128)(2,1)S(1)}, bf16[40,768]{1,0:T(8,128)(2,1)S(1)}, u32[]{:S(2)}, u32[]{:S(2)}) collective-permute-start(bf16[40,768]{1,0:T(8,128)(2,1)S(1)} %get-tuple-element.56), channel_id=1, source_target_pairs={{0,192},{64,0},{128,64},{192,128},{1,193},{65,1},{129,65},{193,129... | collective-permute-start | bytes 184328 | tf_op jit(solution)/shard_map/ppermute | solution.py:60
  129.7 8.2 %collective-permute-start.36 = (bf16[40,768]{1,0:T(8,128)(2,1)S(1)}, bf16[40,768]{1,0:T(8,128)(2,1)S(1)}, u32[]{:S(2)}, u32[]{:S(2)}) collective-permute-start(bf16[40,768]{1,0:T(8,128)(2,1)S(1)} %get-tuple-element.57), channel_id=1, source_target_pairs={{0,128},{64,192},{128,0},{192,64},{1,129},{65,193},{129,1},{193,65... | collective-permute-start | bytes 184328 | tf_op jit(solution)/shard_map/ppermute | solution.py:60
  133.3 6.5 %collective-permute-start.37 = (bf16[40,768]{1,0:T(8,128)(2,1)S(1)}, bf16[40,768]{1,0:T(8,128)(2,1)S(1)}, u32[]{:S(2)}, u32[]{:S(2)}) collective-permute-start(bf16[40,768]{1,0:T(8,128)(2,1)S(1)} %get-tuple-element.58), channel_id=1, source_target_pairs={{0,64},{64,128},{128,192},{192,0},{1,65},{65,129},{129,193},{193,1... | collective-permute-start | bytes 184328 | tf_op jit(solution)/shard_map/ppermute | solution.py:60
  (15 other events, 99.4 us)

commit v2 on v1

--- a/solution.py
+++ b/solution.py
@@ -74,6 +74,10 @@
 
 def hbm(count):
     return [pl.BlockSpec(memory_space=pltpu.HBM)] * count
+
+
+def in_hbm(*arrays):
+    return [pltpu.with_memory_space_constraint(a, pltpu.HBM) for a in arrays]
 
 
 def small(kernel, outs, *operands):
@@ -114,12 +118,35 @@
     return first & here, second & here
 
 
-def select_kernel(ids_ref, tokens_ref, keep_ref, send_ref):
+def select_kernel(ids_hbm, tokens_hbm, keep_ref, send_ref, ids_ref, tokens_ref, sems):
+    fetch = pltpu.make_async_copy(ids_hbm, ids_ref, sems.at[0])
+    fetch_tokens = pltpu.make_async_copy(tokens_hbm, tokens_ref, sems.at[1])
+    fetch.start()
+    fetch_tokens.start()
+    fetch.wait()
     first, second = slots_of(ids_ref[...])
     picks = jnp.where(first | second, 1.0, 0.0).astype(BF16)
+    fetch_tokens.wait()
     chosen = jnp.dot(picks, tokens_ref[...], preferred_element_type=F32).astype(BF16)
     keep_ref[...] = chosen[:KEPT]
     send_ref[...] = chosen[KEPT:]
+
+
+def select(ids, tokens):
+    kept = jax.ShapeDtypeStruct((KEPT, tokens.shape[1]), BF16)
+    return pl.pallas_call(
+        select_kernel,
+        out_shape=[kept, kept],
+        in_specs=hbm(2),
+        out_specs=vmem(2),
+        scratch_shapes=[
+            pltpu.VMEM(ids.shape, ids.dtype),
+            pltpu.VMEM(tokens.shape, BF16),
+            pltpu.SemaphoreType.DMA((2,)),
+        ],
+        compiler_params=pltpu.CompilerParams(vmem_limit_bytes=4 << 20),
+        name="select",
+    )(*in_hbm(ids, tokens))
 
 
 def in_blocks(row):
@@ -184,19 +211,45 @@
     return high, (value - high.astype(F32)).astype(BF16)
 
 
-def stats_kernel(tokens_ref, gain_ref, router_ref, out_ref):
+def stats_kernel(tokens_hbm, gain_hbm, router_hbm, out_ref, gain_ref, tokens_ref, router_ref, sems):
     tokens, width = tokens_ref.shape
     part = lax.axis_index("zl") * 4 + lax.axis_index("x")
     here = pl.ds(pl.multiple_of(part * width, width), width)
+    ways = ((tokens_hbm, tokens_ref), (gain_hbm, gain_ref), (router_hbm.at[:, here], router_ref))
+    fetches = [pltpu.make_async_copy(a, b, sems.at[n]) for n, (a, b) in enumerate(ways)]
+    for fetch in fetches:
+        fetch.start()
+    out_ref[...] = jnp.zeros_like(out_ref)
+    for fetch in fetches:
+        fetch.wait()
     values = tokens_ref[...].astype(F32)
-    router = router_ref[:, here]
+    router = router_ref[...]
     ones = jnp.ones_like(router)
     scaled, squares = halves(values * gain_ref[:, here]), halves(values * values)
-    out_ref[...] = jnp.zeros_like(out_ref)
     for n, (left, terms) in enumerate(((router, scaled), (ones, squares))):
         for k, v in enumerate(halves(sum(transposed_dot(left, t) for t in terms))):
             start = (2 * n + k) * 128
             out_ref[:, start : start + tokens] = v
+
+
+def stats(tokens, gain, router):
+    width = tokens.shape[1]
+    return pl.pallas_call(
+        stats_kernel,
+        out_shape=[
+            jax.ShapeDtypeStruct((EXTRA, width), BF16),
+            jax.ShapeDtypeStruct(gain.shape, F32),
+        ],
+        in_specs=hbm(3),
+        out_specs=vmem(2),
+        scratch_shapes=[
+            pltpu.VMEM(tokens.shape, BF16),
+            pltpu.VMEM((router.shape[0], width), BF16),
+            pltpu.SemaphoreType.DMA((3,)),
+        ],
+        compiler_params=pltpu.CompilerParams(vmem_limit_bytes=4 << 20),
+        name="stats",
+    )(*in_hbm(tokens, gain, router))
 
 
 def stats_in(tile, tokens):
@@ -238,137 +291,211 @@
 
 
 CHUNK = 16
-
-
-def in_hbm(*arrays):
-    return [pltpu.with_memory_space_constraint(a, pltpu.HBM) for a in arrays]
-
-
-def hidden_kernel(width_all, gain_ref, *refs):
-    tiles, others, owns = refs[:16], refs[16:18], refs[18:20]
-    out_ref, sums_ref, x_ref, w_ref, squares_ref, sems = refs[20:]
-    copies = [pltpu.make_async_copy(w, w_ref.at[n], sems.at[n]) for n, w in enumerate(owns)]
+EARLY = 12
+
+
+def prepare(tile, gain, out_ref, row_start, column_at, squares_ref, squares_start):
+    width = tile.shape[1]
+
+    def step(n, _):
+        at = pl.multiple_of(n * CHUNK, CHUNK)
+        values = tile[pl.ds(at, CHUNK), :].astype(F32)
+        row_at = pl.ds(pl.multiple_of(row_start + at, CHUNK), CHUNK)
+        out_ref[row_at, column_at] = (values * gain).astype(BF16)
+        square = values * values
+        squares_at = pl.ds(pl.multiple_of(squares_start + at, CHUNK), CHUNK)
+        squares_ref[squares_at, :] += sum(
+            square[:, j * 128 : (j + 1) * 128] for j in range(width // 128)
+        )
+        return 0
+
+    lax.fori_loop(0, ROWS // CHUNK, step, 0)
+
+
+def add_stats(tile, row_class, sums_ref):
+    experts, tokens = sums_ref.shape[0] // 2, sums_ref.shape[1]
+    own = jnp.where(row_class == 0, 1.0, 0.0)
+    logits, squares = stats_in(tile, tokens)
+    sums_ref[:experts] += logits * own
+    sums_ref[experts:] += squares * own
+
+
+def columns_of(feature, width):
+    return pl.ds(pl.multiple_of(feature * width, width), width)
+
+
+def early_kernel(gain_ref, *refs):
+    tiles, others, owns = refs[:EARLY], refs[EARLY : EARLY + 2], refs[EARLY + 2 : EARLY + 5]
+    acc_ref, squares_ref, sums_ref, *own_refs, x_ref, sems = refs[EARLY + 5 :]
+    copies = [
+        pltpu.make_async_copy(a, b, sems.at[n]) for n, (a, b) in enumerate(zip(owns, own_refs))
+    ]
     for copy in copies:
         copy.start()
-    rows, width = ROWS, tiles[0].shape[1]
-    slices = w_ref.shape[2]
-    experts, tokens = sums_ref.shape[0] // 2, sums_ref.shape[1]
+    width = tiles[0].shape[1]
     squares_ref[...] = jnp.zeros_like(squares_ref)
     sums_ref[...] = jnp.zeros_like(sums_ref)
+    for index in range(16):
+        row_class, feature = tile_place(index // 4, index % 4)
+        column_at = columns_of(feature, width)
+        start = row_class * ROWS
+        if index < EARLY:
+            gain = gain_ref[:, column_at]
+            prepare(tiles[index], gain, x_ref, start, column_at, squares_ref, start)
+            add_stats(tiles[index], row_class, sums_ref)
+        else:
+            row_at = pl.ds(pl.multiple_of(start, ROWS), ROWS)
+            x_ref[row_at, column_at] = jnp.zeros((ROWS, width), BF16)
+    for n, weight in enumerate((*others, *own_refs[:2])):
+        if n >= 2:
+            copies[n - 2].wait()
+        acc_ref[n] = jnp.dot(x_ref[...], weight[...], preferred_element_type=F32)
+    copies[2].wait()
+
+
+def early_of(gain, tiles, others, owns, sums_shape):
+    width_all, slices = owns[0].shape
+    return pl.pallas_call(
+        early_kernel,
+        out_shape=[
+            jax.ShapeDtypeStruct((4, 2 * ROWS, slices), F32),
+            jax.ShapeDtypeStruct((2 * ROWS, 128), F32),
+            jax.ShapeDtypeStruct(sums_shape, F32),
+            *(jax.ShapeDtypeStruct(w.shape, BF16) for w in owns),
+        ],
+        in_specs=vmem(EARLY + 3) + hbm(3),
+        out_specs=vmem(6),
+        scratch_shapes=[
+            pltpu.VMEM((2 * ROWS, width_all), BF16),
+            pltpu.SemaphoreType.DMA((3,)),
+        ],
+        compiler_params=pltpu.CompilerParams(vmem_limit_bytes=20 << 20),
+        cost_estimate=pl.CostEstimate(
+            flops=2 * 2 * ROWS * width_all * 4 * slices,
+            bytes_accessed=2 * width_all * slices * 2,
+            transcendentals=0,
+        ),
+        name="early",
+    )(gain, *tiles, *others, *in_hbm(*owns))
+
+
+def late_kernel(width_all, gain_ref, *refs):
+    tiles, weights, refs = refs[:4], refs[4:8], refs[8:]
+    _, squares_in, sums_in, out_ref, sums_ref, acc_ref, squares_ref, x_ref = refs
+    width = tiles[0].shape[1]
+    slices = weights[0].shape[1]
+    squares_ref[...] = squares_in[...]
+    sums_ref[...] = sums_in[...]
     for index, tile in enumerate(tiles):
-        row_class, feature = tile_place(index // 4, index % 4)
-        column_at = pl.ds(pl.multiple_of(feature * width, width), width)
+        row_class, feature = tile_place(3, index)
+        column_at = columns_of(feature, width)
+        start = row_class * ROWS
         gain = gain_ref[:, column_at]
-
-        def prepare(n, _, tile=tile, row_class=row_class, column_at=column_at, gain=gain):
-            row_at = pl.ds(pl.multiple_of(row_class * rows + n * CHUNK, CHUNK), CHUNK)
-            values = tile[pl.ds(pl.multiple_of(n * CHUNK, CHUNK), CHUNK), :].astype(F32)
-            x_ref[row_at, column_at] = (values * gain).astype(BF16)
-            square = values * values
-            squares_ref[row_at, :] += sum(
-                square[:, j * 128 : (j + 1) * 128] for j in range(width // 128)
+        prepare(tile, gain, x_ref, 0, slice(None), squares_ref, start)
+        add_stats(tile, row_class, sums_ref)
+        row_at = pl.ds(pl.multiple_of(start, ROWS), ROWS)
+        for n, weight in enumerate(weights):
+            acc_ref[n, row_at, :] = acc_ref[n, row_at, :] + jnp.dot(
+                x_ref[...], weight[column_at, :], preferred_element_type=F32
             )
-            return 0
-
-        lax.fori_loop(0, rows // CHUNK, prepare, 0)
-        own = jnp.where(row_class == 0, 1.0, 0.0)
-        logits, squares = stats_in(tile, tokens)
-        sums_ref[:experts] += logits * own
-        sums_ref[experts:] += squares * own
     scale = lax.rsqrt(jnp.sum(squares_ref[...], axis=1, keepdims=True) / width_all + EPSILON)
-
-    def give(start, gate_weight, up_weight):
-        gate = jnp.dot(x_ref[...], gate_weight[...], preferred_element_type=F32) * scale
-        up = jnp.dot(x_ref[...], up_weight[...], preferred_element_type=F32) * scale
+    for half in range(2):
+        gate, up = acc_ref[2 * half] * scale, acc_ref[2 * half + 1] * scale
+        start = (1 - half) * slices
         out_ref[:, start : start + slices] = (gate * (1.0 / (1.0 + jnp.exp(-gate))) * up).astype(
             BF16
         )
 
-    give(slices, *others)
-    for copy in copies:
-        copy.wait()
-    give(0, w_ref.at[0], w_ref.at[1])
-
-
-def hidden_of(gain, tiles, others, owns, sums_shape):
-    rows = ROWS
-    width_all, slices = owns[0].shape
-    return pl.pallas_call(
-        partial(hidden_kernel, width_all),
+
+def late_of(gain, tiles, weights, acc, squares, sums):
+    width_all, slices = weights[0].shape
+    width = tiles[0].shape[1]
+    return pl.pallas_call(
+        partial(late_kernel, width_all),
         out_shape=[
-            jax.ShapeDtypeStruct((2 * rows, 2 * slices), BF16),
-            jax.ShapeDtypeStruct(sums_shape, F32),
-        ],
-        in_specs=vmem(19) + hbm(2),
-        out_specs=vmem(2),
+            jax.ShapeDtypeStruct((2 * ROWS, 2 * slices), BF16),
+            jax.ShapeDtypeStruct(sums.shape, F32),
+            jax.ShapeDtypeStruct(acc.shape, F32),
+        ],
+        in_specs=vmem(12),
+        out_specs=vmem(3),
+        input_output_aliases={9: 2},
         scratch_shapes=[
-            pltpu.VMEM((2 * rows, width_all), BF16),
-            pltpu.VMEM((2, width_all, slices), BF16),
-            pltpu.VMEM((2 * rows, 128), F32),
-            pltpu.SemaphoreType.DMA((2,)),
-        ],
-        compiler_params=pltpu.CompilerParams(vmem_limit_bytes=20 << 20),
+            pltpu.VMEM(squares.shape, F32),
+            pltpu.VMEM((ROWS, width), BF16),
+        ],
+        compiler_params=pltpu.CompilerParams(vmem_limit_bytes=12 << 20),
         cost_estimate=pl.CostEstimate(
-            flops=2 * 2 * rows * width_all * 4 * slices,
-            bytes_accessed=4 * width_all * slices * 2,
+            flops=2 * 4 * ROWS * width * 4 * slices,
+            bytes_accessed=acc.size * 8,
             transcendentals=0,
         ),
-        name="hidden",
-    )(gain, *tiles, *others, *in_hbm(*owns))
-
-
-def down_kernel(places, hidden_ref, own_ref, other_ref, *refs):
+        name="late",
+    )(gain, *tiles, *weights, acc, squares, sums)[:2]
+
+
+def down_kernel(far, places, hidden_ref, own_ref, other_ref, *refs):
     out_refs, y_ref = refs[:-1], refs[-1]
     slices = own_ref.shape[0]
-    rows, width = y_ref.shape[1] // 2, y_ref.shape[2]
-
-    def step(n, _):
-        _, feature = offset_place((n >> 2) * 2, n & 3)
-        column_at = pl.ds(pl.multiple_of(feature * width, width), width)
-        y_ref[n] = (
-            jnp.dot(hidden_ref[:, :slices], own_ref[:, column_at], preferred_element_type=F32)
-            + jnp.dot(hidden_ref[:, slices:], other_ref[:, column_at], preferred_element_type=F32)
+    width = y_ref.shape[2]
+    core = lax.axis_index("c")
+
+    def product(rows, square, ring):
+        _, feature = offset_place(square, ring)
+        column_at = columns_of(feature, width)
+        return (
+            jnp.dot(hidden_ref[rows, :slices], own_ref[:, column_at], preferred_element_type=F32)
+            + jnp.dot(hidden_ref[rows, slices:], other_ref[:, column_at], preferred_element_type=F32)
         ).astype(BF16)
-        return 0
-
-    lax.fori_loop(0, 8, step, 0)
-    core = lax.axis_index("c")
-
-    def give(which):
-        for n in range(8):
-            for row_class in range(2):
-                square, ring = (n >> 2) * 2 + row_class, n & 3
-                outer, inner = (square, ring) if which == 0 else (ring, square)
-                at, start = places[outer * 4 + inner]
-                out_refs[at][start : start + rows, :] = y_ref[
-                    n, row_class * rows : (row_class + 1) * rows, :
-                ]
+
+    both, first, last = slice(None), slice(0, ROWS), slice(ROWS, 2 * ROWS)
 
     @pl.when(core == 0)
     def _():
-        give(0)
+        def step(ring, _):
+            if far:
+                y_ref[ring] = product(last, 3, ring)
+                return 0
+            pair = product(both, 0, ring)
+            y_ref[ring] = pair[:ROWS]
+            y_ref[4 + ring] = pair[ROWS:]
+            y_ref[8 + ring] = product(first, 2, ring)
+            return 0
+
+        lax.fori_loop(0, 4, step, 0)
 
     @pl.when(core == 1)
     def _():
-        give(1)
-
-
-def down_of(shapes, places, hidden, own, other):
+        def step(n, _):
+            ring, square = (3, 2 * n) if far else (n >> 1, 2 * (n & 1))
+            pair = product(both, square, ring)
+            at = square if far else 4 * ring + square
+            y_ref[at] = pair[:ROWS]
+            y_ref[at + 1] = pair[ROWS:]
+            return 0
+
+        lax.fori_loop(0, 2 if far else 6, step, 0)
+
+    for index, (at, start) in enumerate(places):
+        out_refs[at][start : start + ROWS, :] = y_ref[index]
+
+
+def down_of(far, shapes, places, hidden, own, other):
     slices, width_all = own.shape
     width = width_all // 8
     return pl.pallas_call(
-        partial(down_kernel, places),
+        partial(down_kernel, far, places),
         out_shape=[jax.ShapeDtypeStruct((rows, width), BF16) for rows in shapes],
         in_specs=vmem(3),
         out_specs=vmem(len(shapes)),
-        scratch_shapes=[pltpu.VMEM((8, hidden.shape[0], width), BF16)],
-        compiler_params=pltpu.CompilerParams(vmem_limit_bytes=20 << 20),
+        scratch_shapes=[pltpu.VMEM((len(places), ROWS, width), BF16)],
+        compiler_params=pltpu.CompilerParams(vmem_limit_bytes=16 << 20),
         cost_estimate=pl.CostEstimate(
-            flops=2 * hidden.shape[0] * width_all * 2 * slices,
+            flops=2 * len(places) * ROWS * width * 2 * slices,
             bytes_accessed=2 * slices * width_all * 2,
             transcendentals=0,
         ),
-        name="down",
+        name="far" if far else "rest",
     )(hidden, own, other)
 
 
@@ -395,14 +522,14 @@
     ids = expert_ids.T
     kept, block = (KEPT, width), (BLOCK, width)
 
-    keep, send = small(select_kernel, [kept, kept], ids, tokens)
+    keep, send = select(ids, tokens)
     came = across_y(send)
     blocks = small(shuffle_kernel, [block] * FAR, keep, came)
     arrived = [blocks[0]] + [along_z(blocks[k], k) for k in (1, 2, 3)]
     gate_other = other_core(gate_proj)
     up_other = other_core(up_proj)
     down_other = other_core(down_proj)
-    (part_sums,) = small(stats_kernel, [(EXTRA, width)], tokens, gain, router_weight.T)
+    part_sums, gain = stats(tokens, gain, router_weight.T)
     (mine,) = small(pack_kernel, [(ROWS + EXTRA, width)], *arrived, part_sums)
 
     inner = [mine, hop(mine, "x+", "y"), hop(mine, "x-", "z"), hop(mine, "xx", "yz")]
@@ -416,17 +543,19 @@
         outer[3][a] = hop(outer[2][a], "y", "x-")
     tiles = [outer[m][a] for m in range(4) for a in range(4)]
     sums_shape = (2 * router_weight.shape[1], tokens.shape[0])
-    hidden, sums = hidden_of(
-        gain, tiles, (gate_other, up_other), (gate_proj, up_proj), sums_shape
+    acc, squares, sums, gate_own, up_own, down_own = early_of(
+        gain, tiles[:EARLY], (gate_other, up_other), (gate_proj, up_proj, down_proj), sums_shape
     )
-
-    shapes = [ROWS] * 12 + [2 * ROWS] * 2
-    places = {4 * 0 + a: (a, 0) for a in range(4)}
-    places |= {4 * 3 + a: (4 + a, 0) for a in range(4)}
-    places |= {4 * 1 + 0: (8, 0), 4 * 1 + 1: (9, 0), 4 * 2 + 2: (10, 0), 4 * 2 + 3: (11, 0)}
-    places |= {4 * 1 + 2: (12, 0), 4 * 1 + 3: (12, ROWS), 4 * 2 + 0: (13, 0), 4 * 2 + 1: (13, ROWS)}
-    part = down_of(shapes, places, hidden, down_proj, down_other)
-    own, far, near, pairs = part[:4], part[4:8], part[8:12], part[12:]
+    weights = (gate_other, up_other, gate_own, up_own)
+    hidden, sums = late_of(gain, tiles[EARLY:], weights, acc, squares, sums)
+
+    far = down_of(True, [ROWS] * 4, [(a, 0) for a in range(4)], hidden, down_own, down_other)
+    places = [(a, 0) for a in range(4)]
+    places += [(4, 0), (5, 0), (8, 0), (8, ROWS)]
+    places += [(9, 0), (9, ROWS), (6, 0), (7, 0)]
+    shapes = [ROWS] * 8 + [2 * ROWS] * 2
+    rest = down_of(False, shapes, places, hidden, down_own, down_other)
+    own, near, pairs = rest[:4], rest[4:8], rest[8:]
     ways = [("z", "x-"), ("z", "x-"), ("y", "x+"), ("y", "x+")]
     far_in = [hop(far[n], *ways[n]) for n in range(4)]
     first = hop(pairs[0], "y", "x-")

time: 148 us -> 139 us (0.939)
  the two profiles are of different devices: /device:TPU:24 before, /device:TPU:6 now
where the time goes in v2:
time: 139 us
  waiting for transfers between devices  63.5 us (46%)
  starting transfers between devices  57.1 us (41%)
  Pallas kernels  18.6 us (13%)
    ppermute x28, waiting for transfers between devices, hop(): return lax.ppermute(value, OWNER, owner_pairs(step_core0, step_core1))  50.3 us
    ppermute x28, starting transfers between devices, hop(): return lax.ppermute(value, OWNER, owner_pairs(step_core0, step_core1))  27.6 us
    ppermute x6, starting transfers between devices, along_z(): lax.ppermute(value, 'zh', [(i, (i + distance) % FAR) for i in range(FAR)])  22.9 us
    pallas_call x1, Pallas kernels, early_of(): pl.pallas_call(early_kernel, out_shape=[jax.ShapeDtypeStruct((4, 2 * ROWS...  7.86 us
    ppermute x2, waiting for transfers between devices, across_y(): return lax.ppermute(value, ('y2', 'y1'), [(i, 3 - i) for i in range(4)])  6.86 us
    ppermute x6, waiting for transfers between devices, along_z(): lax.ppermute(value, 'zh', [(i, (i + distance) % FAR) for i in range(FAR)])  6.32 us
    ppermute x2, starting transfers between devices, across_y(): return lax.ppermute(value, ('y2', 'y1'), [(i, 3 - i) for i in range(4)])  6.02 us
    pallas_call x2, Pallas kernels, down_of(): pl.pallas_call(partial(down_kernel, far, places), out_shape=[jax.ShapeDty...  3.59 us
  transfers between devices with their start and end apart: 39, of which 23 were waited for; matrix products, arithmetic and copies ran while one was open for 0% of the time, Pallas kernels for 11%

profile of v2, /device:TPU:6, one launch (start us, length us, event | category | flops | bytes accessed | tf_op | source)
XLA Modules:
  0.0 139.4 jit_solution(13157937380471622081)
XLA Ops:
  1.7 3.1 %collective-permute-start = (bf16[72,768]{1,0:T(8,128)(2,1)S(1)}, bf16[72,768]{1,0:T(8,128)(2,1)S(1)}, u32[]{:S(2)}, u32[]{:S(2)}) collective-permute-start(bf16[72,768]{1,0:T(8,128)(2,1)S(1)} %get-tuple-element.43), channel_id=1, source_target_pairs={{0,48},{16,32},{32,16},{48,0},{1,49},{17,33},{33,17},{49,1},{2,50}... | collective-permute-start | bytes 331784 | tf_op jit(solution)/shard_map/ppermute | solution.py:64
  4.8 3.7 %collective-permute-done.came_ref = bf16[72,768]{1,0:T(8,128)(2,1)S(1)} collective-permute-done((bf16[72,768]{1,0:T(8,128)(2,1)S(1)}, bf16[72,768]{1,0:T(8,128)(2,1)S(1)}, u32[]{:S(2)}, u32[]{:S(2)}) %collective-permute-start) | collective-permute-done | bytes 110624 | tf_op jit(solution)/shard_map/ppermute | solution.py:64
  8.7 3.3 %collective-permute-start.1 = (bf16[40,768]{1,0:T(8,128)(2,1)S(1)}, bf16[40,768]{1,0:T(8,128)(2,1)S(1)}, u32[]{:S(2)}, u32[]{:S(2)}) collective-permute-start(bf16[40,768]{1,0:T(8,128)(2,1)S(1)} %get-tuple-element.45), channel_id=1, source_target_pairs={{0,64},{64,128},{128,192},{192,0},{1,65},{65,129},{129,193},{193,1... | collective-permute-start | bytes 184328 | tf_op jit(solution)/shard_map/ppermute | solution.py:60
  12.1 5.4 %collective-permute-start.2 = (bf16[40,768]{1,0:T(8,128)(2,1)S(1)}, bf16[40,768]{1,0:T(8,128)(2,1)S(1)}, u32[]{:S(2)}, u32[]{:S(2)}) collective-permute-start(bf16[40,768]{1,0:T(8,128)(2,1)S(1)} %get-tuple-element.46), channel_id=1, source_target_pairs={{0,128},{64,192},{128,0},{192,64},{1,129},{65,193},{129,1},{193,65... | collective-permute-start | bytes 184328 | tf_op jit(solution)/shard_map/ppermute | solution.py:60
  17.5 3.6 %collective-permute-start.3 = (bf16[40,768]{1,0:T(8,128)(2,1)S(1)}, bf16[40,768]{1,0:T(8,128)(2,1)S(1)}, u32[]{:S(2)}, u32[]{:S(2)}) collective-permute-start(bf16[40,768]{1,0:T(8,128)(2,1)S(1)} %get-tuple-element.47), channel_id=1, source_target_pairs={{0,192},{64,0},{128,64},{192,128},{1,193},{65,1},{129,65},{193,129... | collective-permute-start | bytes 184328 | tf_op jit(solution)/shard_map/ppermute | solution.py:60
  25.7 7.8 %collective-permute-done.9.refs_2_ = bf16[152,768]{1,0:T(8,128)(2,1)S(1)} collective-permute-done((bf16[152,768]{1,0:T(8,128)(2,1)S(1)}, bf16[152,768]{1,0:T(8,128)(2,1)S(1)}, u32[]{:S(2)}, u32[]{:S(2)}) %collective-permute-start.9) | collective-permute-done | bytes 233504 | tf_op jit(solution)/shard_map/ppermute | solution.py:56
  33.8 5.8 %collective-permute-done.6.refs_1_ = bf16[152,768]{1,0:T(8,128)(2,1)S(1)} collective-permute-done((bf16[152,768]{1,0:T(8,128)(2,1)S(1)}, bf16[152,768]{1,0:T(8,128)(2,1)S(1)}, u32[]{:S(2)}, u32[]{:S(2)}) %collective-permute-start.6) | collective-permute-done | bytes 233504 | tf_op jit(solution)/shard_map/ppermute | solution.py:56
  39.6 2.0 %collective-permute-start.19 = (bf16[152,768]{1,0:T(8,128)(2,1)S(1)}, bf16[152,768]{1,0:T(8,128)(2,1)S(1)}, u32[]{:S(2)}, u32[]{:S(2)}) collective-permute-start(bf16[152,768]{1,0:T(8,128)(2,1)S(1)} %shard_map.74.refs_0_), channel_id=1, source_target_pairs={{0,4},{1,5},{2,6},{3,7},{4,0},{5,1},{6,2},{7,3},{8,11},{9,8},{10,9... | collective-permute-start | bytes 700424 | tf_op jit(solution)/shard_map/ppermute | solution.py:56
  41.6 4.0 %collective-permute-done.19.refs_8_ = bf16[152,768]{1,0:T(8,128)(2,1)S(1)} collective-permute-done((bf16[152,768]{1,0:T(8,128)(2,1)S(1)}, bf16[152,768]{1,0:T(8,128)(2,1)S(1)}, u32[]{:S(2)}, u32[]{:S(2)}) %collective-permute-start.19) | collective-permute-done | bytes 233504 | tf_op jit(solution)/shard_map/ppermute | solution.py:56
  45.6 2.0 %collective-permute-start.13 = (bf16[152,768]{1,0:T(8,128)(2,1)S(1)}, bf16[152,768]{1,0:T(8,128)(2,1)S(1)}, u32[]{:S(2)}, u32[]{:S(2)}) collective-permute-start(bf16[152,768]{1,0:T(8,128)(2,1)S(1)} %collective-permute-done.12.refs_3_), channel_id=1, source_target_pairs={{0,4},{1,5},{2,6},{3,7},{4,0},{5,1},{6,2},{7,3},{8,11},{9,8},{10,9... | collective-permute-start | bytes 700424 | tf_op jit(solution)/shard_map/ppermute | solution.py:56
  48.6 3.1 %collective-permute-done.13.refs_11_ = bf16[152,768]{1,0:T(8,128)(2,1)S(1)} collective-permute-done((bf16[152,768]{1,0:T(8,128)(2,1)S(1)}, bf16[152,768]{1,0:T(8,128)(2,1)S(1)}, u32[]{:S(2)}, u32[]{:S(2)}) %collective-permute-start.13) | collective-permute-done | bytes 233504 | tf_op jit(solution)/shard_map/ppermute | solution.py:56
  52.1 2.1 %collective-permute-done.7.refs_5_ = bf16[152,768]{1,0:T(8,128)(2,1)S(1)} collective-permute-done((bf16[152,768]{1,0:T(8,128)(2,1)S(1)}, bf16[152,768]{1,0:T(8,128)(2,1)S(1)}, u32[]{:S(2)}, u32[]{:S(2)}) %collective-permute-start.7) | collective-permute-done | bytes 233504 | tf_op jit(solution)/shard_map/ppermute | solution.py:56
  54.6 3.1 %collective-permute-done.17.refs_6_ = bf16[152,768]{1,0:T(8,128)(2,1)S(1)} collective-permute-done((bf16[152,768]{1,0:T(8,128)(2,1)S(1)}, bf16[152,768]{1,0:T(8,128)(2,1)S(1)}, u32[]{:S(2)}, u32[]{:S(2)}) %collective-permute-start.17) | collective-permute-done | bytes 233504 | tf_op jit(solution)/shard_map/ppermute | solution.py:56
  57.8 2.0 %collective-permute-start.20 = (bf16[152,768]{1,0:T(8,128)(2,1)S(1)}, bf16[152,768]{1,0:T(8,128)(2,1)S(1)}, u32[]{:S(2)}, u32[]{:S(2)}) collective-permute-start(bf16[152,768]{1,0:T(8,128)(2,1)S(1)} %collective-permute-done.6.refs_1_), channel_id=1, source_target_pairs={{0,4},{1,5},{2,6},{3,7},{4,0},{5,1},{6,2},{7,3},{8,11},{9,8},{10,9... | collective-permute-start | bytes 700424 | tf_op jit(solution)/shard_map/ppermute | solution.py:56
  60.3 2.0 %collective-permute-start.5 = (bf16[152,768]{1,0:T(8,128)(2,1)S(1)}, bf16[152,768]{1,0:T(8,128)(2,1)S(1)}, u32[]{:S(2)}, u32[]{:S(2)}) collective-permute-start(bf16[152,768]{1,0:T(8,128)(2,1)S(1)} %collective-permute-done.4.refs_4_), channel_id=1, source_target_pairs={{0,4},{1,5},{2,6},{3,7},{4,0},{5,1},{6,2},{7,3},{8,9},{9,10},{10,1... | collective-permute-start | bytes 700424 | tf_op jit(solution)/shard_map/ppermute | solution.py:56
  65.9 2.0 %collective-permute-start.8 = (bf16[152,768]{1,0:T(8,128)(2,1)S(1)}, bf16[152,768]{1,0:T(8,128)(2,1)S(1)}, u32[]{:S(2)}, u32[]{:S(2)}) collective-permute-start(bf16[152,768]{1,0:T(8,128)(2,1)S(1)} %collective-permute-done.7.refs_5_), channel_id=1, source_target_pairs={{0,4},{1,5},{2,6},{3,7},{4,0},{5,1},{6,2},{7,3},{8,9},{9,10},{10,1... | collective-permute-start | bytes 700424 | tf_op jit(solution)/shard_map/ppermute | solution.py:56
  67.8 7.9 %early.1 = (f32[4,288,256]{2,1,0:T(8,128)S(1)}, f32[288,128]{1,0:T(8,128)S(1)}, f32[16,64]{1,0:T(8,128)S(1)}, bf16[6144,256]{1,0:T(8,128)(2,1)S(1)}, bf16[6144,2...) custom-call(f32[1,6144]{1,0:T(1,128)S(1)} %get-tuple-element.41.gain_ref, bf16[152,768]{1,0:T(8,128)(2,1)S(1)} %shard_map.74.refs_0_, ...), custom_call_target="tpu_custom_call" | custom-call | flops 3623878656 | bytes 6291456 | tf_op jit(solution)/shard_map/early/pallas_call | solution.py:358
  75.7 2.2 %late.1 = (bf16[288,512]{1,0:T(8,128)(2,1)S(1)}, f32[16,64]{1,0:T(8,128)S(1)}, f32[4,288,256]{2,1,0:T(8,128)S(1)}) custom-call(f32[1,6144]{1,0:T(1,128)S(1)} %get-tuple-element.41.gain_ref, bf16[152,768]{1,0:T(8,128)(2,1)S(1)} %collective-permute-done.5.refs_0_, ...), custom_call_target="tpu_custom_call", output_to_operand_aliasing={{2}: (9, {})} | custom-call | flops 905969664 | bytes 2359296 | tf_op jit(solution)/shard_map/late/pallas_call | solution.py:413
  79.6 1.7 %collective-permute-start.28 = (bf16[144,768]{1,0:T(8,128)(2,1)S(1)}, bf16[144,768]{1,0:T(8,128)(2,1)S(1)}, u32[]{:S(2)}, u32[]{:S(2)}) collective-permute-start(bf16[144,768]{1,0:T(8,128)(2,1)S(1)} %get-tuple-element.66), channel_id=1, source_target_pairs={{0,16},{1,17},{2,18},{3,19},{4,20},{5,21},{6,22},{7,23},{8,9},{9,1... | collective-permute-start | bytes 663560 | tf_op jit(solution)/shard_map/ppermute | solution.py:56
  81.4 2.3 %rest.1 = (bf16[144,768]{1,0:T(8,128)(2,1)S(1)}, bf16[144,768]{1,0:T(8,128)(2,1)S(1)}, bf16[144,768]{1,0:T(8,128)(2,1)S(1)}, bf16[144,768]{1,0:T(8,128)(2,1)S(1)...) custom-call(bf16[288,512]{1,0:T(8,128)(2,1)S(1)} %get-tuple-element., ...), custom_call_target="tpu_custom_call" | custom-call | flops 1358954496 | bytes 6291456 | tf_op jit(solution)/shard_map/rest/pallas_call | solution.py:486
  84.3 1.8 %collective-permute-start.22 = (bf16[144,768]{1,0:T(8,128)(2,1)S(1)}, bf16[144,768]{1,0:T(8,128)(2,1)S(1)}, u32[]{:S(2)}, u32[]{:S(2)}) collective-permute-start(bf16[144,768]{1,0:T(8,128)(2,1)S(1)} %get-tuple-element.59), channel_id=1, source_target_pairs={{0,4},{1,5},{2,6},{3,7},{4,0},{5,1},{6,2},{7,3},{8,11},{9,8},{10,9... | collective-permute-start | bytes 663560 | tf_op jit(solution)/shard_map/ppermute | solution.py:56
  88.3 1.7 %collective-permute-done.25.refs_1_ = bf16[144,768]{1,0:T(8,128)(2,1)S(1)} collective-permute-done((bf16[144,768]{1,0:T(8,128)(2,1)S(1)}, bf16[144,768]{1,0:T(8,128)(2,1)S(1)}, u32[]{:S(2)}, u32[]{:S(2)}) %collective-permute-start.25) | collective-permute-done | bytes 221216 | tf_op jit(solution)/shard_map/ppermute | solution.py:56
  90.3 2.2 %collective-permute-done.22.refs_1_ = bf16[144,768]{1,0:T(8,128)(2,1)S(1)} collective-permute-done((bf16[144,768]{1,0:T(8,128)(2,1)S(1)}, bf16[144,768]{1,0:T(8,128)(2,1)S(1)}, u32[]{:S(2)}, u32[]{:S(2)}) %collective-permute-start.22) | collective-permute-done | bytes 221216 | tf_op jit(solution)/shard_map/ppermute | solution.py:56
  92.5 2.5 %collective-permute-start.26 = (bf16[144,768]{1,0:T(8,128)(2,1)S(1)}, bf16[144,768]{1,0:T(8,128)(2,1)S(1)}, u32[]{:S(2)}, u32[]{:S(2)}) collective-permute-start(bf16[144,768]{1,0:T(8,128)(2,1)S(1)} %shard_map.77), channel_id=1, source_target_pairs={{0,16},{1,17},{2,18},{3,19},{4,20},{5,21},{6,22},{7,23},{8,11},{9,... | collective-permute-start | bytes 663560 | tf_op jit(solution)/shard_map/ppermute | solution.py:56
  95.1 9.1 %collective-permute-done.33.refs_1_ = bf16[144,768]{1,0:T(8,128)(2,1)S(1)} collective-permute-done((bf16[144,768]{1,0:T(8,128)(2,1)S(1)}, bf16[144,768]{1,0:T(8,128)(2,1)S(1)}, u32[]{:S(2)}, u32[]{:S(2)}) %collective-permute-start.33) | collective-permute-done | bytes 221216 | tf_op jit(solution)/shard_map/ppermute | solution.py:56
  104.2 1.7 %collective-permute-start.23 = (bf16[144,768]{1,0:T(8,128)(2,1)S(1)}, bf16[144,768]{1,0:T(8,128)(2,1)S(1)}, u32[]{:S(2)}, u32[]{:S(2)}) collective-permute-start(bf16[144,768]{1,0:T(8,128)(2,1)S(1)} %shard_map.75), channel_id=1, source_target_pairs={{0,16},{1,17},{2,18},{3,19},{4,20},{5,21},{6,22},{7,23},{8,11},{9,... | collective-permute-start | bytes 663560 | tf_op jit(solution)/shard_map/ppermute | solution.py:56
  110.3 3.3 %collective-permute-done.34.refs_3_ = bf16[144,768]{1,0:T(8,128)(2,1)S(1)} collective-permute-done((bf16[144,768]{1,0:T(8,128)(2,1)S(1)}, bf16[144,768]{1,0:T(8,128)(2,1)S(1)}, u32[]{:S(2)}, u32[]{:S(2)}) %collective-permute-start.34) | collective-permute-done | bytes 221216 | tf_op jit(solution)/shard_map/ppermute | solution.py:56
  116.3 6.0 %collective-permute-start.35 = (bf16[40,768]{1,0:T(8,128)(2,1)S(1)}, bf16[40,768]{1,0:T(8,128)(2,1)S(1)}, u32[]{:S(2)}, u32[]{:S(2)}) collective-permute-start(bf16[40,768]{1,0:T(8,128)(2,1)S(1)} %get-tuple-element.72), channel_id=1, source_target_pairs={{0,192},{64,0},{128,64},{192,128},{1,193},{65,1},{129,65},{193,129... | collective-permute-start | bytes 184328 | tf_op jit(solution)/shard_map/ppermute | solution.py:60
  122.2 3.4 %collective-permute-start.36 = (bf16[40,768]{1,0:T(8,128)(2,1)S(1)}, bf16[40,768]{1,0:T(8,128)(2,1)S(1)}, u32[]{:S(2)}, u32[]{:S(2)}) collective-permute-start(bf16[40,768]{1,0:T(8,128)(2,1)S(1)} %get-tuple-element.73), channel_id=1, source_target_pairs={{0,128},{64,192},{128,0},{192,64},{1,129},{65,193},{129,1},{193,65... | collective-permute-start | bytes 184328 | tf_op jit(solution)/shard_map/ppermute | solution.py:60
  126.9 3.6 %collective-permute-done.36.refs_2_ = bf16[40,768]{1,0:T(8,128)(2,1)S(1)} collective-permute-done((bf16[40,768]{1,0:T(8,128)(2,1)S(1)}, bf16[40,768]{1,0:T(8,128)(2,1)S(1)}, u32[]{:S(2)}, u32[]{:S(2)}) %collective-permute-start.36) | collective-permute-done | bytes 61472 | tf_op jit(solution)/shard_map/ppermute | solution.py:60
  132.2 2.9 %collective-permute-start.38 = (bf16[72,768]{1,0:T(8,128)(2,1)S(1)}, bf16[72,768]{1,0:T(8,128)(2,1)S(1)}, u32[]{:S(2)}, u32[]{:S(2)}) collective-permute-start(bf16[72,768]{1,0:T(8,128)(2,1)S(1)} %get-tuple-element.76), channel_id=1, source_target_pairs={{0,48},{16,32},{32,16},{48,0},{1,49},{17,33},{33,17},{49,1},{2,50}... | collective-permute-start | bytes 331784 | tf_op jit(solution)/shard_map/ppermute | solution.py:64
  135.2 3.1 %collective-permute-done.38.came_ref = bf16[72,768]{1,0:T(8,128)(2,1)S(1)} collective-permute-done((bf16[72,768]{1,0:T(8,128)(2,1)S(1)}, bf16[72,768]{1,0:T(8,128)(2,1)S(1)}, u32[]{:S(2)}, u32[]{:S(2)}) %collective-permute-start.38) | collective-permute-done | bytes 110624 | tf_op jit(solution)/shard_map/ppermute | solution.py:64
  (67 shorter events, 28.6 us)
Async XLA Ops:
  0.0 64.3 %collective-permute-start.15 = (bf16[6144,256]{1,0:T(8,128)(2,1)}, bf16[6144,256]{1,0:T(8,128)(2,1)S(1)}, u32[]{:S(2)}, u32[]{:S(2)}) collective-permute-start(bf16[6144,256]{1,0:T(8,128)(2,1)} %refs_14_.1), channel_id=1, source_target_pairs={{0,8},{8,0},{1,9},{9,1},{2,10},{10,2},{3,11},{11,3},{4,12},{12,4},... | collective-permute-start | bytes 9437192 | tf_op jit(solution)/shard_map/ppermute | solution.py:68
  0.0 65.9 %collective-permute-start.16 = (bf16[6144,256]{1,0:T(8,128)(2,1)}, bf16[6144,256]{1,0:T(8,128)(2,1)S(1)}, u32[]{:S(2)}, u32[]{:S(2)}) collective-permute-start(bf16[6144,256]{1,0:T(8,128)(2,1)} %refs_15_.1), channel_id=1, source_target_pairs={{0,8},{8,0},{1,9},{9,1},{2,10},{10,2},{3,11},{11,3},{4,12},{12,4},... | collective-permute-start | bytes 9437192 | tf_op jit(solution)/shard_map/ppermute | solution.py:68
  0.5 77.5 %collective-permute-start.21 = (bf16[256,6144]{1,0:T(8,128)(2,1)}, bf16[256,6144]{1,0:T(8,128)(2,1)S(1)}, u32[]{:S(2)}, u32[]{:S(2)}) collective-permute-start(bf16[256,6144]{1,0:T(8,128)(2,1)} %refs_16_.1), channel_id=1, source_target_pairs={{0,8},{8,0},{1,9},{9,1},{2,10},{10,2},{3,11},{11,3},{4,12},{12,4},... | collective-permute-start | bytes 9437192 | tf_op jit(solution)/shard_map/ppermute | solution.py:68
  1.7 6.8 %collective-permute-start = (bf16[72,768]{1,0:T(8,128)(2,1)S(1)}, bf16[72,768]{1,0:T(8,128)(2,1)S(1)}, u32[]{:S(2)}, u32[]{:S(2)}) collective-permute-start(bf16[72,768]{1,0:T(8,128)(2,1)S(1)} %get-tuple-element.43), channel_id=1, source_target_pairs={{0,48},{16,32},{32,16},{48,0},{1,49},{17,33},{33,17},{49,1},{2,50}... | collective-permute-start | bytes 331784 | tf_op jit(solution)/shard_map/ppermute | solution.py:64
  8.7 8.7 %collective-permute-start.1 = (bf16[40,768]{1,0:T(8,128)(2,1)S(1)}, bf16[40,768]{1,0:T(8,128)(2,1)S(1)}, u32[]{:S(2)}, u32[]{:S(2)}) collective-permute-start(bf16[40,768]{1,0:T(8,128)(2,1)S(1)} %get-tuple-element.45), channel_id=1, source_target_pairs={{0,64},{64,128},{128,192},{192,0},{1,65},{65,129},{129,193},{193,1... | collective-permute-start | bytes 184328 | tf_op jit(solution)/shard_map/ppermute | solution.py:60
  12.1 10.2 %collective-permute-start.2 = (bf16[40,768]{1,0:T(8,128)(2,1)S(1)}, bf16[40,768]{1,0:T(8,128)(2,1)S(1)}, u32[]{:S(2)}, u32[]{:S(2)}) collective-permute-start(bf16[40,768]{1,0:T(8,128)(2,1)S(1)} %get-tuple-element.46), channel_id=1, source_target_pairs={{0,128},{64,192},{128,0},{192,64},{1,129},{65,193},{129,1},{193,65... | collective-permute-start | bytes 184328 | tf_op jit(solution)/shard_map/ppermute | solution.py:60
  23.6 9.9 %collective-permute-start.9 = (bf16[152,768]{1,0:T(8,128)(2,1)S(1)}, bf16[152,768]{1,0:T(8,128)(2,1)S(1)}, u32[]{:S(2)}, u32[]{:S(2)}) collective-permute-start(bf16[152,768]{1,0:T(8,128)(2,1)S(1)} %shard_map.74.refs_0_), channel_id=1, source_target_pairs={{0,3},{1,0},{2,1},{3,2},{4,7},{5,4},{6,5},{7,6},{8,12},{9,13},{10,... | collective-permute-start | bytes 700424 | tf_op jit(solution)/shard_map/ppermute | solution.py:56
  24.6 9.0 %collective-permute-start.12 = (bf16[152,768]{1,0:T(8,128)(2,1)S(1)}, bf16[152,768]{1,0:T(8,128)(2,1)S(1)}, u32[]{:S(2)}, u32[]{:S(2)}) collective-permute-start(bf16[152,768]{1,0:T(8,128)(2,1)S(1)} %shard_map.74.refs_0_), channel_id=1, source_target_pairs={{0,2},{1,3},{2,0},{3,1},{4,6},{5,7},{6,4},{7,5},{8,28},{9,29},{10,... | collective-permute-start | bytes 700424 | tf_op jit(solution)/shard_map/ppermute | solution.py:56
  33.5 6.1 %collective-permute-start.6 = (bf16[152,768]{1,0:T(8,128)(2,1)S(1)}, bf16[152,768]{1,0:T(8,128)(2,1)S(1)}, u32[]{:S(2)}, u32[]{:S(2)}) collective-permute-start(bf16[152,768]{1,0:T(8,128)(2,1)S(1)} %shard_map.74.refs_0_), channel_id=1, source_target_pairs={{0,1},{1,2},{2,3},{3,0},{4,5},{5,6},{6,7},{7,4},{8,24},{9,25},{10,... | collective-permute-start | bytes 700424 | tf_op jit(solution)/shard_map/ppermute | solution.py:56
  33.5 8.0 %collective-permute-start.4 = (bf16[152,768]{1,0:T(8,128)(2,1)S(1)}, bf16[152,768]{1,0:T(8,128)(2,1)S(1)}, u32[]{:S(2)}, u32[]{:S(2)}) collective-permute-start(bf16[152,768]{1,0:T(8,128)(2,1)S(1)} %shard_map.74.refs_0_), channel_id=1, source_target_pairs={{0,16},{1,17},{2,18},{3,19},{4,20},{5,21},{6,22},{7,23},{8,9},{9,1... | collective-permute-start | bytes 700424 | tf_op jit(solution)/shard_map/ppermute | solution.py:56
  39.6 6.1 %collective-permute-start.19 = (bf16[152,768]{1,0:T(8,128)(2,1)S(1)}, bf16[152,768]{1,0:T(8,128)(2,1)S(1)}, u32[]{:S(2)}, u32[]{:S(2)}) collective-permute-start(bf16[152,768]{1,0:T(8,128)(2,1)S(1)} %shard_map.74.refs_0_), channel_id=1, source_target_pairs={{0,4},{1,5},{2,6},{3,7},{4,0},{5,1},{6,2},{7,3},{8,11},{9,8},{10,9... | collective-permute-start | bytes 700424 | tf_op jit(solution)/shard_map/ppermute | solution.py:56
  41.5 6.6 %collective-permute-start.10 = (bf16[152,768]{1,0:T(8,128)(2,1)S(1)}, bf16[152,768]{1,0:T(8,128)(2,1)S(1)}, u32[]{:S(2)}, u32[]{:S(2)}) collective-permute-start(bf16[152,768]{1,0:T(8,128)(2,1)S(1)} %collective-permute-done.9.refs_2_), channel_id=1, source_target_pairs={{0,4},{1,5},{2,6},{3,7},{4,0},{5,1},{6,2},{7,3},{8,11},{9,8},{10,9... | collective-permute-start | bytes 700424 | tf_op jit(solution)/shard_map/ppermute | solution.py:56
  45.6 6.1 %collective-permute-start.13 = (bf16[152,768]{1,0:T(8,128)(2,1)S(1)}, bf16[152,768]{1,0:T(8,128)(2,1)S(1)}, u32[]{:S(2)}, u32[]{:S(2)}) collective-permute-start(bf16[152,768]{1,0:T(8,128)(2,1)S(1)} %collective-permute-done.12.refs_3_), channel_id=1, source_target_pairs={{0,4},{1,5},{2,6},{3,7},{4,0},{5,1},{6,2},{7,3},{8,11},{9,8},{10,9... | collective-permute-start | bytes 700424 | tf_op jit(solution)/shard_map/ppermute | solution.py:56
  57.8 6.1 %collective-permute-start.20 = (bf16[152,768]{1,0:T(8,128)(2,1)S(1)}, bf16[152,768]{1,0:T(8,128)(2,1)S(1)}, u32[]{:S(2)}, u32[]{:S(2)}) collective-permute-start(bf16[152,768]{1,0:T(8,128)(2,1)S(1)} %collective-permute-done.6.refs_1_), channel_id=1, source_target_pairs={{0,4},{1,5},{2,6},{3,7},{4,0},{5,1},{6,2},{7,3},{8,11},{9,8},{10,9... | collective-permute-start | bytes 700424 | tf_op jit(solution)/shard_map/ppermute | solution.py:56
  60.3 15.4 %collective-permute-start.5 = (bf16[152,768]{1,0:T(8,128)(2,1)S(1)}, bf16[152,768]{1,0:T(8,128)(2,1)S(1)}, u32[]{:S(2)}, u32[]{:S(2)}) collective-permute-start(bf16[152,768]{1,0:T(8,128)(2,1)S(1)} %collective-permute-done.4.refs_4_), channel_id=1, source_target_pairs={{0,4},{1,5},{2,6},{3,7},{4,0},{5,1},{6,2},{7,3},{8,9},{9,10},{10,1... | collective-permute-start | bytes 700424 | tf_op jit(solution)/shard_map/ppermute | solution.py:56
  63.8 11.9 %collective-permute-start.11 = (bf16[152,768]{1,0:T(8,128)(2,1)S(1)}, bf16[152,768]{1,0:T(8,128)(2,1)S(1)}, u32[]{:S(2)}, u32[]{:S(2)}) collective-permute-start(bf16[152,768]{1,0:T(8,128)(2,1)S(1)} %collective-permute-done.10.refs_10_), channel_id=1, source_target_pairs={{0,16},{1,17},{2,18},{3,19},{4,20},{5,21},{6,22},{7,23},{8,11},{9,... | collective-permute-start | bytes 700424 | tf_op jit(solution)/shard_map/ppermute | solution.py:56
  64.3 11.4 %collective-permute-start.14 = (bf16[152,768]{1,0:T(8,128)(2,1)S(1)}, bf16[152,768]{1,0:T(8,128)(2,1)S(1)}, u32[]{:S(2)}, u32[]{:S(2)}) collective-permute-start(bf16[152,768]{1,0:T(8,128)(2,1)S(1)} %collective-permute-done.13.refs_11_), channel_id=1, source_target_pairs={{0,16},{1,17},{2,18},{3,19},{4,20},{5,21},{6,22},{7,23},{8,11},{9,... | collective-permute-start | bytes 700424 | tf_op jit(solution)/shard_map/ppermute | solution.py:56
  65.9 9.9 %collective-permute-start.8 = (bf16[152,768]{1,0:T(8,128)(2,1)S(1)}, bf16[152,768]{1,0:T(8,128)(2,1)S(1)}, u32[]{:S(2)}, u32[]{:S(2)}) collective-permute-start(bf16[152,768]{1,0:T(8,128)(2,1)S(1)} %collective-permute-done.7.refs_5_), channel_id=1, source_target_pairs={{0,4},{1,5},{2,6},{3,7},{4,0},{5,1},{6,2},{7,3},{8,9},{9,10},{10,1... | collective-permute-start | bytes 700424 | tf_op jit(solution)/shard_map/ppermute | solution.py:56
  79.3 6.9 %collective-permute-start.32 = (bf16[144,768]{1,0:T(8,128)(2,1)S(1)}, bf16[144,768]{1,0:T(8,128)(2,1)S(1)}, u32[]{:S(2)}, u32[]{:S(2)}) collective-permute-start(bf16[144,768]{1,0:T(8,128)(2,1)S(1)} %get-tuple-element.70), channel_id=1, source_target_pairs={{0,16},{1,17},{2,18},{3,19},{4,20},{5,21},{6,22},{7,23},{8,9},{9,1... | collective-permute-start | bytes 663560 | tf_op jit(solution)/shard_map/ppermute | solution.py:56
  79.6 8.0 %collective-permute-start.28 = (bf16[144,768]{1,0:T(8,128)(2,1)S(1)}, bf16[144,768]{1,0:T(8,128)(2,1)S(1)}, u32[]{:S(2)}, u32[]{:S(2)}) collective-permute-start(bf16[144,768]{1,0:T(8,128)(2,1)S(1)} %get-tuple-element.66), channel_id=1, source_target_pairs={{0,16},{1,17},{2,18},{3,19},{4,20},{5,21},{6,22},{7,23},{8,9},{9,1... | collective-permute-start | bytes 663560 | tf_op jit(solution)/shard_map/ppermute | solution.py:56
  83.7 22.3 %collective-permute-start.30 = (bf16[288,768]{1,0:T(8,128)(2,1)S(1)}, bf16[288,768]{1,0:T(8,128)(2,1)S(1)}, u32[]{:S(2)}, u32[]{:S(2)}) collective-permute-start(bf16[288,768]{1,0:T(8,128)(2,1)S(1)} %get-tuple-element.67), channel_id=1, source_target_pairs={{0,16},{1,17},{2,18},{3,19},{4,20},{5,21},{6,22},{7,23},{8,11},{9,... | collective-permute-start | bytes 1327112 | tf_op jit(solution)/shard_map/ppermute | solution.py:56
  84.3 8.2 %collective-permute-start.22 = (bf16[144,768]{1,0:T(8,128)(2,1)S(1)}, bf16[144,768]{1,0:T(8,128)(2,1)S(1)}, u32[]{:S(2)}, u32[]{:S(2)}) collective-permute-start(bf16[144,768]{1,0:T(8,128)(2,1)S(1)} %get-tuple-element.59), channel_id=1, source_target_pairs={{0,4},{1,5},{2,6},{3,7},{4,0},{5,1},{6,2},{7,3},{8,11},{9,8},{10,9... | collective-permute-start | bytes 663560 | tf_op jit(solution)/shard_map/ppermute | solution.py:56
  86.1 22.4 %collective-permute-start.24 = (bf16[288,768]{1,0:T(8,128)(2,1)S(1)}, bf16[288,768]{1,0:T(8,128)(2,1)S(1)}, u32[]{:S(2)}, u32[]{:S(2)}) collective-permute-start(bf16[288,768]{1,0:T(8,128)(2,1)S(1)} %get-tuple-element.60), channel_id=1, source_target_pairs={{0,4},{1,5},{2,6},{3,7},{4,0},{5,1},{6,2},{7,3},{8,9},{9,10},{10,1... | collective-permute-start | bytes 1327112 | tf_op jit(solution)/shard_map/ppermute | solution.py:56
  87.6 16.6 %collective-permute-start.33 = (bf16[144,768]{1,0:T(8,128)(2,1)S(1)}, bf16[144,768]{1,0:T(8,128)(2,1)S(1)}, u32[]{:S(2)}, u32[]{:S(2)}) collective-permute-start(bf16[144,768]{1,0:T(8,128)(2,1)S(1)} %shard_map.81), channel_id=1, source_target_pairs={{0,4},{1,5},{2,6},{3,7},{4,0},{5,1},{6,2},{7,3},{8,9},{9,10},{10,1... | collective-permute-start | bytes 663560 | tf_op jit(solution)/shard_map/ppermute | solution.py:56
  90.0 17.2 %collective-permute-start.29 = (bf16[144,768]{1,0:T(8,128)(2,1)S(1)}, bf16[144,768]{1,0:T(8,128)(2,1)S(1)}, u32[]{:S(2)}, u32[]{:S(2)}) collective-permute-start(bf16[144,768]{1,0:T(8,128)(2,1)S(1)} %shard_map.79), channel_id=1, source_target_pairs={{0,4},{1,5},{2,6},{3,7},{4,0},{5,1},{6,2},{7,3},{8,9},{9,10},{10,1... | collective-permute-start | bytes 663560 | tf_op jit(solution)/shard_map/ppermute | solution.py:56
  92.5 16.0 %collective-permute-start.26 = (bf16[144,768]{1,0:T(8,128)(2,1)S(1)}, bf16[144,768]{1,0:T(8,128)(2,1)S(1)}, u32[]{:S(2)}, u32[]{:S(2)}) collective-permute-start(bf16[144,768]{1,0:T(8,128)(2,1)S(1)} %shard_map.77), channel_id=1, source_target_pairs={{0,16},{1,17},{2,18},{3,19},{4,20},{5,21},{6,22},{7,23},{8,11},{9,... | collective-permute-start | bytes 663560 | tf_op jit(solution)/shard_map/ppermute | solution.py:56
  106.0 7.5 %collective-permute-start.34 = (bf16[144,768]{1,0:T(8,128)(2,1)S(1)}, bf16[144,768]{1,0:T(8,128)(2,1)S(1)}, u32[]{:S(2)}, u32[]{:S(2)}) collective-permute-start(bf16[144,768]{1,0:T(8,128)(2,1)S(1)} %shard_map.82), channel_id=1, source_target_pairs={{0,2},{1,3},{2,0},{3,1},{4,6},{5,7},{6,4},{7,5},{8,28},{9,29},{10,... | collective-permute-start | bytes 663560 | tf_op jit(solution)/shard_map/ppermute | solution.py:56
  107.4 7.1 %collective-permute-start.31 = (bf16[144,768]{1,0:T(8,128)(2,1)S(1)}, bf16[144,768]{1,0:T(8,128)(2,1)S(1)}, u32[]{:S(2)}, u32[]{:S(2)}) collective-permute-start(bf16[144,768]{1,0:T(8,128)(2,1)S(1)} %shard_map.80), channel_id=1, source_target_pairs={{0,1},{1,2},{2,3},{3,0},{4,5},{5,6},{6,7},{7,4},{8,12},{9,13},{10,... | collective-permute-start | bytes 663560 | tf_op jit(solution)/shard_map/ppermute | solution.py:56
  108.6 7.3 %collective-permute-start.27 = (bf16[144,768]{1,0:T(8,128)(2,1)S(1)}, bf16[144,768]{1,0:T(8,128)(2,1)S(1)}, u32[]{:S(2)}, u32[]{:S(2)}) collective-permute-start(bf16[144,768]{1,0:T(8,128)(2,1)S(1)} %shard_map.78), channel_id=1, source_target_pairs={{0,3},{1,0},{2,1},{3,2},{4,7},{5,4},{6,5},{7,6},{8,24},{9,25},{10,... | collective-permute-start | bytes 663560 | tf_op jit(solution)/shard_map/ppermute | solution.py:56
  116.3 10.6 %collective-permute-start.35 = (bf16[40,768]{1,0:T(8,128)(2,1)S(1)}, bf16[40,768]{1,0:T(8,128)(2,1)S(1)}, u32[]{:S(2)}, u32[]{:S(2)}) collective-permute-start(bf16[40,768]{1,0:T(8,128)(2,1)S(1)} %get-tuple-element.72), channel_id=1, source_target_pairs={{0,192},{64,0},{128,64},{192,128},{1,193},{65,1},{129,65},{193,129... | collective-permute-start | bytes 184328 | tf_op jit(solution)/shard_map/ppermute | solution.py:60
  122.2 8.2 %collective-permute-start.36 = (bf16[40,768]{1,0:T(8,128)(2,1)S(1)}, bf16[40,768]{1,0:T(8,128)(2,1)S(1)}, u32[]{:S(2)}, u32[]{:S(2)}) collective-permute-start(bf16[40,768]{1,0:T(8,128)(2,1)S(1)} %get-tuple-element.73), channel_id=1, source_target_pairs={{0,128},{64,192},{128,0},{192,64},{1,129},{65,193},{129,1},{193,65... | collective-permute-start | bytes 184328 | tf_op jit(solution)/shard_map/ppermute | solution.py:60
  125.7 6.3 %collective-permute-start.37 = (bf16[40,768]{1,0:T(8,128)(2,1)S(1)}, bf16[40,768]{1,0:T(8,128)(2,1)S(1)}, u32[]{:S(2)}, u32[]{:S(2)}) collective-permute-start(bf16[40,768]{1,0:T(8,128)(2,1)S(1)} %get-tuple-element.74), channel_id=1, source_target_pairs={{0,64},{64,128},{128,192},{192,0},{1,65},{65,129},{129,193},{193,1... | collective-permute-start | bytes 184328 | tf_op jit(solution)/shard_map/ppermute | solution.py:60
  (8 other events, 90.1 us)

commit v3 on v2

--- a/solution.py
+++ b/solution.py
@@ -177,8 +177,30 @@
     out_ref[ROWS:] = sums_ref[...]
 
 
+def pair_kernel(first_ref, second_ref, out_ref):
+    out_ref[0] = first_ref[...]
+    out_ref[1] = second_ref[...]
+
+
+def views(tiles, keys):
+    arrays = []
+    where = []
+    for key in keys:
+        array, at = tiles[key]
+        known = [n for n, a in enumerate(arrays) if a is array]
+        if not known:
+            known = [len(arrays)]
+            arrays.append(array)
+        where.append((known[0], at))
+    return arrays, where
+
+
+def viewed(refs, where):
+    return [refs[n] if at is None else refs[n].at[at] for n, at in where]
+
+
 def unpack_kernel(*refs):
-    terms, out_refs = refs[:FAR], refs[FAR:]
+    terms, out_refs = refs[:-FAR], refs[-FAR:]
     total = sum(t[...].astype(F32) for t in terms).astype(BF16)
 
     def source_of(row):
@@ -211,13 +233,21 @@
     return high, (value - high.astype(F32)).astype(BF16)
 
 
-def stats_kernel(tokens_hbm, gain_hbm, router_hbm, out_ref, gain_ref, tokens_ref, router_ref, sems):
+def stats_kernel(tokens_hbm, gain_hbm, router_hbm, *refs):
+    weights, out_ref, gain_ref, weight_refs = refs[:3], refs[3], refs[4], refs[5:8]
+    tokens_ref, router_ref, sems, weight_sems = refs[8:]
     tokens, width = tokens_ref.shape
     part = lax.axis_index("zl") * 4 + lax.axis_index("x")
     here = pl.ds(pl.multiple_of(part * width, width), width)
     ways = ((tokens_hbm, tokens_ref), (gain_hbm, gain_ref), (router_hbm.at[:, here], router_ref))
     fetches = [pltpu.make_async_copy(a, b, sems.at[n]) for n, (a, b) in enumerate(ways)]
     for fetch in fetches:
+        fetch.start()
+    later = [
+        pltpu.make_async_copy(a, b, weight_sems.at[n])
+        for n, (a, b) in enumerate(zip(weights, weight_refs))
+    ]
+    for fetch in later:
         fetch.start()
     out_ref[...] = jnp.zeros_like(out_ref)
     for fetch in fetches:
@@ -230,26 +260,30 @@
         for k, v in enumerate(halves(sum(transposed_dot(left, t) for t in terms))):
             start = (2 * n + k) * 128
             out_ref[:, start : start + tokens] = v
-
-
-def stats(tokens, gain, router):
+    for fetch in later:
+        fetch.wait()
+
+
+def stats(tokens, gain, router, *weights):
     width = tokens.shape[1]
     return pl.pallas_call(
         stats_kernel,
         out_shape=[
             jax.ShapeDtypeStruct((EXTRA, width), BF16),
             jax.ShapeDtypeStruct(gain.shape, F32),
+            *(jax.ShapeDtypeStruct(w.shape, BF16) for w in weights),
         ],
-        in_specs=hbm(3),
-        out_specs=vmem(2),
+        in_specs=hbm(6),
+        out_specs=vmem(5),
         scratch_shapes=[
             pltpu.VMEM(tokens.shape, BF16),
             pltpu.VMEM((router.shape[0], width), BF16),
             pltpu.SemaphoreType.DMA((3,)),
+            pltpu.SemaphoreType.DMA((3,)),
         ],
         compiler_params=pltpu.CompilerParams(vmem_limit_bytes=4 << 20),
         name="stats",
-    )(*in_hbm(tokens, gain, router))
+    )(*in_hbm(tokens, gain, router, *weights))
 
 
 def stats_in(tile, tokens):
@@ -290,8 +324,10 @@
     return offset_place(jnp.where(core == 0, outer, inner), jnp.where(core == 0, inner, outer))
 
 
-CHUNK = 16
-EARLY = 12
+CHUNK = 48
+FIRST = ((0, 0), (0, 1), (0, 2), (0, 3), (1, 0), (1, 3), (2, 1), (2, 2))
+SECOND = ((1, 1), (1, 2), (2, 0), (2, 3))
+LAST = ((3, 0), (3, 1), (3, 2), (3, 3))
 
 
 def prepare(tile, gain, out_ref, row_start, column_at, squares_ref, squares_start):
@@ -300,10 +336,10 @@
     def step(n, _):
         at = pl.multiple_of(n * CHUNK, CHUNK)
         values = tile[pl.ds(at, CHUNK), :].astype(F32)
-        row_at = pl.ds(pl.multiple_of(row_start + at, CHUNK), CHUNK)
+        row_at = pl.ds(pl.multiple_of(row_start + at, 16), CHUNK)
         out_ref[row_at, column_at] = (values * gain).astype(BF16)
         square = values * values
-        squares_at = pl.ds(pl.multiple_of(squares_start + at, CHUNK), CHUNK)
+        squares_at = pl.ds(pl.multiple_of(squares_start + at, 16), CHUNK)
         squares_ref[squares_at, :] += sum(
             square[:, j * 128 : (j + 1) * 128] for j in range(width // 128)
         )
@@ -324,70 +360,80 @@
     return pl.ds(pl.multiple_of(feature * width, width), width)
 
 
-def early_kernel(gain_ref, *refs):
-    tiles, others, owns = refs[:EARLY], refs[EARLY : EARLY + 2], refs[EARLY + 2 : EARLY + 5]
-    acc_ref, squares_ref, sums_ref, *own_refs, x_ref, sems = refs[EARLY + 5 :]
-    copies = [
-        pltpu.make_async_copy(a, b, sems.at[n]) for n, (a, b) in enumerate(zip(owns, own_refs))
-    ]
-    for copy in copies:
-        copy.start()
+def place_tile(key, tile, gain_ref, x_ref, squares_ref, sums_ref):
+    row_class, feature = tile_place(*key)
+    column_at = columns_of(feature, tile.shape[1])
+    start = row_class * ROWS
+    prepare(tile, gain_ref[:, column_at], x_ref, start, column_at, squares_ref, start)
+    add_stats(tile, row_class, sums_ref)
+
+
+def fill_kernel(where, gain_ref, *refs):
+    tiles, (x_ref, squares_ref, sums_ref) = viewed(refs, where), refs[-3:]
     width = tiles[0].shape[1]
     squares_ref[...] = jnp.zeros_like(squares_ref)
     sums_ref[...] = jnp.zeros_like(sums_ref)
-    for index in range(16):
-        row_class, feature = tile_place(index // 4, index % 4)
-        column_at = columns_of(feature, width)
-        start = row_class * ROWS
-        if index < EARLY:
-            gain = gain_ref[:, column_at]
-            prepare(tiles[index], gain, x_ref, start, column_at, squares_ref, start)
-            add_stats(tiles[index], row_class, sums_ref)
-        else:
-            row_at = pl.ds(pl.multiple_of(start, ROWS), ROWS)
-            x_ref[row_at, column_at] = jnp.zeros((ROWS, width), BF16)
-    for n, weight in enumerate((*others, *own_refs[:2])):
-        if n >= 2:
-            copies[n - 2].wait()
+    for key, tile in zip(FIRST, tiles):
+        place_tile(key, tile, gain_ref, x_ref, squares_ref, sums_ref)
+    for key in LAST:
+        row_class, feature = tile_place(*key)
+        row_at = pl.ds(pl.multiple_of(row_class * ROWS, ROWS), ROWS)
+        x_ref[row_at, columns_of(feature, width)] = jnp.zeros((ROWS, width), BF16)
+
+
+def early_kernel(where, gain_ref, *refs):
+    tiles, weights = viewed(refs, where), refs[-11:-7]
+    acc_ref, x_ref, squares_ref, sums_ref = refs[-4:]
+    for key, tile in zip(SECOND, tiles):
+        place_tile(key, tile, gain_ref, x_ref, squares_ref, sums_ref)
+    for n, weight in enumerate(weights):
         acc_ref[n] = jnp.dot(x_ref[...], weight[...], preferred_element_type=F32)
-    copies[2].wait()
-
-
-def early_of(gain, tiles, others, owns, sums_shape):
-    width_all, slices = owns[0].shape
-    return pl.pallas_call(
-        early_kernel,
-        out_shape=[
-            jax.ShapeDtypeStruct((4, 2 * ROWS, slices), F32),
-            jax.ShapeDtypeStruct((2 * ROWS, 128), F32),
-            jax.ShapeDtypeStruct(sums_shape, F32),
-            *(jax.ShapeDtypeStruct(w.shape, BF16) for w in owns),
-        ],
-        in_specs=vmem(EARLY + 3) + hbm(3),
-        out_specs=vmem(6),
-        scratch_shapes=[
-            pltpu.VMEM((2 * ROWS, width_all), BF16),
-            pltpu.SemaphoreType.DMA((3,)),
-        ],
-        compiler_params=pltpu.CompilerParams(vmem_limit_bytes=20 << 20),
+
+
+def early_of(gain, tiles, weights, sums_shape):
+    width_all, slices = weights[0].shape
+    given = [
+        jax.ShapeDtypeStruct((2 * ROWS, width_all), BF16),
+        jax.ShapeDtypeStruct((2 * ROWS, 128), F32),
+        jax.ShapeDtypeStruct(sums_shape, F32),
+    ]
+    arrays, where = views(tiles, FIRST)
+    filled = pl.pallas_call(
+        partial(fill_kernel, where),
+        out_shape=given,
+        in_specs=vmem(1 + len(arrays)),
+        out_specs=vmem(3),
+        compiler_params=pltpu.CompilerParams(vmem_limit_bytes=8 << 20),
+        name="fill",
+    )(gain, *arrays)
+    arrays, where = views(tiles, SECOND)
+    at = 1 + len(arrays) + 4
+    acc, _, squares, sums = pl.pallas_call(
+        partial(early_kernel, where),
+        out_shape=[jax.ShapeDtypeStruct((4, 2 * ROWS, slices), F32), *given],
+        in_specs=vmem(at + 3),
+        out_specs=vmem(4),
+        input_output_aliases={at + n: 1 + n for n in range(3)},
+        compiler_params=pltpu.CompilerParams(vmem_limit_bytes=12 << 20),
         cost_estimate=pl.CostEstimate(
             flops=2 * 2 * ROWS * width_all * 4 * slices,
-            bytes_accessed=2 * width_all * slices * 2,
+            bytes_accessed=4 * width_all * slices * 2,
             transcendentals=0,
         ),
         name="early",
-    )(gain, *tiles, *others, *in_hbm(*owns))
-
-
-def late_kernel(width_all, gain_ref, *refs):
-    tiles, weights, refs = refs[:4], refs[4:8], refs[8:]
-    _, squares_in, sums_in, out_ref, sums_ref, acc_ref, squares_ref, x_ref = refs
+    )(gain, *arrays, *weights, *filled)
+    return acc, squares, sums
+
+
+def late_kernel(width_all, where, gain_ref, *refs):
+    tiles, weights = viewed(refs, where), refs[-12:-8]
+    _, squares_in, sums_in, out_ref, sums_ref, acc_ref, squares_ref, x_ref = refs[-8:]
     width = tiles[0].shape[1]
     slices = weights[0].shape[1]
     squares_ref[...] = squares_in[...]
     sums_ref[...] = sums_in[...]
-    for index, tile in enumerate(tiles):
-        row_class, feature = tile_place(3, index)
+    for key, tile in zip(LAST, tiles):
+        row_class, feature = tile_place(*key)
         column_at = columns_of(feature, width)
         start = row_class * ROWS
         gain = gain_ref[:, column_at]
@@ -409,17 +455,19 @@
 
 def late_of(gain, tiles, weights, acc, squares, sums):
     width_all, slices = weights[0].shape
-    width = tiles[0].shape[1]
+    arrays, where = views(tiles, LAST)
+    width = arrays[0].shape[-1]
+    at = 1 + len(arrays) + 4
     return pl.pallas_call(
-        partial(late_kernel, width_all),
+        partial(late_kernel, width_all, where),
         out_shape=[
             jax.ShapeDtypeStruct((2 * ROWS, 2 * slices), BF16),
             jax.ShapeDtypeStruct(sums.shape, F32),
             jax.ShapeDtypeStruct(acc.shape, F32),
         ],
-        in_specs=vmem(12),
+        in_specs=vmem(at + 3),
         out_specs=vmem(3),
-        input_output_aliases={9: 2},
+        input_output_aliases={at: 2},
         scratch_shapes=[
             pltpu.VMEM(squares.shape, F32),
             pltpu.VMEM((ROWS, width), BF16),
@@ -431,7 +479,7 @@
             transcendentals=0,
         ),
         name="late",
-    )(gain, *tiles, *weights, acc, squares, sums)[:2]
+    )(gain, *arrays, *weights, acc, squares, sums)[:2]
 
 
 def down_kernel(far, places, hidden_ref, own_ref, other_ref, *refs):
@@ -529,43 +577,55 @@
     gate_other = other_core(gate_proj)
     up_other = other_core(up_proj)
     down_other = other_core(down_proj)
-    part_sums, gain = stats(tokens, gain, router_weight.T)
+    part_sums, gain, gate_own, up_own, down_own = stats(
+        tokens, gain, router_weight.T, gate_proj, up_proj, down_proj
+    )
     (mine,) = small(pack_kernel, [(ROWS + EXTRA, width)], *arrived, part_sums)
 
-    inner = [mine, hop(mine, "x+", "y"), hop(mine, "x-", "z"), hop(mine, "xx", "yz")]
-    outer = [inner, [], [], [None] * 4]
-    for a in range(4):
-        outer[1].append(hop(inner[a], "y", "x+"))
-        outer[2].append(hop(inner[a], "z", "x-"))
-    for a in (0, 1):
-        outer[3][a] = hop(outer[1][a], "z", "x+")
-    for a in (2, 3):
-        outer[3][a] = hop(outer[2][a], "y", "x-")
-    tiles = [outer[m][a] for m in range(4) for a in range(4)]
+    one = hop(mine, "x+", "y")
+    two = hop(mine, "x-", "z")
+    opposite = hop(mine, "xx", "yz")
+    (pair,) = small(pair_kernel, [(2, ROWS + EXTRA, width)], one, two)
+    ring_one = [hop(v, "y", "x+") for v in (mine, pair, opposite)]
+    ring_two = [hop(v, "z", "x-") for v in (mine, pair, opposite)]
+    far_ones = [
+        hop(ring_one[0], "z", "x+"), hop(ring_two[1], "y", "x-"), hop(ring_one[2], "z", "x+")
+    ]
+    tiles = {(0, 0): (mine, None), (0, 1): (one, None), (0, 2): (two, None), (0, 3): (opposite, None)}
+    for m, ring in enumerate((ring_one, ring_two, far_ones), 1):
+        tiles[m, 0], tiles[m, 3] = (ring[0], None), (ring[2], None)
+        tiles[m, 1], tiles[m, 2] = (ring[1], 0), (ring[1], 1)
+
     sums_shape = (2 * router_weight.shape[1], tokens.shape[0])
-    acc, squares, sums, gate_own, up_own, down_own = early_of(
-        gain, tiles[:EARLY], (gate_other, up_other), (gate_proj, up_proj, down_proj), sums_shape
-    )
     weights = (gate_other, up_other, gate_own, up_own)
-    hidden, sums = late_of(gain, tiles[EARLY:], weights, acc, squares, sums)
-
-    far = down_of(True, [ROWS] * 4, [(a, 0) for a in range(4)], hidden, down_own, down_other)
+    acc, squares, sums = early_of(gain, tiles, weights, sums_shape)
+    hidden, sums = late_of(gain, tiles, weights, acc, squares, sums)
+
+    places = [(0, 0), (0, ROWS), (1, 0), (1, ROWS)]
+    far = down_of(True, [2 * ROWS] * 2, places, hidden, down_own, down_other)
     places = [(a, 0) for a in range(4)]
     places += [(4, 0), (5, 0), (8, 0), (8, ROWS)]
-    places += [(9, 0), (9, ROWS), (6, 0), (7, 0)]
-    shapes = [ROWS] * 8 + [2 * ROWS] * 2
+    places += [(9, 0), (10, 0), (6, 0), (7, 0)]
+    shapes = [ROWS] * 8 + [2 * ROWS] + [ROWS] * 2
     rest = down_of(False, shapes, places, hidden, down_own, down_other)
-    own, near, pairs = rest[:4], rest[4:8], rest[8:]
-    ways = [("z", "x-"), ("z", "x-"), ("y", "x+"), ("y", "x+")]
-    far_in = [hop(far[n], *ways[n]) for n in range(4)]
-    first = hop(pairs[0], "y", "x-")
-    second = hop(pairs[1], "z", "x+")
+    own, near, pair, singles = rest[:4], rest[4:8], rest[8], rest[9:]
+    far_pairs = [hop(far[0], "z", "x-"), hop(far[1], "y", "x+")]
+    far_in = [(far_pairs[n >> 1], (n & 1) * ROWS) for n in range(4)]
+    pair_in = hop(pair, "y", "x-")
+    singles_in = [hop(singles[n], "z", "x+") for n in range(2)]
     ways = [("y", "x-"), ("y", "x-"), ("z", "x+"), ("z", "x+")]
     near_in = [hop(added(near[n], far_in[n]), *ways[n]) for n in range(4)]
-    in_pairs = [(second, 0), (second, ROWS), (first, 0), (first, ROWS)]
-    total = [added(own[n], near_in[n], in_pairs[n]) for n in range(4)]
+    parts = [
+        (own[0], near_in[0], singles_in[0]),
+        (own[1], near_in[1], singles_in[1]),
+        (own[2], near_in[2], (pair_in, 0)),
+        (own[3], near_in[3], (pair_in, ROWS)),
+    ]
     terms = [
-        total[0], hop(total[1], "x-", "y"), hop(total[2], "x+", "z"), hop(total[3], "xx", "yz")
+        *parts[0],
+        hop(added(*parts[1]), "x-", "y"),
+        hop(added(*parts[2]), "x+", "z"),
+        hop(added(*parts[3]), "xx", "yz"),
     ]
     blocks = small(unpack_kernel, [block] * FAR, *terms)
     back = [blocks[0]] + [along_z(blocks[k], FAR - k) for k in (1, 2, 3)]

time: 139 us -> 128 us (0.921)
  starting transfers between devices: 57.1 us -> 50.8 us
  waiting for transfers between devices: 63.5 us -> 58.6 us
    ppermute x28 -> x24, waiting for transfers between devices: 50.3 us -> 45.6 us  [hop(): return lax.ppermute(value, OWNER, owner_pairs(step_core0, step_core1))]
    ppermute x28 -> x24, starting transfers between devices: 27.6 us -> 24.1 us  [hop(): return lax.ppermute(value, OWNER, owner_pairs(step_core0, step_core1))]
    pallas_call x2 -> x3, Pallas kernels: 10.1 us -> 6.96 us  [the longest x1 4.16 us: early_of(): pl.pallas_call(partial(early_kernel, where), out_shape=[jax.ShapeDtypeStr...]
    pallas_call x1, Pallas kernels: 1.15 us -> 3.87 us  [stats(): pl.pallas_call(stats_kernel, out_shape=[jax.ShapeDtypeStruct((EXTRA, widt...]
    ppermute x6, starting transfers between devices: 22.9 us -> 20.7 us  [along_z(): lax.ppermute(value, 'zh', [(i, (i + distance) % FAR) for i in range(FAR)])]
  transfers between devices with their start and end apart: 39 -> 35, of which waited for: 23 -> 20; matrix products, arithmetic and copies ran while one was open for 0% -> 0% of each run, Pallas kernels for 11% -> 12%
where the time goes in v3:
time: 128 us
  waiting for transfers between devices  58.6 us (46%)
  starting transfers between devices  50.8 us (40%)
  Pallas kernels  18.2 us (14%)
    ppermute x24, waiting for transfers between devices, hop(): return lax.ppermute(value, OWNER, owner_pairs(step_core0, step_core1))  45.6 us
    ppermute x24, starting transfers between devices, hop(): return lax.ppermute(value, OWNER, owner_pairs(step_core0, step_core1))  24.1 us
    ppermute x6, starting transfers between devices, along_z(): lax.ppermute(value, 'zh', [(i, (i + distance) % FAR) for i in range(FAR)])  20.7 us
    ppermute x2, waiting for transfers between devices, across_y(): return lax.ppermute(value, ('y2', 'y1'), [(i, 3 - i) for i in range(4)])  7.45 us
    ppermute x6, waiting for transfers between devices, along_z(): lax.ppermute(value, 'zh', [(i, (i + distance) % FAR) for i in range(FAR)])  5.6 us
    ppermute x2, starting transfers between devices, across_y(): return lax.ppermute(value, ('y2', 'y1'), [(i, 3 - i) for i in range(4)])  5.43 us
    pallas_call x1, Pallas kernels, early_of(): pl.pallas_call(partial(early_kernel, where), out_shape=[jax.ShapeDtypeStr...  4.16 us
    pallas_call x1, Pallas kernels, stats(): pl.pallas_call(stats_kernel, out_shape=[jax.ShapeDtypeStruct((EXTRA, widt...  3.87 us
  transfers between devices with their start and end apart: 35, of which 20 were waited for; matrix products, arithmetic and copies ran while one was open for 0% of the time, Pallas kernels for 12%

profile of v3, /device:TPU:6, one launch (start us, length us, event | category | flops | bytes accessed | tf_op | source)
XLA Modules:
  0.0 127.8 jit_solution(107570506522512284)
XLA Ops:
  1.7 3.1 %collective-permute-start = (bf16[72,768]{1,0:T(8,128)(2,1)S(1)}, bf16[72,768]{1,0:T(8,128)(2,1)S(1)}, u32[]{:S(2)}, u32[]{:S(2)}) collective-permute-start(bf16[72,768]{1,0:T(8,128)(2,1)S(1)} %get-tuple-element.45), channel_id=1, source_target_pairs={{0,48},{16,32},{32,16},{48,0},{1,49},{17,33},{33,17},{49,1},{2,50}... | collective-permute-start | bytes 331784 | tf_op jit(solution)/shard_map/ppermute | solution.py:64
  4.8 3.7 %collective-permute-done.came_ref = bf16[72,768]{1,0:T(8,128)(2,1)S(1)} collective-permute-done((bf16[72,768]{1,0:T(8,128)(2,1)S(1)}, bf16[72,768]{1,0:T(8,128)(2,1)S(1)}, u32[]{:S(2)}, u32[]{:S(2)}) %collective-permute-start) | collective-permute-done | bytes 110624 | tf_op jit(solution)/shard_map/ppermute | solution.py:64
  8.7 3.3 %collective-permute-start.1 = (bf16[40,768]{1,0:T(8,128)(2,1)S(1)}, bf16[40,768]{1,0:T(8,128)(2,1)S(1)}, u32[]{:S(2)}, u32[]{:S(2)}) collective-permute-start(bf16[40,768]{1,0:T(8,128)(2,1)S(1)} %get-tuple-element.47), channel_id=1, source_target_pairs={{0,64},{64,128},{128,192},{192,0},{1,65},{65,129},{129,193},{193,1... | collective-permute-start | bytes 184328 | tf_op jit(solution)/shard_map/ppermute | solution.py:60
  12.1 5.4 %collective-permute-start.2 = (bf16[40,768]{1,0:T(8,128)(2,1)S(1)}, bf16[40,768]{1,0:T(8,128)(2,1)S(1)}, u32[]{:S(2)}, u32[]{:S(2)}) collective-permute-start(bf16[40,768]{1,0:T(8,128)(2,1)S(1)} %get-tuple-element.48), channel_id=1, source_target_pairs={{0,128},{64,192},{128,0},{192,64},{1,129},{65,193},{129,1},{193,65... | collective-permute-start | bytes 184328 | tf_op jit(solution)/shard_map/ppermute | solution.py:60
  17.5 3.6 %collective-permute-start.3 = (bf16[40,768]{1,0:T(8,128)(2,1)S(1)}, bf16[40,768]{1,0:T(8,128)(2,1)S(1)}, u32[]{:S(2)}, u32[]{:S(2)}) collective-permute-start(bf16[40,768]{1,0:T(8,128)(2,1)S(1)} %get-tuple-element.49), channel_id=1, source_target_pairs={{0,192},{64,0},{128,64},{192,128},{1,193},{65,1},{129,65},{193,129... | collective-permute-start | bytes 184328 | tf_op jit(solution)/shard_map/ppermute | solution.py:60
  21.1 3.9 %stats.1 = (bf16[8,768]{1,0:T(8,128)(2,1)S(1)}, f32[1,6144]{1,0:T(1,128)S(1)}, bf16[6144,256]{1,0:T(8,128)(2,1)S(1)}, bf16[6144,256]{1,0:T(8,128)(2,1)S(1)}, bf16[256,6144]{1,0:T(8,128)(2,1)S(1)}) custom-call(bf16[64,768]{1,0:T(8,128)(2,1)} %tokens_hbm.3, f32[1,6144]{1,0:T(1,128)} %bitcast.6, bf16[8,6144]{1,0:T(8,128)(2,1)} %bitcast.5, ...), custom_call_target="tpu_custom_call" | custom-call | tf_op jit(solution)/shard_map/stats/pallas_call | solution.py:269
  27.3 4.0 %collective-permute-done.6.first_ref.refs_1_ = bf16[152,768]{1,0:T(8,128)(2,1)S(1)} collective-permute-done((bf16[152,768]{1,0:T(8,128)(2,1)S(1)}, bf16[152,768]{1,0:T(8,128)(2,1)S(1)}, u32[]{:S(2)}, u32[]{:S(2)}) %collective-permute-start.6) | collective-permute-done | bytes 233504 | tf_op jit(solution)/shard_map/ppermute | solution.py:56
  33.3 8.1 %collective-permute-done.10.refs_3_ = bf16[152,768]{1,0:T(8,128)(2,1)S(1)} collective-permute-done((bf16[152,768]{1,0:T(8,128)(2,1)S(1)}, bf16[152,768]{1,0:T(8,128)(2,1)S(1)}, u32[]{:S(2)}, u32[]{:S(2)}) %collective-permute-start.10) | collective-permute-done | bytes 233504 | tf_op jit(solution)/shard_map/ppermute | solution.py:56
  41.4 2.8 %collective-permute-start.16 = (bf16[152,768]{1,0:T(8,128)(2,1)S(1)}, bf16[152,768]{1,0:T(8,128)(2,1)S(1)}, u32[]{:S(2)}, u32[]{:S(2)}) collective-permute-start(bf16[152,768]{1,0:T(8,128)(2,1)S(1)} %shard_map.74.refs_0_), channel_id=1, source_target_pairs={{0,4},{1,5},{2,6},{3,7},{4,0},{5,1},{6,2},{7,3},{8,11},{9,8},{10,9... | collective-permute-start | bytes 700424 | tf_op jit(solution)/shard_map/ppermute | solution.py:56
  44.2 4.0 %collective-permute-done.16.refs_1_ = bf16[152,768]{1,0:T(8,128)(2,1)S(1)} collective-permute-done((bf16[152,768]{1,0:T(8,128)(2,1)S(1)}, bf16[152,768]{1,0:T(8,128)(2,1)S(1)}, u32[]{:S(2)}, u32[]{:S(2)}) %collective-permute-start.16) | collective-permute-done | bytes 233504 | tf_op jit(solution)/shard_map/ppermute | solution.py:56
  48.2 2.0 %collective-permute-start.17 = (bf16[152,768]{1,0:T(8,128)(2,1)S(1)}, bf16[152,768]{1,0:T(8,128)(2,1)S(1)}, u32[]{:S(2)}, u32[]{:S(2)}) collective-permute-start(bf16[152,768]{1,0:T(8,128)(2,1)S(1)} %collective-permute-done.10.refs_3_), channel_id=1, source_target_pairs={{0,4},{1,5},{2,6},{3,7},{4,0},{5,1},{6,2},{7,3},{8,11},{9,8},{10,9... | collective-permute-start | bytes 700424 | tf_op jit(solution)/shard_map/ppermute | solution.py:56
  50.4 3.9 %collective-permute-done.17.refs_2_ = bf16[152,768]{1,0:T(8,128)(2,1)S(1)} collective-permute-done((bf16[152,768]{1,0:T(8,128)(2,1)S(1)}, bf16[152,768]{1,0:T(8,128)(2,1)S(1)}, u32[]{:S(2)}, u32[]{:S(2)}) %collective-permute-start.17) | collective-permute-done | bytes 233504 | tf_op jit(solution)/shard_map/ppermute | solution.py:56
  54.3 5.0 %collective-permute-done.8.refs_6_ = bf16[2,152,768]{2,1,0:T(8,128)(2,1)S(1)} collective-permute-done((bf16[2,152,768]{2,1,0:T(8,128)(2,1)S(1)}, bf16[2,152,768]{2,1,0:T(8,128)(2,1)S(1)}, u32[]{:S(2)}, u32[]{:S(2)}) %collective-permute-start.8) | collective-permute-done | bytes 466976 | tf_op jit(solution)/shard_map/ppermute | solution.py:56
  60.1 2.8 %collective-permute-done.15.refs_0_ = bf16[2,152,768]{2,1,0:T(8,128)(2,1)S(1)} collective-permute-done((bf16[2,152,768]{2,1,0:T(8,128)(2,1)S(1)}, bf16[2,152,768]{2,1,0:T(8,128)(2,1)S(1)}, u32[]{:S(2)}, u32[]{:S(2)}) %collective-permute-start.15) | collective-permute-done | bytes 466976 | tf_op jit(solution)/shard_map/ppermute | solution.py:56
  62.9 2.0 %collective-permute-start.5 = (bf16[152,768]{1,0:T(8,128)(2,1)S(1)}, bf16[152,768]{1,0:T(8,128)(2,1)S(1)}, u32[]{:S(2)}, u32[]{:S(2)}) collective-permute-start(bf16[152,768]{1,0:T(8,128)(2,1)S(1)} %collective-permute-done.4.refs_4_), channel_id=1, source_target_pairs={{0,4},{1,5},{2,6},{3,7},{4,0},{5,1},{6,2},{7,3},{8,9},{9,10},{10,1... | collective-permute-start | bytes 700424 | tf_op jit(solution)/shard_map/ppermute | solution.py:56
  64.9 4.2 %early.1 = (f32[4,288,256]{2,1,0:T(8,128)S(1)}, bf16[288,6144]{1,0:T(8,128)(2,1)S(1)}, f32[288,128]{1,0:T(8,128)S(1)}, f32[16,64]{1,0:T(8,128)S(1)}) custom-call(f32[1,6144]{1,0:T(1,128)S(1)} %get-tuple-element.43.gain_ref, bf16[2,152,768]{2,1,0:T(8,128)(2,1)S(1)} %collective-permute-done.15.refs_0_, ...), custom_call_target="tpu_custom_call", output_to_operand_aliasing={{1}: (8, {}), {2}: (9, {}), {3}: (10, {})} | custom-call | flops 3623878656 | bytes 12582912 | tf_op jit(solution)/shard_map/early/pallas_call | solution.py:411
  69.1 2.3 %collective-permute-done.12.refs_2_ = bf16[152,768]{1,0:T(8,128)(2,1)S(1)} collective-permute-done((bf16[152,768]{1,0:T(8,128)(2,1)S(1)}, bf16[152,768]{1,0:T(8,128)(2,1)S(1)}, u32[]{:S(2)}, u32[]{:S(2)}) %collective-permute-start.12) | collective-permute-done | bytes 233504 | tf_op jit(solution)/shard_map/ppermute | solution.py:56
  71.4 2.0 %late.1 = (bf16[288,512]{1,0:T(8,128)(2,1)S(1)}, f32[16,64]{1,0:T(8,128)S(1)}, f32[4,288,256]{2,1,0:T(8,128)S(1)}) custom-call(f32[1,6144]{1,0:T(1,128)S(1)} %get-tuple-element.43.gain_ref, bf16[152,768]{1,0:T(8,128)(2,1)S(1)} %collective-permute-done.5.refs_0_, ...), custom_call_target="tpu_custom_call", output_to_operand_aliasing={{2}: (8, {})} | custom-call | flops 905969664 | bytes 2359296 | tf_op jit(solution)/shard_map/late/pallas_call | solution.py:461
  74.8 2.1 %collective-permute-start.19 = (bf16[288,768]{1,0:T(8,128)(2,1)S(1)}, bf16[288,768]{1,0:T(8,128)(2,1)S(1)}, u32[]{:S(2)}, u32[]{:S(2)}) collective-permute-start(bf16[288,768]{1,0:T(8,128)(2,1)S(1)} %get-tuple-element.64), channel_id=1, source_target_pairs={{0,4},{1,5},{2,6},{3,7},{4,0},{5,1},{6,2},{7,3},{8,11},{9,8},{10,9... | collective-permute-start | bytes 1327112 | tf_op jit(solution)/shard_map/ppermute | solution.py:56
  76.9 2.3 %rest.1 = (bf16[144,768]{1,0:T(8,128)(2,1)S(1)}, bf16[144,768]{1,0:T(8,128)(2,1)S(1)}, bf16[144,768]{1,0:T(8,128)(2,1)S(1)}, bf16[144,768]{1,0:T(8,128)(2,1)S(1)...) custom-call(bf16[288,512]{1,0:T(8,128)(2,1)S(1)} %get-tuple-element., ...), custom_call_target="tpu_custom_call" | custom-call | flops 1358954496 | bytes 6291456 | tf_op jit(solution)/shard_map/rest/pallas_call | solution.py:534
  79.2 2.0 %collective-permute-start.27 = (bf16[288,768]{1,0:T(8,128)(2,1)S(1)}, bf16[288,768]{1,0:T(8,128)(2,1)S(1)}, u32[]{:S(2)}, u32[]{:S(2)}) collective-permute-start(bf16[288,768]{1,0:T(8,128)(2,1)S(1)} %get-tuple-element.72), channel_id=1, source_target_pairs={{0,16},{1,17},{2,18},{3,19},{4,20},{5,21},{6,22},{7,23},{8,11},{9,... | collective-permute-start | bytes 1327112 | tf_op jit(solution)/shard_map/ppermute | solution.py:56
  81.2 1.8 %collective-permute-done.25.refs_1_ = bf16[288,768]{1,0:T(8,128)(2,1)S(1)} collective-permute-done((bf16[288,768]{1,0:T(8,128)(2,1)S(1)}, bf16[288,768]{1,0:T(8,128)(2,1)S(1)}, u32[]{:S(2)}, u32[]{:S(2)}) %collective-permute-start.25) | collective-permute-done | bytes 442400 | tf_op jit(solution)/shard_map/ppermute | solution.py:56
  83.2 2.1 %collective-permute-start.29 = (bf16[144,768]{1,0:T(8,128)(2,1)S(1)}, bf16[144,768]{1,0:T(8,128)(2,1)S(1)}, u32[]{:S(2)}, u32[]{:S(2)}) collective-permute-start(bf16[144,768]{1,0:T(8,128)(2,1)S(1)} %shard_map.81), channel_id=1, source_target_pairs={{0,4},{1,5},{2,6},{3,7},{4,0},{5,1},{6,2},{7,3},{8,9},{9,10},{10,1... | collective-permute-start | bytes 663560 | tf_op jit(solution)/shard_map/ppermute | solution.py:56
  85.4 2.0 %collective-permute-start.23 = (bf16[144,768]{1,0:T(8,128)(2,1)S(1)}, bf16[144,768]{1,0:T(8,128)(2,1)S(1)}, u32[]{:S(2)}, u32[]{:S(2)}) collective-permute-start(bf16[144,768]{1,0:T(8,128)(2,1)S(1)} %get-tuple-element.68), channel_id=1, source_target_pairs={{0,4},{1,5},{2,6},{3,7},{4,0},{5,1},{6,2},{7,3},{8,9},{9,10},{10,1... | collective-permute-start | bytes 663560 | tf_op jit(solution)/shard_map/ppermute | solution.py:56
  87.9 1.8 %collective-permute-done.27.refs_2_ = bf16[288,768]{1,0:T(8,128)(2,1)S(1)} collective-permute-done((bf16[288,768]{1,0:T(8,128)(2,1)S(1)}, bf16[288,768]{1,0:T(8,128)(2,1)S(1)}, u32[]{:S(2)}, u32[]{:S(2)}) %collective-permute-start.27) | collective-permute-done | bytes 442400 | tf_op jit(solution)/shard_map/ppermute | solution.py:56
  92.7 3.4 %collective-permute-done.26.refs_1_ = bf16[144,768]{1,0:T(8,128)(2,1)S(1)} collective-permute-done((bf16[144,768]{1,0:T(8,128)(2,1)S(1)}, bf16[144,768]{1,0:T(8,128)(2,1)S(1)}, u32[]{:S(2)}, u32[]{:S(2)}) %collective-permute-start.26) | collective-permute-done | bytes 221216 | tf_op jit(solution)/shard_map/ppermute | solution.py:56
  96.3 2.2 %collective-permute-done.23.refs_2_ = bf16[144,768]{1,0:T(8,128)(2,1)S(1)} collective-permute-done((bf16[144,768]{1,0:T(8,128)(2,1)S(1)}, bf16[144,768]{1,0:T(8,128)(2,1)S(1)}, u32[]{:S(2)}, u32[]{:S(2)}) %collective-permute-start.23) | collective-permute-done | bytes 221216 | tf_op jit(solution)/shard_map/ppermute | solution.py:56
  106.5 5.1 %collective-permute-start.31 = (bf16[40,768]{1,0:T(8,128)(2,1)S(1)}, bf16[40,768]{1,0:T(8,128)(2,1)S(1)}, u32[]{:S(2)}, u32[]{:S(2)}) collective-permute-start(bf16[40,768]{1,0:T(8,128)(2,1)S(1)} %get-tuple-element.76), channel_id=1, source_target_pairs={{0,192},{64,0},{128,64},{192,128},{1,193},{65,1},{129,65},{193,129... | collective-permute-start | bytes 184328 | tf_op jit(solution)/shard_map/ppermute | solution.py:60
  113.0 1.9 %collective-permute-start.33 = (bf16[40,768]{1,0:T(8,128)(2,1)S(1)}, bf16[40,768]{1,0:T(8,128)(2,1)S(1)}, u32[]{:S(2)}, u32[]{:S(2)}) collective-permute-start(bf16[40,768]{1,0:T(8,128)(2,1)S(1)} %get-tuple-element.78), channel_id=1, source_target_pairs={{0,64},{64,128},{128,192},{192,0},{1,65},{65,129},{129,193},{193,1... | collective-permute-start | bytes 184328 | tf_op jit(solution)/shard_map/ppermute | solution.py:60
  114.9 5.6 %collective-permute-done.32.refs_2_ = bf16[40,768]{1,0:T(8,128)(2,1)S(1)} collective-permute-done((bf16[40,768]{1,0:T(8,128)(2,1)S(1)}, bf16[40,768]{1,0:T(8,128)(2,1)S(1)}, u32[]{:S(2)}, u32[]{:S(2)}) %collective-permute-start.32) | collective-permute-done | bytes 61472 | tf_op jit(solution)/shard_map/ppermute | solution.py:60
  120.7 2.3 %collective-permute-start.34 = (bf16[72,768]{1,0:T(8,128)(2,1)S(1)}, bf16[72,768]{1,0:T(8,128)(2,1)S(1)}, u32[]{:S(2)}, u32[]{:S(2)}) collective-permute-start(bf16[72,768]{1,0:T(8,128)(2,1)S(1)} %get-tuple-element.80), channel_id=1, source_target_pairs={{0,48},{16,32},{32,16},{48,0},{1,49},{17,33},{33,17},{49,1},{2,50}... | collective-permute-start | bytes 331784 | tf_op jit(solution)/shard_map/ppermute | solution.py:64
  123.0 3.7 %collective-permute-done.34.came_ref = bf16[72,768]{1,0:T(8,128)(2,1)S(1)} collective-permute-done((bf16[72,768]{1,0:T(8,128)(2,1)S(1)}, bf16[72,768]{1,0:T(8,128)(2,1)S(1)}, u32[]{:S(2)}, u32[]{:S(2)}) %collective-permute-start.34) | collective-permute-done | bytes 110624 | tf_op jit(solution)/shard_map/ppermute | solution.py:64
  (60 shorter events, 23.1 us)
Async XLA Ops:
  0.0 64.9 %collective-permute-start.13 = (bf16[6144,256]{1,0:T(8,128)(2,1)}, bf16[6144,256]{1,0:T(8,128)(2,1)S(1)}, u32[]{:S(2)}, u32[]{:S(2)}) collective-permute-start(bf16[6144,256]{1,0:T(8,128)(2,1)} %refs_0_.1), channel_id=1, source_target_pairs={{0,8},{8,0},{1,9},{9,1},{2,10},{10,2},{3,11},{11,3},{4,12},{12,4},... | collective-permute-start | bytes 9437192 | tf_op jit(solution)/shard_map/ppermute | solution.py:68
  0.0 64.9 %collective-permute-start.14 = (bf16[6144,256]{1,0:T(8,128)(2,1)}, bf16[6144,256]{1,0:T(8,128)(2,1)S(1)}, u32[]{:S(2)}, u32[]{:S(2)}) collective-permute-start(bf16[6144,256]{1,0:T(8,128)(2,1)} %refs_1_.1), channel_id=1, source_target_pairs={{0,8},{8,0},{1,9},{9,1},{2,10},{10,2},{3,11},{11,3},{4,12},{12,4},... | collective-permute-start | bytes 9437192 | tf_op jit(solution)/shard_map/ppermute | solution.py:68
  0.5 72.9 %collective-permute-start.18 = (bf16[256,6144]{1,0:T(8,128)(2,1)}, bf16[256,6144]{1,0:T(8,128)(2,1)S(1)}, u32[]{:S(2)}, u32[]{:S(2)}) collective-permute-start(bf16[256,6144]{1,0:T(8,128)(2,1)} %refs_2_.1), channel_id=1, source_target_pairs={{0,8},{8,0},{1,9},{9,1},{2,10},{10,2},{3,11},{11,3},{4,12},{12,4},... | collective-permute-start | bytes 9437192 | tf_op jit(solution)/shard_map/ppermute | solution.py:68
  1.7 6.8 %collective-permute-start = (bf16[72,768]{1,0:T(8,128)(2,1)S(1)}, bf16[72,768]{1,0:T(8,128)(2,1)S(1)}, u32[]{:S(2)}, u32[]{:S(2)}) collective-permute-start(bf16[72,768]{1,0:T(8,128)(2,1)S(1)} %get-tuple-element.45), channel_id=1, source_target_pairs={{0,48},{16,32},{32,16},{48,0},{1,49},{17,33},{33,17},{49,1},{2,50}... | collective-permute-start | bytes 331784 | tf_op jit(solution)/shard_map/ppermute | solution.py:64
  8.7 8.7 %collective-permute-start.1 = (bf16[40,768]{1,0:T(8,128)(2,1)S(1)}, bf16[40,768]{1,0:T(8,128)(2,1)S(1)}, u32[]{:S(2)}, u32[]{:S(2)}) collective-permute-start(bf16[40,768]{1,0:T(8,128)(2,1)S(1)} %get-tuple-element.47), channel_id=1, source_target_pairs={{0,64},{64,128},{128,192},{192,0},{1,65},{65,129},{129,193},{193,1... | collective-permute-start | bytes 184328 | tf_op jit(solution)/shard_map/ppermute | solution.py:60
  12.1 12.9 %collective-permute-start.2 = (bf16[40,768]{1,0:T(8,128)(2,1)S(1)}, bf16[40,768]{1,0:T(8,128)(2,1)S(1)}, u32[]{:S(2)}, u32[]{:S(2)}) collective-permute-start(bf16[40,768]{1,0:T(8,128)(2,1)S(1)} %get-tuple-element.48), channel_id=1, source_target_pairs={{0,128},{64,192},{128,0},{192,64},{1,129},{65,193},{129,1},{193,65... | collective-permute-start | bytes 184328 | tf_op jit(solution)/shard_map/ppermute | solution.py:60
  17.5 7.5 %collective-permute-start.3 = (bf16[40,768]{1,0:T(8,128)(2,1)S(1)}, bf16[40,768]{1,0:T(8,128)(2,1)S(1)}, u32[]{:S(2)}, u32[]{:S(2)}) collective-permute-start(bf16[40,768]{1,0:T(8,128)(2,1)S(1)} %get-tuple-element.49), channel_id=1, source_target_pairs={{0,192},{64,0},{128,64},{192,128},{1,193},{65,1},{129,65},{193,129... | collective-permute-start | bytes 184328 | tf_op jit(solution)/shard_map/ppermute | solution.py:60
  25.2 6.1 %collective-permute-start.6 = (bf16[152,768]{1,0:T(8,128)(2,1)S(1)}, bf16[152,768]{1,0:T(8,128)(2,1)S(1)}, u32[]{:S(2)}, u32[]{:S(2)}) collective-permute-start(bf16[152,768]{1,0:T(8,128)(2,1)S(1)} %shard_map.74.refs_0_), channel_id=1, source_target_pairs={{0,1},{1,2},{2,3},{3,0},{4,5},{5,6},{6,7},{7,4},{8,24},{9,25},{10,... | collective-permute-start | bytes 700424 | tf_op jit(solution)/shard_map/ppermute | solution.py:56
  25.8 7.3 %collective-permute-start.7 = (bf16[152,768]{1,0:T(8,128)(2,1)S(1)}, bf16[152,768]{1,0:T(8,128)(2,1)S(1)}, u32[]{:S(2)}, u32[]{:S(2)}) collective-permute-start(bf16[152,768]{1,0:T(8,128)(2,1)S(1)} %shard_map.74.refs_0_), channel_id=1, source_target_pairs={{0,3},{1,0},{2,1},{3,2},{4,7},{5,4},{6,5},{7,6},{8,12},{9,13},{10,... | collective-permute-start | bytes 700424 | tf_op jit(solution)/shard_map/ppermute | solution.py:56
  31.4 10.0 %collective-permute-start.10 = (bf16[152,768]{1,0:T(8,128)(2,1)S(1)}, bf16[152,768]{1,0:T(8,128)(2,1)S(1)}, u32[]{:S(2)}, u32[]{:S(2)}) collective-permute-start(bf16[152,768]{1,0:T(8,128)(2,1)S(1)} %shard_map.74.refs_0_), channel_id=1, source_target_pairs={{0,2},{1,3},{2,0},{3,1},{4,6},{5,7},{6,4},{7,5},{8,28},{9,29},{10,... | collective-permute-start | bytes 700424 | tf_op jit(solution)/shard_map/ppermute | solution.py:56
  33.0 11.1 %collective-permute-start.4 = (bf16[152,768]{1,0:T(8,128)(2,1)S(1)}, bf16[152,768]{1,0:T(8,128)(2,1)S(1)}, u32[]{:S(2)}, u32[]{:S(2)}) collective-permute-start(bf16[152,768]{1,0:T(8,128)(2,1)S(1)} %shard_map.74.refs_0_), channel_id=1, source_target_pairs={{0,16},{1,17},{2,18},{3,19},{4,20},{5,21},{6,22},{7,23},{8,9},{9,1... | collective-permute-start | bytes 700424 | tf_op jit(solution)/shard_map/ppermute | solution.py:56
  41.4 6.9 %collective-permute-start.16 = (bf16[152,768]{1,0:T(8,128)(2,1)S(1)}, bf16[152,768]{1,0:T(8,128)(2,1)S(1)}, u32[]{:S(2)}, u32[]{:S(2)}) collective-permute-start(bf16[152,768]{1,0:T(8,128)(2,1)S(1)} %shard_map.74.refs_0_), channel_id=1, source_target_pairs={{0,4},{1,5},{2,6},{3,7},{4,0},{5,1},{6,2},{7,3},{8,11},{9,8},{10,9... | collective-permute-start | bytes 700424 | tf_op jit(solution)/shard_map/ppermute | solution.py:56
  44.2 6.1 %collective-permute-start.11 = (bf16[152,768]{1,0:T(8,128)(2,1)S(1)}, bf16[152,768]{1,0:T(8,128)(2,1)S(1)}, u32[]{:S(2)}, u32[]{:S(2)}) collective-permute-start(bf16[152,768]{1,0:T(8,128)(2,1)S(1)} %collective-permute-done.10.refs_3_), channel_id=1, source_target_pairs={{0,16},{1,17},{2,18},{3,19},{4,20},{5,21},{6,22},{7,23},{8,9},{9,1... | collective-permute-start | bytes 700424 | tf_op jit(solution)/shard_map/ppermute | solution.py:56
  50.3 9.0 %collective-permute-start.8 = (bf16[2,152,768]{2,1,0:T(8,128)(2,1)S(1)}, bf16[2,152,768]{2,1,0:T(8,128)(2,1)S(1)}, u32[]{:S(2)}, u32[]{:S(2)}) collective-permute-start(bf16[2,152,768]{2,1,0:T(8,128)(2,1)S(1)} %shard_map.75), channel_id=1, source_target_pairs={{0,4},{1,5},{2,6},{3,7},{4,0},{5,1},{6,2},{7,3},{8,11},{9,8},{10,9... | collective-permute-start | bytes 1400840 | tf_op jit(solution)/shard_map/ppermute | solution.py:56
  54.3 8.6 %collective-permute-start.15 = (bf16[2,152,768]{2,1,0:T(8,128)(2,1)S(1)}, bf16[2,152,768]{2,1,0:T(8,128)(2,1)S(1)}, u32[]{:S(2)}, u32[]{:S(2)}) collective-permute-start(bf16[2,152,768]{2,1,0:T(8,128)(2,1)S(1)} %shard_map.75), channel_id=1, source_target_pairs={{0,16},{1,17},{2,18},{3,19},{4,20},{5,21},{6,22},{7,23},{8,9},{9,1... | collective-permute-start | bytes 1400840 | tf_op jit(solution)/shard_map/ppermute | solution.py:56
  59.3 12.1 %collective-permute-start.9 = (bf16[2,152,768]{2,1,0:T(8,128)(2,1)S(1)}, bf16[2,152,768]{2,1,0:T(8,128)(2,1)S(1)}, u32[]{:S(2)}, u32[]{:S(2)}) collective-permute-start(bf16[2,152,768]{2,1,0:T(8,128)(2,1)S(1)} %collective-permute-done.8.refs_6_), channel_id=1, source_target_pairs={{0,16},{1,17},{2,18},{3,19},{4,20},{5,21},{6,22},{7,23},{8,11},{9,... | collective-permute-start | bytes 1400840 | tf_op jit(solution)/shard_map/ppermute | solution.py:56
  62.9 6.2 %collective-permute-start.5 = (bf16[152,768]{1,0:T(8,128)(2,1)S(1)}, bf16[152,768]{1,0:T(8,128)(2,1)S(1)}, u32[]{:S(2)}, u32[]{:S(2)}) collective-permute-start(bf16[152,768]{1,0:T(8,128)(2,1)S(1)} %collective-permute-done.4.refs_4_), channel_id=1, source_target_pairs={{0,4},{1,5},{2,6},{3,7},{4,0},{5,1},{6,2},{7,3},{8,9},{9,10},{10,1... | collective-permute-start | bytes 700424 | tf_op jit(solution)/shard_map/ppermute | solution.py:56
  64.9 6.5 %collective-permute-start.12 = (bf16[152,768]{1,0:T(8,128)(2,1)S(1)}, bf16[152,768]{1,0:T(8,128)(2,1)S(1)}, u32[]{:S(2)}, u32[]{:S(2)}) collective-permute-start(bf16[152,768]{1,0:T(8,128)(2,1)S(1)} %collective-permute-done.11.refs_5_), channel_id=1, source_target_pairs={{0,4},{1,5},{2,6},{3,7},{4,0},{5,1},{6,2},{7,3},{8,9},{9,10},{10,1... | collective-permute-start | bytes 700424 | tf_op jit(solution)/shard_map/ppermute | solution.py:56
  74.7 8.4 %collective-permute-start.25 = (bf16[288,768]{1,0:T(8,128)(2,1)S(1)}, bf16[288,768]{1,0:T(8,128)(2,1)S(1)}, u32[]{:S(2)}, u32[]{:S(2)}) collective-permute-start(bf16[288,768]{1,0:T(8,128)(2,1)S(1)} %get-tuple-element.71), channel_id=1, source_target_pairs={{0,16},{1,17},{2,18},{3,19},{4,20},{5,21},{6,22},{7,23},{8,9},{9,1... | collective-permute-start | bytes 1327112 | tf_op jit(solution)/shard_map/ppermute | solution.py:56
  74.8 12.6 %collective-permute-start.19 = (bf16[288,768]{1,0:T(8,128)(2,1)S(1)}, bf16[288,768]{1,0:T(8,128)(2,1)S(1)}, u32[]{:S(2)}, u32[]{:S(2)}) collective-permute-start(bf16[288,768]{1,0:T(8,128)(2,1)S(1)} %get-tuple-element.64), channel_id=1, source_target_pairs={{0,4},{1,5},{2,6},{3,7},{4,0},{5,1},{6,2},{7,3},{8,11},{9,8},{10,9... | collective-permute-start | bytes 1327112 | tf_op jit(solution)/shard_map/ppermute | solution.py:56
  79.2 10.4 %collective-permute-start.27 = (bf16[288,768]{1,0:T(8,128)(2,1)S(1)}, bf16[288,768]{1,0:T(8,128)(2,1)S(1)}, u32[]{:S(2)}, u32[]{:S(2)}) collective-permute-start(bf16[288,768]{1,0:T(8,128)(2,1)S(1)} %get-tuple-element.72), channel_id=1, source_target_pairs={{0,16},{1,17},{2,18},{3,19},{4,20},{5,21},{6,22},{7,23},{8,11},{9,... | collective-permute-start | bytes 1327112 | tf_op jit(solution)/shard_map/ppermute | solution.py:56
  83.2 8.4 %collective-permute-start.29 = (bf16[144,768]{1,0:T(8,128)(2,1)S(1)}, bf16[144,768]{1,0:T(8,128)(2,1)S(1)}, u32[]{:S(2)}, u32[]{:S(2)}) collective-permute-start(bf16[144,768]{1,0:T(8,128)(2,1)S(1)} %shard_map.81), channel_id=1, source_target_pairs={{0,4},{1,5},{2,6},{3,7},{4,0},{5,1},{6,2},{7,3},{8,9},{9,10},{10,1... | collective-permute-start | bytes 663560 | tf_op jit(solution)/shard_map/ppermute | solution.py:56
  85.3 10.7 %collective-permute-start.26 = (bf16[144,768]{1,0:T(8,128)(2,1)S(1)}, bf16[144,768]{1,0:T(8,128)(2,1)S(1)}, u32[]{:S(2)}, u32[]{:S(2)}) collective-permute-start(bf16[144,768]{1,0:T(8,128)(2,1)S(1)} %shard_map.79), channel_id=1, source_target_pairs={{0,4},{1,5},{2,6},{3,7},{4,0},{5,1},{6,2},{7,3},{8,9},{9,10},{10,1... | collective-permute-start | bytes 663560 | tf_op jit(solution)/shard_map/ppermute | solution.py:56
  85.4 13.0 %collective-permute-start.23 = (bf16[144,768]{1,0:T(8,128)(2,1)S(1)}, bf16[144,768]{1,0:T(8,128)(2,1)S(1)}, u32[]{:S(2)}, u32[]{:S(2)}) collective-permute-start(bf16[144,768]{1,0:T(8,128)(2,1)S(1)} %get-tuple-element.68), channel_id=1, source_target_pairs={{0,4},{1,5},{2,6},{3,7},{4,0},{5,1},{6,2},{7,3},{8,9},{9,10},{10,1... | collective-permute-start | bytes 663560 | tf_op jit(solution)/shard_map/ppermute | solution.py:56
  87.5 11.3 %collective-permute-start.22 = (bf16[144,768]{1,0:T(8,128)(2,1)S(1)}, bf16[144,768]{1,0:T(8,128)(2,1)S(1)}, u32[]{:S(2)}, u32[]{:S(2)}) collective-permute-start(bf16[144,768]{1,0:T(8,128)(2,1)S(1)} %shard_map.77), channel_id=1, source_target_pairs={{0,16},{1,17},{2,18},{3,19},{4,20},{5,21},{6,22},{7,23},{8,11},{9,... | collective-permute-start | bytes 663560 | tf_op jit(solution)/shard_map/ppermute | solution.py:56
  89.6 12.4 %collective-permute-start.21 = (bf16[144,768]{1,0:T(8,128)(2,1)S(1)}, bf16[144,768]{1,0:T(8,128)(2,1)S(1)}, u32[]{:S(2)}, u32[]{:S(2)}) collective-permute-start(bf16[144,768]{1,0:T(8,128)(2,1)S(1)} %get-tuple-element.65), channel_id=1, source_target_pairs={{0,4},{1,5},{2,6},{3,7},{4,0},{5,1},{6,2},{7,3},{8,9},{9,10},{10,1... | collective-permute-start | bytes 663560 | tf_op jit(solution)/shard_map/ppermute | solution.py:56
  91.5 10.5 %collective-permute-start.20 = (bf16[144,768]{1,0:T(8,128)(2,1)S(1)}, bf16[144,768]{1,0:T(8,128)(2,1)S(1)}, u32[]{:S(2)}, u32[]{:S(2)}) collective-permute-start(bf16[144,768]{1,0:T(8,128)(2,1)S(1)} %shard_map.76), channel_id=1, source_target_pairs={{0,16},{1,17},{2,18},{3,19},{4,20},{5,21},{6,22},{7,23},{8,11},{9,... | collective-permute-start | bytes 663560 | tf_op jit(solution)/shard_map/ppermute | solution.py:56
  96.1 7.4 %collective-permute-start.30 = (bf16[144,768]{1,0:T(8,128)(2,1)S(1)}, bf16[144,768]{1,0:T(8,128)(2,1)S(1)}, u32[]{:S(2)}, u32[]{:S(2)}) collective-permute-start(bf16[144,768]{1,0:T(8,128)(2,1)S(1)} %shard_map.82), channel_id=1, source_target_pairs={{0,2},{1,3},{2,0},{3,1},{4,6},{5,7},{6,4},{7,5},{8,28},{9,29},{10,... | collective-permute-start | bytes 663560 | tf_op jit(solution)/shard_map/ppermute | solution.py:56
  98.9 7.2 %collective-permute-start.24 = (bf16[144,768]{1,0:T(8,128)(2,1)S(1)}, bf16[144,768]{1,0:T(8,128)(2,1)S(1)}, u32[]{:S(2)}, u32[]{:S(2)}) collective-permute-start(bf16[144,768]{1,0:T(8,128)(2,1)S(1)} %shard_map.78), channel_id=1, source_target_pairs={{0,3},{1,0},{2,1},{3,2},{4,7},{5,4},{6,5},{7,6},{8,24},{9,25},{10,... | collective-permute-start | bytes 663560 | tf_op jit(solution)/shard_map/ppermute | solution.py:56
  106.5 8.4 %collective-permute-start.31 = (bf16[40,768]{1,0:T(8,128)(2,1)S(1)}, bf16[40,768]{1,0:T(8,128)(2,1)S(1)}, u32[]{:S(2)}, u32[]{:S(2)}) collective-permute-start(bf16[40,768]{1,0:T(8,128)(2,1)S(1)} %get-tuple-element.76), channel_id=1, source_target_pairs={{0,192},{64,0},{128,64},{192,128},{1,193},{65,1},{129,65},{193,129... | collective-permute-start | bytes 184328 | tf_op jit(solution)/shard_map/ppermute | solution.py:60
  111.6 8.9 %collective-permute-start.32 = (bf16[40,768]{1,0:T(8,128)(2,1)S(1)}, bf16[40,768]{1,0:T(8,128)(2,1)S(1)}, u32[]{:S(2)}, u32[]{:S(2)}) collective-permute-start(bf16[40,768]{1,0:T(8,128)(2,1)S(1)} %get-tuple-element.77), channel_id=1, source_target_pairs={{0,128},{64,192},{128,0},{192,64},{1,129},{65,193},{129,1},{193,65... | collective-permute-start | bytes 184328 | tf_op jit(solution)/shard_map/ppermute | solution.py:60
  113.0 7.5 %collective-permute-start.33 = (bf16[40,768]{1,0:T(8,128)(2,1)S(1)}, bf16[40,768]{1,0:T(8,128)(2,1)S(1)}, u32[]{:S(2)}, u32[]{:S(2)}) collective-permute-start(bf16[40,768]{1,0:T(8,128)(2,1)S(1)} %get-tuple-element.78), channel_id=1, source_target_pairs={{0,64},{64,128},{128,192},{192,0},{1,65},{65,129},{129,193},{193,1... | collective-permute-start | bytes 184328 | tf_op jit(solution)/shard_map/ppermute | solution.py:60
  (4 other events, 57.4 us)

commit v4 on v3

--- a/solution.py
+++ b/solution.py
@@ -18,6 +18,8 @@
 FAR = 4
 KEPT = FAR * CAP
 ROWS = 2 * KEPT
+NEAR = 56
+CROSSED = 24
 EXTRA = 8
 BLOCK = 40
 EPSILON = 1e-05
@@ -39,29 +41,39 @@
     return 1 - y, 1 - z, x
 
 
-def owner_pairs(step_core0, step_core1):
+def owner_pairs(*steps):
     pairs = []
     for y in range(2):
-        for core, step in enumerate((step_core0, step_core1)):
+        for z in range(2):
+            for x in range(4):
+                for group, step in enumerate(steps):
+                    ends = ((y, z, x), place(y, z, x, step))
+                    pairs.append(
+                        tuple(((j * 2 + (group ^ (j + k + n) & 1)) * 2 + k) * 4 + n for j, k, n in ends)
+                    )
+    return pairs
+
+
+def hop(value, step_core0, step_core1):
+    return lax.ppermute(value, OWNER, owner_pairs(step_core0, step_core1))
+
+
+def along_z(value, distance):
+    pairs = []
+    for h in range(FAR):
+        for c in range(2):
             for z in range(2):
                 for x in range(4):
-                    y_to, z_to, x_to = place(y, z, x, step)
-                    source = ((y * 2 + core) * 2 + z) * 4 + x
-                    target = ((y_to * 2 + core) * 2 + z_to) * 4 + x_to
-                    pairs.append((source, target))
-    return pairs
-
-
-def hop(value, step_core0, step_core1):
-    return lax.ppermute(value, OWNER, owner_pairs(step_core0, step_core1))
-
-
-def along_z(value, distance):
-    return lax.ppermute(value, "zh", [(i, (i + distance) % FAR) for i in range(FAR)])
+                    target = (h + distance) % FAR, c ^ (z + x) & 1
+                    pairs.append(
+                        tuple(((i * 2 + j) * 2 + z) * 4 + x for i, j in ((h, c), target))
+                    )
+    return lax.ppermute(value, ("zh", "c", "zl", "x"), pairs)
 
 
 def across_y(value):
-    return lax.ppermute(value, ("y2", "y1"), [(i, 3 - i) for i in range(4)])
+    pairs = [(i * 2 + c, (3 - i) * 2 + 1 - c) for i in range(4) for c in range(2)]
+    return lax.ppermute(value, ("y2", "y1", "c"), pairs)
 
 
 def other_core(value):
@@ -99,13 +111,26 @@
     return jnp.dot(picks, joined, preferred_element_type=F32)
 
 
-def slots_of(ids):
+def leaving(row):
+    part = jnp.where(row >= NEAR, 1, 0) + jnp.where(row >= 2 * NEAR, 1, 0)
+    row = row - part * NEAR
+    k = (row * 3641) >> 16
+    half = jnp.where(part == 2, k, part)
+    distance = jnp.where(part == 2, 2, jnp.where(k == 2, 3, k))
+    return half, distance, row - k * CAP, k < jnp.where(part == 2, 2, 3)
+
+
+def returning(row):
+    k = (row * 3641) >> 16
+    return k >> 2, k & 3, row - k * CAP, row >= 0
+
+
+def slots_of(ids, order, rows):
     tokens = ids.shape[1]
-    slot = lax.broadcasted_iota(jnp.int32, (ROWS, tokens), 0)
-    k = (slot * 3641) >> 16
-    inside = slot - k * CAP
+    slot = lax.broadcasted_iota(jnp.int32, (rows, tokens), 0)
+    half, distance, inside, valid = order(slot)
     zh, y2 = lax.axis_index("zh"), lax.axis_index("y2")
-    expert = ((zh + k) & 3) * 2 + (y2 ^ (k >> 2))
+    expert = ((zh + distance) & 3) * 2 + (y2 ^ half)
     first, second = ids[0:1, :] == expert, ids[1:2, :] == expert
     routed = jnp.where(first | second, 1.0, 0.0).astype(BF16)
     earlier = lax.broadcasted_iota(jnp.int32, (tokens, tokens), 0) < lax.broadcasted_iota(
@@ -114,31 +139,32 @@
     before = jnp.dot(
         routed, jnp.where(earlier, 1.0, 0.0).astype(BF16), preferred_element_type=F32
     )
-    here = before == inside.astype(F32)
+    here = (before == inside.astype(F32)) & valid
     return first & here, second & here
 
 
-def select_kernel(ids_hbm, tokens_hbm, keep_ref, send_ref, ids_ref, tokens_ref, sems):
+def select_kernel(ids_hbm, tokens_hbm, keep_ref, send_ref, far_ref, ids_ref, tokens_ref, sems):
     fetch = pltpu.make_async_copy(ids_hbm, ids_ref, sems.at[0])
     fetch_tokens = pltpu.make_async_copy(tokens_hbm, tokens_ref, sems.at[1])
     fetch.start()
     fetch_tokens.start()
     fetch.wait()
-    first, second = slots_of(ids_ref[...])
+    first, second = slots_of(ids_ref[...], leaving, 2 * NEAR + BLOCK)
     picks = jnp.where(first | second, 1.0, 0.0).astype(BF16)
     fetch_tokens.wait()
     chosen = jnp.dot(picks, tokens_ref[...], preferred_element_type=F32).astype(BF16)
-    keep_ref[...] = chosen[:KEPT]
-    send_ref[...] = chosen[KEPT:]
+    keep_ref[...] = chosen[:NEAR]
+    send_ref[...] = chosen[NEAR : 2 * NEAR]
+    far_ref[...] = chosen[2 * NEAR :]
 
 
 def select(ids, tokens):
-    kept = jax.ShapeDtypeStruct((KEPT, tokens.shape[1]), BF16)
+    sizes = (NEAR, NEAR, BLOCK)
     return pl.pallas_call(
         select_kernel,
-        out_shape=[kept, kept],
+        out_shape=[jax.ShapeDtypeStruct((n, tokens.shape[1]), BF16) for n in sizes],
         in_specs=hbm(2),
-        out_specs=vmem(2),
+        out_specs=vmem(3),
         scratch_shapes=[
             pltpu.VMEM(ids.shape, ids.dtype),
             pltpu.VMEM(tokens.shape, BF16),
@@ -156,25 +182,38 @@
     return block, inside, half
 
 
-def shuffle_kernel(keep_ref, came_ref, *out_refs):
+def shuffle_kernel(keep_ref, came_ref, sums_ref, stay_ref, *out_refs):
     def source_of(row):
         block, inside, half = in_blocks(row)
-        return half * KEPT + block * CAP + inside - half * CAP, inside < 2 * CAP
-
-    rows = moved((FAR * BLOCK, 0), source_of, keep_ref, came_ref)
-    for k, out in enumerate(out_refs):
+        return half * NEAR + block * CAP + inside - half * CAP, inside < 2 * CAP
+
+    rows = moved((3 * BLOCK, 0), source_of, keep_ref, came_ref)
+    stay_ref[:BLOCK] = rows[:BLOCK].astype(BF16)
+    stay_ref[BLOCK:] = sums_ref[...]
+    for k, out in enumerate(out_refs, 1):
         out[...] = rows[k * BLOCK : (k + 1) * BLOCK].astype(BF16)
 
 
-def pack_kernel(*refs):
-    *blocks, sums_ref, out_ref = refs
+def cross_kernel(far_ref, out_ref):
+    def source_of(row):
+        return row + CAP, row < CAP
+
+    out_ref[...] = moved((CROSSED, 0), source_of, far_ref).astype(BF16)
+
+
+def pack_kernel(stay_ref, one_ref, two_ref, three_ref, crossed_ref, out_ref):
+    start = BLOCK + EXTRA
 
     def source_of(row):
         block = (row * 1821) >> 16
-        return block * BLOCK + row - block * 2 * CAP, row >= 0
-
-    out_ref[:ROWS] = moved((ROWS, 0), source_of, *blocks).astype(BF16)
-    out_ref[ROWS:] = sums_ref[...]
+        inside = row - block * 2 * CAP
+        source = jnp.where(block == 0, 0, start + (block - 1) * BLOCK) + inside
+        crossed = (block == 2) & (inside >= CAP)
+        return jnp.where(crossed, start + 3 * BLOCK + inside - CAP, source), row >= 0
+
+    refs = (stay_ref, one_ref, two_ref, three_ref, crossed_ref)
+    out_ref[:ROWS] = moved((ROWS, 0), source_of, *refs).astype(BF16)
+    out_ref[ROWS:] = stay_ref[BLOCK:]
 
 
 def pair_kernel(first_ref, second_ref, out_ref):
@@ -233,21 +272,13 @@
     return high, (value - high.astype(F32)).astype(BF16)
 
 
-def stats_kernel(tokens_hbm, gain_hbm, router_hbm, *refs):
-    weights, out_ref, gain_ref, weight_refs = refs[:3], refs[3], refs[4], refs[5:8]
-    tokens_ref, router_ref, sems, weight_sems = refs[8:]
+def stats_kernel(tokens_hbm, gain_hbm, router_hbm, out_ref, gain_ref, tokens_ref, router_ref, sems):
     tokens, width = tokens_ref.shape
     part = lax.axis_index("zl") * 4 + lax.axis_index("x")
     here = pl.ds(pl.multiple_of(part * width, width), width)
     ways = ((tokens_hbm, tokens_ref), (gain_hbm, gain_ref), (router_hbm.at[:, here], router_ref))
     fetches = [pltpu.make_async_copy(a, b, sems.at[n]) for n, (a, b) in enumerate(ways)]
     for fetch in fetches:
-        fetch.start()
-    later = [
-        pltpu.make_async_copy(a, b, weight_sems.at[n])
-        for n, (a, b) in enumerate(zip(weights, weight_refs))
-    ]
-    for fetch in later:
         fetch.start()
     out_ref[...] = jnp.zeros_like(out_ref)
     for fetch in fetches:
@@ -260,30 +291,50 @@
         for k, v in enumerate(halves(sum(transposed_dot(left, t) for t in terms))):
             start = (2 * n + k) * 128
             out_ref[:, start : start + tokens] = v
-    for fetch in later:
-        fetch.wait()
-
-
-def stats(tokens, gain, router, *weights):
+
+
+def stats(tokens, gain, router):
     width = tokens.shape[1]
     return pl.pallas_call(
         stats_kernel,
         out_shape=[
             jax.ShapeDtypeStruct((EXTRA, width), BF16),
             jax.ShapeDtypeStruct(gain.shape, F32),
-            *(jax.ShapeDtypeStruct(w.shape, BF16) for w in weights),
         ],
-        in_specs=hbm(6),
-        out_specs=vmem(5),
+        in_specs=hbm(3),
+        out_specs=vmem(2),
         scratch_shapes=[
             pltpu.VMEM(tokens.shape, BF16),
             pltpu.VMEM((router.shape[0], width), BF16),
             pltpu.SemaphoreType.DMA((3,)),
-            pltpu.SemaphoreType.DMA((3,)),
         ],
         compiler_params=pltpu.CompilerParams(vmem_limit_bytes=4 << 20),
         name="stats",
-    )(*in_hbm(tokens, gain, router, *weights))
+    )(*in_hbm(tokens, gain, router))
+
+
+def fetch_kernel(*refs):
+    count = len(refs) // 2
+    sems = refs[-1]
+    copies = [
+        pltpu.make_async_copy(refs[n], refs[count + n], sems.at[n]) for n in range(count)
+    ]
+    for copy in copies:
+        copy.start()
+    for copy in copies:
+        copy.wait()
+
+
+def fetched(*arrays):
+    return pl.pallas_call(
+        fetch_kernel,
+        out_shape=[jax.ShapeDtypeStruct(a.shape, a.dtype) for a in arrays],
+        in_specs=hbm(len(arrays)),
+        out_specs=vmem(len(arrays)),
+        scratch_shapes=[pltpu.SemaphoreType.DMA((len(arrays),))],
+        compiler_params=pltpu.CompilerParams(vmem_limit_bytes=4 << 20),
+        name="fetch",
+    )(*in_hbm(*arrays))
 
 
 def stats_in(tile, tokens):
@@ -304,7 +355,7 @@
     ]
     gate_first = 1.0 / (1.0 + jnp.exp(logits[1] - logits[0]))
     gate_second = 1.0 / (1.0 + jnp.exp(logits[0] - logits[1]))
-    first, second = slots_of(ids)
+    first, second = slots_of(ids, returning, ROWS)
     weights = jnp.where(first, gate_first, 0.0) + jnp.where(second, gate_second, 0.0)
     rows = jnp.concatenate([keep_ref[...], came_ref[...]], axis=0)
     out_ref[...] = sum(
@@ -319,9 +370,14 @@
     return square & 1, feature
 
 
+def group_index():
+    place_sum = lax.axis_index("y1") + lax.axis_index("zl") + lax.axis_index("x")
+    return lax.axis_index("c") ^ (place_sum & 1)
+
+
 def tile_place(outer, inner):
-    core = lax.axis_index("c")
-    return offset_place(jnp.where(core == 0, outer, inner), jnp.where(core == 0, inner, outer))
+    group = group_index()
+    return offset_place(jnp.where(group == 0, outer, inner), jnp.where(group == 0, inner, outer))
 
 
 CHUNK = 48
@@ -382,15 +438,18 @@
 
 
 def early_kernel(where, gain_ref, *refs):
-    tiles, weights = viewed(refs, where), refs[-11:-7]
-    acc_ref, x_ref, squares_ref, sums_ref = refs[-4:]
+    tiles, weights, later = viewed(refs, where), refs[-14:-10], refs[-10]
+    later_ref, acc_ref, x_ref, squares_ref, sums_ref, sem = refs[-6:]
+    fetch = pltpu.make_async_copy(later, later_ref, sem.at[0])
+    fetch.start()
     for key, tile in zip(SECOND, tiles):
         place_tile(key, tile, gain_ref, x_ref, squares_ref, sums_ref)
     for n, weight in enumerate(weights):
         acc_ref[n] = jnp.dot(x_ref[...], weight[...], preferred_element_type=F32)
-
-
-def early_of(gain, tiles, weights, sums_shape):
+    fetch.wait()
+
+
+def early_of(gain, tiles, weights, later, sums_shape):
     width_all, slices = weights[0].shape
     given = [
         jax.ShapeDtypeStruct((2 * ROWS, width_all), BF16),
@@ -407,13 +466,18 @@
         name="fill",
     )(gain, *arrays)
     arrays, where = views(tiles, SECOND)
-    at = 1 + len(arrays) + 4
-    acc, _, squares, sums = pl.pallas_call(
+    at = 1 + len(arrays) + 5
+    later_out, acc, _, squares, sums = pl.pallas_call(
         partial(early_kernel, where),
-        out_shape=[jax.ShapeDtypeStruct((4, 2 * ROWS, slices), F32), *given],
-        in_specs=vmem(at + 3),
-        out_specs=vmem(4),
-        input_output_aliases={at + n: 1 + n for n in range(3)},
+        out_shape=[
+            jax.ShapeDtypeStruct(later.shape, later.dtype),
+            jax.ShapeDtypeStruct((4, 2 * ROWS, slices), F32),
+            *given,
+        ],
+        in_specs=vmem(at - 1) + hbm(1) + vmem(3),
+        out_specs=vmem(5),
+        input_output_aliases={at + n: 2 + n for n in range(3)},
+        scratch_shapes=[pltpu.SemaphoreType.DMA((1,))],
         compiler_params=pltpu.CompilerParams(vmem_limit_bytes=12 << 20),
         cost_estimate=pl.CostEstimate(
             flops=2 * 2 * ROWS * width_all * 4 * slices,
@@ -421,8 +485,8 @@
             transcendentals=0,
         ),
         name="early",
-    )(gain, *arrays, *weights, *filled)
-    return acc, squares, sums
+    )(gain, *arrays, *weights, *in_hbm(later), *filled)
+    return acc, squares, sums, later_out
 
 
 def late_kernel(width_all, where, gain_ref, *refs):
@@ -486,7 +550,7 @@
     out_refs, y_ref = refs[:-1], refs[-1]
     slices = own_ref.shape[0]
     width = y_ref.shape[2]
-    core = lax.axis_index("c")
+    group = group_index()
 
     def product(rows, square, ring):
         _, feature = offset_place(square, ring)
@@ -498,7 +562,7 @@
 
     both, first, last = slice(None), slice(0, ROWS), slice(ROWS, 2 * ROWS)
 
-    @pl.when(core == 0)
+    @pl.when(group == 0)
     def _():
         def step(ring, _):
             if far:
@@ -512,7 +576,7 @@
 
         lax.fori_loop(0, 4, step, 0)
 
-    @pl.when(core == 1)
+    @pl.when(group == 1)
     def _():
         def step(n, _):
             ring, square = (3, 2 * n) if far else (n >> 1, 2 * (n & 1))
@@ -570,17 +634,22 @@
     ids = expert_ids.T
     kept, block = (KEPT, width), (BLOCK, width)
 
-    keep, send = select(ids, tokens)
+    keep, send, far = select(ids, tokens)
+    part_sums, gain = stats(tokens, gain, router_weight.T)
     came = across_y(send)
-    blocks = small(shuffle_kernel, [block] * FAR, keep, came)
-    arrived = [blocks[0]] + [along_z(blocks[k], k) for k in (1, 2, 3)]
+    far = along_z(far, 2)
+    stay, *blocks = small(
+        shuffle_kernel, [(BLOCK + EXTRA, width), block, block], keep, came, part_sums
+    )
+    one, three = along_z(blocks[0], 1), along_z(blocks[1], 3)
+    stay = along_z(stay, 0)
+    (crossed,) = small(cross_kernel, [(CROSSED, width)], far)
+    crossed = across_y(crossed)
     gate_other = other_core(gate_proj)
     up_other = other_core(up_proj)
     down_other = other_core(down_proj)
-    part_sums, gain, gate_own, up_own, down_own = stats(
-        tokens, gain, router_weight.T, gate_proj, up_proj, down_proj
-    )
-    (mine,) = small(pack_kernel, [(ROWS + EXTRA, width)], *arrived, part_sums)
+    (mine,) = small(pack_kernel, [(ROWS + EXTRA, width)], stay, one, far, three, crossed)
+    gate_own, up_own = fetched(gate_proj, up_proj)
 
     one = hop(mine, "x+", "y")
     two = hop(mine, "x-", "z")
@@ -598,8 +667,9 @@
 
     sums_shape = (2 * router_weight.shape[1], tokens.shape[0])
     weights = (gate_other, up_other, gate_own, up_own)
-    acc, squares, sums = early_of(gain, tiles, weights, sums_shape)
+    acc, squares, sums, down_own = early_of(gain, tiles, weights, down_proj, sums_shape)
     hidden, sums = late_of(gain, tiles, weights, acc, squares, sums)
+    sums = along_z(sums, 0)
 
     places = [(0, 0), (0, ROWS), (1, 0), (1, ROWS)]
     far = down_of(True, [2 * ROWS] * 2, places, hidden, down_own, down_other)
@@ -628,7 +698,7 @@
         hop(added(*parts[3]), "xx", "yz"),
     ]
     blocks = small(unpack_kernel, [block] * FAR, *terms)
-    back = [blocks[0]] + [along_z(blocks[k], FAR - k) for k in (1, 2, 3)]
+    back = [along_z(blocks[k], (FAR - k) % FAR) for k in range(FAR)]
     keep, send = small(unshuffle_kernel, [kept, kept], *back)
     came = across_y(send)
     return pl.pallas_call(

time: 128 us -> 132 us (1.031)
  the two profiles are of different devices: /device:TPU:6 before, /device:TPU:33 now
where the time goes in v4:
time: 132 us
  starting transfers between devices  63.5 us (48%)
  waiting for transfers between devices  49.5 us (38%)
  Pallas kernels  18.5 us (14%)
    ppermute x24, waiting for transfers between devices, hop(): return lax.ppermute(value, OWNER, owner_pairs(step_core0, step_core1))  35.3 us
    ppermute x9, starting transfers between devices, along_z(): return lax.ppermute(value, ('zh', 'c', 'zl', 'x'), pairs)  32.7 us
    ppermute x24, starting transfers between devices, hop(): return lax.ppermute(value, OWNER, owner_pairs(step_core0, step_core1))  25.8 us
    ppermute x3, waiting for transfers between devices, across_y(): return lax.ppermute(value, ('y2', 'y1', 'c'), pairs)  7.26 us
    ppermute x9, waiting for transfers between devices, along_z(): return lax.ppermute(value, ('zh', 'c', 'zl', 'x'), pairs)  6.94 us
    pallas_call x1, Pallas kernels, early_of(): pl.pallas_call(partial(early_kernel, where), out_shape=[jax.ShapeDtypeStr...  4.18 us
    ppermute x3, starting transfers between devices, across_y(): return lax.ppermute(value, ('y2', 'y1', 'c'), pairs)  3.73 us
    pallas_call x2, Pallas kernels, down_of(): pl.pallas_call(partial(down_kernel, far, places), out_shape=[jax.ShapeDty...  3.58 us
  transfers between devices with their start and end apart: 39, of which 19 were waited for; matrix products, arithmetic and copies ran while one was open for 0% of the time, Pallas kernels for 12%

profile of v4, /device:TPU:33, one launch (start us, length us, event | category | flops | bytes accessed | tf_op | source)
XLA Modules:
  0.0 131.7 jit_solution(10150395325043665036)
XLA Ops:
  2.3 2.7 %collective-permute-start = (bf16[56,768]{1,0:T(8,128)(2,1)S(1)}, bf16[56,768]{1,0:T(8,128)(2,1)S(1)}, u32[]{:S(2)}, u32[]{:S(2)}) collective-permute-start(bf16[56,768]{1,0:T(8,128)(2,1)S(1)} %get-tuple-element.45), channel_id=1, source_target_pairs={{0,56},{8,48},{16,40},{24,32},{32,24},{40,16},{48,8},{56,0},{1,57}... | collective-permute-start | bytes 258056 | tf_op jit(solution)/shard_map/ppermute | solution.py:76
  5.0 6.4 %collective-permute-start.3 = (bf16[40,768]{1,0:T(8,128)(2,1)S(1)}, bf16[40,768]{1,0:T(8,128)(2,1)S(1)}, u32[]{:S(2)}, u32[]{:S(2)}) collective-permute-start(bf16[40,768]{1,0:T(8,128)(2,1)S(1)} %get-tuple-element.49), channel_id=1, source_target_pairs={{0,128},{1,137},{2,130},{3,139},{4,140},{5,133},{6,142},{7,135},{8... | collective-permute-start | bytes 184328 | tf_op jit(solution)/shard_map/ppermute | solution.py:71
  15.1 4.1 %collective-permute-done.5.crossed_ref = bf16[24,768]{1,0:T(8,128)(2,1)S(1)} collective-permute-done((bf16[24,768]{1,0:T(8,128)(2,1)S(1)}, bf16[24,768]{1,0:T(8,128)(2,1)S(1)}, u32[]{:S(2)}, u32[]{:S(2)}) %collective-permute-start.5) | collective-permute-done | bytes 36896 | tf_op jit(solution)/shard_map/ppermute | solution.py:76
  19.2 2.6 %collective-permute-start.1 = (bf16[48,768]{1,0:T(8,128)(2,1)S(1)}, bf16[48,768]{1,0:T(8,128)(2,1)S(1)}, u32[]{:S(2)}, u32[]{:S(2)}) collective-permute-start(bf16[48,768]{1,0:T(8,128)(2,1)S(1)} %get-tuple-element.47), channel_id=1, source_target_pairs={{0,0},{1,9},{2,2},{3,11},{4,12},{5,5},{6,14},{7,7},{8,8},{9,1},{10... | collective-permute-start | bytes 221192 | tf_op jit(solution)/shard_map/ppermute | solution.py:71
  21.8 4.0 %collective-permute-start.4 = (bf16[40,768]{1,0:T(8,128)(2,1)S(1)}, bf16[40,768]{1,0:T(8,128)(2,1)S(1)}, u32[]{:S(2)}, u32[]{:S(2)}) collective-permute-start(bf16[40,768]{1,0:T(8,128)(2,1)S(1)} %get-tuple-element.50), channel_id=1, source_target_pairs={{0,192},{1,201},{2,194},{3,203},{4,204},{5,197},{6,206},{7,199},{8... | collective-permute-start | bytes 184328 | tf_op jit(solution)/shard_map/ppermute | solution.py:71
  28.0 2.4 %collective-permute-start.9 = (bf16[152,768]{1,0:T(8,128)(2,1)S(1)}, bf16[152,768]{1,0:T(8,128)(2,1)S(1)}, u32[]{:S(2)}, u32[]{:S(2)}) collective-permute-start(bf16[152,768]{1,0:T(8,128)(2,1)S(1)} %shard_map.75.refs_0_), channel_id=1, source_target_pairs={{0,11},{8,4},{9,0},{1,13},{2,9},{10,6},{11,2},{3,15},{12,7},{4,8},... | collective-permute-start | bytes 700424 | tf_op jit(solution)/shard_map/ppermute | solution.py:58
  30.4 3.7 %collective-permute-done.8.first_ref.refs_1_ = bf16[152,768]{1,0:T(8,128)(2,1)S(1)} collective-permute-done((bf16[152,768]{1,0:T(8,128)(2,1)S(1)}, bf16[152,768]{1,0:T(8,128)(2,1)S(1)}, u32[]{:S(2)}, u32[]{:S(2)}) %collective-permute-start.8) | collective-permute-done | bytes 233504 | tf_op jit(solution)/shard_map/ppermute | solution.py:58
  34.1 1.8 %collective-permute-start.12 = (bf16[152,768]{1,0:T(8,128)(2,1)S(1)}, bf16[152,768]{1,0:T(8,128)(2,1)S(1)}, u32[]{:S(2)}, u32[]{:S(2)}) collective-permute-start(bf16[152,768]{1,0:T(8,128)(2,1)S(1)} %shard_map.75.refs_0_), channel_id=1, source_target_pairs={{0,2},{8,28},{9,11},{1,21},{2,0},{10,30},{11,9},{3,23},{12,14},{4,... | collective-permute-start | bytes 700424 | tf_op jit(solution)/shard_map/ppermute | solution.py:58
  35.9 5.2 %collective-permute-done.12.refs_3_ = bf16[152,768]{1,0:T(8,128)(2,1)S(1)} collective-permute-done((bf16[152,768]{1,0:T(8,128)(2,1)S(1)}, bf16[152,768]{1,0:T(8,128)(2,1)S(1)}, u32[]{:S(2)}, u32[]{:S(2)}) %collective-permute-start.12) | collective-permute-done | bytes 233504 | tf_op jit(solution)/shard_map/ppermute | solution.py:58
  41.2 4.3 %collective-permute-start.18 = (bf16[152,768]{1,0:T(8,128)(2,1)S(1)}, bf16[152,768]{1,0:T(8,128)(2,1)S(1)}, u32[]{:S(2)}, u32[]{:S(2)}) collective-permute-start(bf16[152,768]{1,0:T(8,128)(2,1)S(1)} %shard_map.75.refs_0_), channel_id=1, source_target_pairs={{0,12},{8,3},{9,5},{1,8},{2,14},{10,1},{11,7},{3,10},{12,0},{4,15}... | collective-permute-start | bytes 700424 | tf_op jit(solution)/shard_map/ppermute | solution.py:58
  45.5 4.0 %collective-permute-done.18.refs_1_ = bf16[152,768]{1,0:T(8,128)(2,1)S(1)} collective-permute-done((bf16[152,768]{1,0:T(8,128)(2,1)S(1)}, bf16[152,768]{1,0:T(8,128)(2,1)S(1)}, u32[]{:S(2)}, u32[]{:S(2)}) %collective-permute-start.18) | collective-permute-done | bytes 233504 | tf_op jit(solution)/shard_map/ppermute | solution.py:58
  51.4 3.9 %collective-permute-done.19.refs_2_ = bf16[152,768]{1,0:T(8,128)(2,1)S(1)} collective-permute-done((bf16[152,768]{1,0:T(8,128)(2,1)S(1)}, bf16[152,768]{1,0:T(8,128)(2,1)S(1)}, u32[]{:S(2)}, u32[]{:S(2)}) %collective-permute-start.19) | collective-permute-done | bytes 233504 | tf_op jit(solution)/shard_map/ppermute | solution.py:58
  55.3 5.0 %collective-permute-done.10.refs_6_ = bf16[2,152,768]{2,1,0:T(8,128)(2,1)S(1)} collective-permute-done((bf16[2,152,768]{2,1,0:T(8,128)(2,1)S(1)}, bf16[2,152,768]{2,1,0:T(8,128)(2,1)S(1)}, u32[]{:S(2)}, u32[]{:S(2)}) %collective-permute-start.10) | collective-permute-done | bytes 466976 | tf_op jit(solution)/shard_map/ppermute | solution.py:58
  60.3 2.9 %fetch.1 = (bf16[6144,256]{1,0:T(8,128)(2,1)S(1)}, bf16[6144,256]{1,0:T(8,128)(2,1)S(1)}) custom-call(bf16[6144,256]{1,0:T(8,128)(2,1)} %refs_0_.1, bf16[6144,256]{1,0:T(8,128)(2,1)} %refs_1_.1), custom_call_target="tpu_custom_call" | custom-call | tf_op jit(solution)/shard_map/fetch/pallas_call | solution.py:329
  65.8 4.2 %early.1 = (bf16[256,6144]{1,0:T(8,128)(2,1)S(1)}, f32[4,288,256]{2,1,0:T(8,128)S(1)}, bf16[288,6144]{1,0:T(8,128)(2,1)S(1)}, f32[288,128]{1,0:T(8,128)S(1)}, f32[16,64]{1,0:T(8,128)S(1)}) custom-call(f32[1,6144]{1,0:T(1,128)S(1)} %get-tuple-element.43.gain_ref, ...), custom_call_target="tpu_custom_call", output_to_operand_aliasing={{2}: (9, {}), {3}: (10, {}), {4}: (11, {})} | custom-call | flops 3623878656 | bytes 12582912 | tf_op jit(solution)/shard_map/early/pallas_call | solution.py:470
  70.0 2.3 %collective-permute-done.14.refs_2_ = bf16[152,768]{1,0:T(8,128)(2,1)S(1)} collective-permute-done((bf16[152,768]{1,0:T(8,128)(2,1)S(1)}, bf16[152,768]{1,0:T(8,128)(2,1)S(1)}, u32[]{:S(2)}, u32[]{:S(2)}) %collective-permute-start.14) | collective-permute-done | bytes 233504 | tf_op jit(solution)/shard_map/ppermute | solution.py:58
  72.4 2.0 %late.1 = (bf16[288,512]{1,0:T(8,128)(2,1)S(1)}, f32[16,64]{1,0:T(8,128)S(1)}, f32[4,288,256]{2,1,0:T(8,128)S(1)}) custom-call(f32[1,6144]{1,0:T(1,128)S(1)} %get-tuple-element.43.gain_ref, bf16[152,768]{1,0:T(8,128)(2,1)S(1)} %collective-permute-done.7.refs_0_, ...), custom_call_target="tpu_custom_call", output_to_operand_aliasing={{2}: (8, {})} | custom-call | flops 905969664 | bytes 2359296 | tf_op jit(solution)/shard_map/late/pallas_call | solution.py:525
  75.6 1.5 %collective-permute-start.28 = (bf16[288,768]{1,0:T(8,128)(2,1)S(1)}, bf16[288,768]{1,0:T(8,128)(2,1)S(1)}, u32[]{:S(2)}, u32[]{:S(2)}) collective-permute-start(bf16[288,768]{1,0:T(8,128)(2,1)S(1)} %get-tuple-element.71), channel_id=1, source_target_pairs={{0,24},{8,1},{9,17},{1,10},{2,26},{10,3},{11,19},{3,8},{12,20},{4,... | collective-permute-start | bytes 1327112 | tf_op jit(solution)/shard_map/ppermute | solution.py:58
  78.6 2.3 %rest.1 = (bf16[144,768]{1,0:T(8,128)(2,1)S(1)}, bf16[144,768]{1,0:T(8,128)(2,1)S(1)}, bf16[144,768]{1,0:T(8,128)(2,1)S(1)}, bf16[144,768]{1,0:T(8,128)(2,1)S(1)...) custom-call(bf16[288,512]{1,0:T(8,128)(2,1)S(1)} %get-tuple-element., ...), custom_call_target="tpu_custom_call" | custom-call | flops 1358954496 | bytes 6291456 | tf_op jit(solution)/shard_map/rest/pallas_call | solution.py:598
  81.1 2.6 %collective-permute-done.28.refs_1_ = bf16[288,768]{1,0:T(8,128)(2,1)S(1)} collective-permute-done((bf16[288,768]{1,0:T(8,128)(2,1)S(1)}, bf16[288,768]{1,0:T(8,128)(2,1)S(1)}, u32[]{:S(2)}, u32[]{:S(2)}) %collective-permute-start.28) | collective-permute-done | bytes 442400 | tf_op jit(solution)/shard_map/ppermute | solution.py:58
  86.7 2.1 %collective-permute-start.25 = (bf16[144,768]{1,0:T(8,128)(2,1)S(1)}, bf16[144,768]{1,0:T(8,128)(2,1)S(1)}, u32[]{:S(2)}, u32[]{:S(2)}) collective-permute-start(bf16[144,768]{1,0:T(8,128)(2,1)S(1)} %shard_map.78), channel_id=1, source_target_pairs={{0,24},{8,3},{9,17},{1,8},{2,26},{10,1},{11,19},{3,10},{12,20},{4,... | collective-permute-start | bytes 663560 | tf_op jit(solution)/shard_map/ppermute | solution.py:58
  89.5 1.8 %collective-permute-start.23 = (bf16[144,768]{1,0:T(8,128)(2,1)S(1)}, bf16[144,768]{1,0:T(8,128)(2,1)S(1)}, u32[]{:S(2)}, u32[]{:S(2)}) collective-permute-start(bf16[144,768]{1,0:T(8,128)(2,1)S(1)} %shard_map.77), channel_id=1, source_target_pairs={{0,24},{8,3},{9,17},{1,8},{2,26},{10,1},{11,19},{3,10},{12,20},{4,... | collective-permute-start | bytes 663560 | tf_op jit(solution)/shard_map/ppermute | solution.py:58
  92.1 2.2 %collective-permute-done.26.refs_2_ = bf16[144,768]{1,0:T(8,128)(2,1)S(1)} collective-permute-done((bf16[144,768]{1,0:T(8,128)(2,1)S(1)}, bf16[144,768]{1,0:T(8,128)(2,1)S(1)}, u32[]{:S(2)}, u32[]{:S(2)}) %collective-permute-start.26) | collective-permute-done | bytes 221216 | tf_op jit(solution)/shard_map/ppermute | solution.py:58
  94.4 3.0 %collective-permute-start.27 = (bf16[144,768]{1,0:T(8,128)(2,1)S(1)}, bf16[144,768]{1,0:T(8,128)(2,1)S(1)}, u32[]{:S(2)}, u32[]{:S(2)}) collective-permute-start(bf16[144,768]{1,0:T(8,128)(2,1)S(1)} %shard_map.79), channel_id=1, source_target_pairs={{0,11},{8,16},{9,0},{1,25},{2,9},{10,18},{11,2},{3,27},{12,7},{4,2... | collective-permute-start | bytes 663560 | tf_op jit(solution)/shard_map/ppermute | solution.py:58
  97.4 2.4 %collective-permute-done.33.refs_5_ = bf16[144,768]{1,0:T(8,128)(2,1)S(1)} collective-permute-done((bf16[144,768]{1,0:T(8,128)(2,1)S(1)}, bf16[144,768]{1,0:T(8,128)(2,1)S(1)}, u32[]{:S(2)}, u32[]{:S(2)}) %collective-permute-start.33) | collective-permute-done | bytes 221216 | tf_op jit(solution)/shard_map/ppermute | solution.py:58
  99.8 2.7 %collective-permute-done.31.refs_4_ = bf16[144,768]{1,0:T(8,128)(2,1)S(1)} collective-permute-done((bf16[144,768]{1,0:T(8,128)(2,1)S(1)}, bf16[144,768]{1,0:T(8,128)(2,1)S(1)}, u32[]{:S(2)}, u32[]{:S(2)}) %collective-permute-start.31) | collective-permute-done | bytes 221216 | tf_op jit(solution)/shard_map/ppermute | solution.py:58
  102.9 9.1 %collective-permute-start.34 = (bf16[40,768]{1,0:T(8,128)(2,1)S(1)}, bf16[40,768]{1,0:T(8,128)(2,1)S(1)}, u32[]{:S(2)}, u32[]{:S(2)}) collective-permute-start(bf16[40,768]{1,0:T(8,128)(2,1)S(1)} %get-tuple-element.75), channel_id=1, source_target_pairs={{0,0},{1,9},{2,2},{3,11},{4,12},{5,5},{6,14},{7,7},{8,8},{9,1},{10... | collective-permute-start | bytes 184328 | tf_op jit(solution)/shard_map/ppermute | solution.py:71
  112.1 3.9 %collective-permute-start.35 = (bf16[40,768]{1,0:T(8,128)(2,1)S(1)}, bf16[40,768]{1,0:T(8,128)(2,1)S(1)}, u32[]{:S(2)}, u32[]{:S(2)}) collective-permute-start(bf16[40,768]{1,0:T(8,128)(2,1)S(1)} %get-tuple-element.76), channel_id=1, source_target_pairs={{0,192},{1,201},{2,194},{3,203},{4,204},{5,197},{6,206},{7,199},{8... | collective-permute-start | bytes 184328 | tf_op jit(solution)/shard_map/ppermute | solution.py:71
  115.9 1.9 %collective-permute-start.36 = (bf16[40,768]{1,0:T(8,128)(2,1)S(1)}, bf16[40,768]{1,0:T(8,128)(2,1)S(1)}, u32[]{:S(2)}, u32[]{:S(2)}) collective-permute-start(bf16[40,768]{1,0:T(8,128)(2,1)S(1)} %get-tuple-element.77), channel_id=1, source_target_pairs={{0,128},{1,137},{2,130},{3,139},{4,140},{5,133},{6,142},{7,135},{8... | collective-permute-start | bytes 184328 | tf_op jit(solution)/shard_map/ppermute | solution.py:71
  119.2 4.8 %collective-permute-done.36.refs_2_ = bf16[40,768]{1,0:T(8,128)(2,1)S(1)} collective-permute-done((bf16[40,768]{1,0:T(8,128)(2,1)S(1)}, bf16[40,768]{1,0:T(8,128)(2,1)S(1)}, u32[]{:S(2)}, u32[]{:S(2)}) %collective-permute-start.36) | collective-permute-done | bytes 61472 | tf_op jit(solution)/shard_map/ppermute | solution.py:71
  124.4 2.3 %collective-permute-start.20 = (f32[16,64]{1,0:T(8,128)S(1)}, f32[16,64]{1,0:T(8,128)S(1)}, u32[]{:S(2)}, u32[]{:S(2)}) collective-permute-start(f32[16,64]{1,0:T(8,128)S(1)} %get-tuple-element.59), channel_id=1, source_target_pairs={{0,0},{1,9},{2,2},{3,11},{4,12},{5,5},{6,14},{7,7},{8,8},{9,1},{10... | collective-permute-start | bytes 12296 | tf_op jit(solution)/shard_map/ppermute | solution.py:71
  127.5 3.1 %collective-permute-done.38.came_ref = bf16[72,768]{1,0:T(8,128)(2,1)S(1)} collective-permute-done((bf16[72,768]{1,0:T(8,128)(2,1)S(1)}, bf16[72,768]{1,0:T(8,128)(2,1)S(1)}, u32[]{:S(2)}, u32[]{:S(2)}) %collective-permute-start.38) | collective-permute-done | bytes 110624 | tf_op jit(solution)/shard_map/ppermute | solution.py:76
  (70 shorter events, 23.9 us)
Async XLA Ops:
  0.0 65.2 %collective-permute-start.15 = (bf16[6144,256]{1,0:T(8,128)(2,1)}, bf16[6144,256]{1,0:T(8,128)(2,1)S(1)}, u32[]{:S(2)}, u32[]{:S(2)}) collective-permute-start(bf16[6144,256]{1,0:T(8,128)(2,1)} %refs_0_.1), channel_id=1, source_target_pairs={{0,8},{8,0},{1,9},{9,1},{2,10},{10,2},{3,11},{11,3},{4,12},{12,4},... | collective-permute-start | bytes 9437192 | tf_op jit(solution)/shard_map/ppermute | solution.py:80
  0.7 65.1 %collective-permute-start.16 = (bf16[6144,256]{1,0:T(8,128)(2,1)}, bf16[6144,256]{1,0:T(8,128)(2,1)S(1)}, u32[]{:S(2)}, u32[]{:S(2)}) collective-permute-start(bf16[6144,256]{1,0:T(8,128)(2,1)} %refs_1_.1), channel_id=1, source_target_pairs={{0,8},{8,0},{1,9},{9,1},{2,10},{10,2},{3,11},{11,3},{4,12},{12,4},... | collective-permute-start | bytes 9437192 | tf_op jit(solution)/shard_map/ppermute | solution.py:80
  0.7 73.7 %collective-permute-start.21 = (bf16[256,6144]{1,0:T(8,128)(2,1)}, bf16[256,6144]{1,0:T(8,128)(2,1)S(1)}, u32[]{:S(2)}, u32[]{:S(2)}) collective-permute-start(bf16[256,6144]{1,0:T(8,128)(2,1)} %refs_7_.1), channel_id=1, source_target_pairs={{0,8},{8,0},{1,9},{9,1},{2,10},{10,2},{3,11},{11,3},{4,12},{12,4},... | collective-permute-start | bytes 9437192 | tf_op jit(solution)/shard_map/ppermute | solution.py:80
  2.3 10.3 %collective-permute-start = (bf16[56,768]{1,0:T(8,128)(2,1)S(1)}, bf16[56,768]{1,0:T(8,128)(2,1)S(1)}, u32[]{:S(2)}, u32[]{:S(2)}) collective-permute-start(bf16[56,768]{1,0:T(8,128)(2,1)S(1)} %get-tuple-element.45), channel_id=1, source_target_pairs={{0,56},{8,48},{16,40},{24,32},{32,24},{40,16},{48,8},{56,0},{1,57}... | collective-permute-start | bytes 258056 | tf_op jit(solution)/shard_map/ppermute | solution.py:76
  5.0 9.0 %collective-permute-start.3 = (bf16[40,768]{1,0:T(8,128)(2,1)S(1)}, bf16[40,768]{1,0:T(8,128)(2,1)S(1)}, u32[]{:S(2)}, u32[]{:S(2)}) collective-permute-start(bf16[40,768]{1,0:T(8,128)(2,1)S(1)} %get-tuple-element.49), channel_id=1, source_target_pairs={{0,128},{1,137},{2,130},{3,139},{4,140},{5,133},{6,142},{7,135},{8... | collective-permute-start | bytes 184328 | tf_op jit(solution)/shard_map/ppermute | solution.py:71
  12.8 9.0 %collective-permute-start.2 = (bf16[40,768]{1,0:T(8,128)(2,1)S(1)}, bf16[40,768]{1,0:T(8,128)(2,1)S(1)}, u32[]{:S(2)}, u32[]{:S(2)}) collective-permute-start(bf16[40,768]{1,0:T(8,128)(2,1)S(1)} %get-tuple-element.48), channel_id=1, source_target_pairs={{0,64},{1,73},{2,66},{3,75},{4,76},{5,69},{6,78},{7,71},{8,72},{9,... | collective-permute-start | bytes 184328 | tf_op jit(solution)/shard_map/ppermute | solution.py:71
  19.2 7.9 %collective-permute-start.1 = (bf16[48,768]{1,0:T(8,128)(2,1)S(1)}, bf16[48,768]{1,0:T(8,128)(2,1)S(1)}, u32[]{:S(2)}, u32[]{:S(2)}) collective-permute-start(bf16[48,768]{1,0:T(8,128)(2,1)S(1)} %get-tuple-element.47), channel_id=1, source_target_pairs={{0,0},{1,9},{2,2},{3,11},{4,12},{5,5},{6,14},{7,7},{8,8},{9,1},{10... | collective-permute-start | bytes 221192 | tf_op jit(solution)/shard_map/ppermute | solution.py:71
  27.3 6.8 %collective-permute-start.8 = (bf16[152,768]{1,0:T(8,128)(2,1)S(1)}, bf16[152,768]{1,0:T(8,128)(2,1)S(1)}, u32[]{:S(2)}, u32[]{:S(2)}) collective-permute-start(bf16[152,768]{1,0:T(8,128)(2,1)S(1)} %shard_map.75.refs_0_), channel_id=1, source_target_pairs={{0,9},{8,16},{9,2},{1,25},{2,11},{10,18},{11,0},{3,27},{12,5},{4,2... | collective-permute-start | bytes 700424 | tf_op jit(solution)/shard_map/ppermute | solution.py:58
  28.0 8.0 %collective-permute-start.9 = (bf16[152,768]{1,0:T(8,128)(2,1)S(1)}, bf16[152,768]{1,0:T(8,128)(2,1)S(1)}, u32[]{:S(2)}, u32[]{:S(2)}) collective-permute-start(bf16[152,768]{1,0:T(8,128)(2,1)S(1)} %shard_map.75.refs_0_), channel_id=1, source_target_pairs={{0,11},{8,4},{9,0},{1,13},{2,9},{10,6},{11,2},{3,15},{12,7},{4,8},... | collective-permute-start | bytes 700424 | tf_op jit(solution)/shard_map/ppermute | solution.py:58
  34.1 7.1 %collective-permute-start.12 = (bf16[152,768]{1,0:T(8,128)(2,1)S(1)}, bf16[152,768]{1,0:T(8,128)(2,1)S(1)}, u32[]{:S(2)}, u32[]{:S(2)}) collective-permute-start(bf16[152,768]{1,0:T(8,128)(2,1)S(1)} %shard_map.75.refs_0_), channel_id=1, source_target_pairs={{0,2},{8,28},{9,11},{1,21},{2,0},{10,30},{11,9},{3,23},{12,14},{4,... | collective-permute-start | bytes 700424 | tf_op jit(solution)/shard_map/ppermute | solution.py:58
  35.9 9.5 %collective-permute-start.6 = (bf16[152,768]{1,0:T(8,128)(2,1)S(1)}, bf16[152,768]{1,0:T(8,128)(2,1)S(1)}, u32[]{:S(2)}, u32[]{:S(2)}) collective-permute-start(bf16[152,768]{1,0:T(8,128)(2,1)S(1)} %shard_map.75.refs_0_), channel_id=1, source_target_pairs={{0,24},{8,1},{9,17},{1,10},{2,26},{10,3},{11,19},{3,8},{12,20},{4,... | collective-permute-start | bytes 700424 | tf_op jit(solution)/shard_map/ppermute | solution.py:58
  41.2 8.4 %collective-permute-start.18 = (bf16[152,768]{1,0:T(8,128)(2,1)S(1)}, bf16[152,768]{1,0:T(8,128)(2,1)S(1)}, u32[]{:S(2)}, u32[]{:S(2)}) collective-permute-start(bf16[152,768]{1,0:T(8,128)(2,1)S(1)} %shard_map.75.refs_0_), channel_id=1, source_target_pairs={{0,12},{8,3},{9,5},{1,8},{2,14},{10,1},{11,7},{3,10},{12,0},{4,15}... | collective-permute-start | bytes 700424 | tf_op jit(solution)/shard_map/ppermute | solution.py:58
  51.3 9.0 %collective-permute-start.10 = (bf16[2,152,768]{2,1,0:T(8,128)(2,1)S(1)}, bf16[2,152,768]{2,1,0:T(8,128)(2,1)S(1)}, u32[]{:S(2)}, u32[]{:S(2)}) collective-permute-start(bf16[2,152,768]{2,1,0:T(8,128)(2,1)S(1)} %shard_map.76), channel_id=1, source_target_pairs={{0,12},{8,3},{9,5},{1,8},{2,14},{10,1},{11,7},{3,10},{12,0},{4,15}... | collective-permute-start | bytes 1400840 | tf_op jit(solution)/shard_map/ppermute | solution.py:58
  55.3 8.7 %collective-permute-start.17 = (bf16[2,152,768]{2,1,0:T(8,128)(2,1)S(1)}, bf16[2,152,768]{2,1,0:T(8,128)(2,1)S(1)}, u32[]{:S(2)}, u32[]{:S(2)}) collective-permute-start(bf16[2,152,768]{2,1,0:T(8,128)(2,1)S(1)} %shard_map.76), channel_id=1, source_target_pairs={{0,24},{8,1},{9,17},{1,10},{2,26},{10,3},{11,19},{3,8},{12,20},{4,... | collective-permute-start | bytes 1400840 | tf_op jit(solution)/shard_map/ppermute | solution.py:58
  60.3 12.1 %collective-permute-start.11 = (bf16[2,152,768]{2,1,0:T(8,128)(2,1)S(1)}, bf16[2,152,768]{2,1,0:T(8,128)(2,1)S(1)}, u32[]{:S(2)}, u32[]{:S(2)}) collective-permute-start(bf16[2,152,768]{2,1,0:T(8,128)(2,1)S(1)} %collective-permute-done.10.refs_6_), channel_id=1, source_target_pairs={{0,24},{8,3},{9,17},{1,8},{2,26},{10,1},{11,19},{3,10},{12,20},{4,... | collective-permute-start | bytes 1400840 | tf_op jit(solution)/shard_map/ppermute | solution.py:58
  65.2 7.1 %collective-permute-start.14 = (bf16[152,768]{1,0:T(8,128)(2,1)S(1)}, bf16[152,768]{1,0:T(8,128)(2,1)S(1)}, u32[]{:S(2)}, u32[]{:S(2)}) collective-permute-start(bf16[152,768]{1,0:T(8,128)(2,1)S(1)} %collective-permute-done.13.refs_5_), channel_id=1, source_target_pairs={{0,12},{8,1},{9,5},{1,10},{2,14},{10,3},{11,7},{3,8},{12,0},{4,13}... | collective-permute-start | bytes 700424 | tf_op jit(solution)/shard_map/ppermute | solution.py:58
  75.6 8.1 %collective-permute-start.28 = (bf16[288,768]{1,0:T(8,128)(2,1)S(1)}, bf16[288,768]{1,0:T(8,128)(2,1)S(1)}, u32[]{:S(2)}, u32[]{:S(2)}) collective-permute-start(bf16[288,768]{1,0:T(8,128)(2,1)S(1)} %get-tuple-element.71), channel_id=1, source_target_pairs={{0,24},{8,1},{9,17},{1,10},{2,26},{10,3},{11,19},{3,8},{12,20},{4,... | collective-permute-start | bytes 1327112 | tf_op jit(solution)/shard_map/ppermute | solution.py:58
  77.2 9.5 %collective-permute-start.22 = (bf16[288,768]{1,0:T(8,128)(2,1)S(1)}, bf16[288,768]{1,0:T(8,128)(2,1)S(1)}, u32[]{:S(2)}, u32[]{:S(2)}) collective-permute-start(bf16[288,768]{1,0:T(8,128)(2,1)S(1)} %get-tuple-element.64), channel_id=1, source_target_pairs={{0,12},{8,3},{9,5},{1,8},{2,14},{10,1},{11,7},{3,10},{12,0},{4,15}... | collective-permute-start | bytes 1327112 | tf_op jit(solution)/shard_map/ppermute | solution.py:58
  80.9 8.1 %collective-permute-start.30 = (bf16[288,768]{1,0:T(8,128)(2,1)S(1)}, bf16[288,768]{1,0:T(8,128)(2,1)S(1)}, u32[]{:S(2)}, u32[]{:S(2)}) collective-permute-start(bf16[288,768]{1,0:T(8,128)(2,1)S(1)} %get-tuple-element.72), channel_id=1, source_target_pairs={{0,24},{8,3},{9,17},{1,8},{2,26},{10,1},{11,19},{3,10},{12,20},{4,... | collective-permute-start | bytes 1327112 | tf_op jit(solution)/shard_map/ppermute | solution.py:58
  84.8 7.1 %collective-permute-start.29 = (bf16[144,768]{1,0:T(8,128)(2,1)S(1)}, bf16[144,768]{1,0:T(8,128)(2,1)S(1)}, u32[]{:S(2)}, u32[]{:S(2)}) collective-permute-start(bf16[144,768]{1,0:T(8,128)(2,1)S(1)} %shard_map.80), channel_id=1, source_target_pairs={{0,12},{8,1},{9,5},{1,10},{2,14},{10,3},{11,7},{3,8},{12,0},{4,13}... | collective-permute-start | bytes 663560 | tf_op jit(solution)/shard_map/ppermute | solution.py:58
  85.8 8.5 %collective-permute-start.26 = (bf16[144,768]{1,0:T(8,128)(2,1)S(1)}, bf16[144,768]{1,0:T(8,128)(2,1)S(1)}, u32[]{:S(2)}, u32[]{:S(2)}) collective-permute-start(bf16[144,768]{1,0:T(8,128)(2,1)S(1)} %get-tuple-element.68), channel_id=1, source_target_pairs={{0,12},{8,1},{9,5},{1,10},{2,14},{10,3},{11,7},{3,8},{12,0},{4,13}... | collective-permute-start | bytes 663560 | tf_op jit(solution)/shard_map/ppermute | solution.py:58
  86.7 7.6 %collective-permute-start.25 = (bf16[144,768]{1,0:T(8,128)(2,1)S(1)}, bf16[144,768]{1,0:T(8,128)(2,1)S(1)}, u32[]{:S(2)}, u32[]{:S(2)}) collective-permute-start(bf16[144,768]{1,0:T(8,128)(2,1)S(1)} %shard_map.78), channel_id=1, source_target_pairs={{0,24},{8,3},{9,17},{1,8},{2,26},{10,1},{11,19},{3,10},{12,20},{4,... | collective-permute-start | bytes 663560 | tf_op jit(solution)/shard_map/ppermute | solution.py:58
  89.0 8.4 %collective-permute-start.24 = (bf16[144,768]{1,0:T(8,128)(2,1)S(1)}, bf16[144,768]{1,0:T(8,128)(2,1)S(1)}, u32[]{:S(2)}, u32[]{:S(2)}) collective-permute-start(bf16[144,768]{1,0:T(8,128)(2,1)S(1)} %get-tuple-element.65), channel_id=1, source_target_pairs={{0,12},{8,1},{9,5},{1,10},{2,14},{10,3},{11,7},{3,8},{12,0},{4,13}... | collective-permute-start | bytes 663560 | tf_op jit(solution)/shard_map/ppermute | solution.py:58
  89.5 7.9 %collective-permute-start.23 = (bf16[144,768]{1,0:T(8,128)(2,1)S(1)}, bf16[144,768]{1,0:T(8,128)(2,1)S(1)}, u32[]{:S(2)}, u32[]{:S(2)}) collective-permute-start(bf16[144,768]{1,0:T(8,128)(2,1)S(1)} %shard_map.77), channel_id=1, source_target_pairs={{0,24},{8,3},{9,17},{1,8},{2,26},{10,1},{11,19},{3,10},{12,20},{4,... | collective-permute-start | bytes 663560 | tf_op jit(solution)/shard_map/ppermute | solution.py:58
  91.9 7.9 %collective-permute-start.33 = (bf16[144,768]{1,0:T(8,128)(2,1)S(1)}, bf16[144,768]{1,0:T(8,128)(2,1)S(1)}, u32[]{:S(2)}, u32[]{:S(2)}) collective-permute-start(bf16[144,768]{1,0:T(8,128)(2,1)S(1)} %shard_map.83), channel_id=1, source_target_pairs={{0,2},{8,28},{9,11},{1,21},{2,0},{10,30},{11,9},{3,23},{12,14},{4,... | collective-permute-start | bytes 663560 | tf_op jit(solution)/shard_map/ppermute | solution.py:58
  94.3 8.3 %collective-permute-start.31 = (bf16[144,768]{1,0:T(8,128)(2,1)S(1)}, bf16[144,768]{1,0:T(8,128)(2,1)S(1)}, u32[]{:S(2)}, u32[]{:S(2)}) collective-permute-start(bf16[144,768]{1,0:T(8,128)(2,1)S(1)} %shard_map.81), channel_id=1, source_target_pairs={{0,9},{8,4},{9,2},{1,13},{2,11},{10,6},{11,0},{3,15},{12,5},{4,8},... | collective-permute-start | bytes 663560 | tf_op jit(solution)/shard_map/ppermute | solution.py:58
  94.4 8.2 %collective-permute-start.27 = (bf16[144,768]{1,0:T(8,128)(2,1)S(1)}, bf16[144,768]{1,0:T(8,128)(2,1)S(1)}, u32[]{:S(2)}, u32[]{:S(2)}) collective-permute-start(bf16[144,768]{1,0:T(8,128)(2,1)S(1)} %shard_map.79), channel_id=1, source_target_pairs={{0,11},{8,16},{9,0},{1,25},{2,9},{10,18},{11,2},{3,27},{12,7},{4,2... | collective-permute-start | bytes 663560 | tf_op jit(solution)/shard_map/ppermute | solution.py:58
  102.9 16.3 %collective-permute-start.34 = (bf16[40,768]{1,0:T(8,128)(2,1)S(1)}, bf16[40,768]{1,0:T(8,128)(2,1)S(1)}, u32[]{:S(2)}, u32[]{:S(2)}) collective-permute-start(bf16[40,768]{1,0:T(8,128)(2,1)S(1)} %get-tuple-element.75), channel_id=1, source_target_pairs={{0,0},{1,9},{2,2},{3,11},{4,12},{5,5},{6,14},{7,7},{8,8},{9,1},{10... | collective-permute-start | bytes 184328 | tf_op jit(solution)/shard_map/ppermute | solution.py:71
  112.1 7.2 %collective-permute-start.35 = (bf16[40,768]{1,0:T(8,128)(2,1)S(1)}, bf16[40,768]{1,0:T(8,128)(2,1)S(1)}, u32[]{:S(2)}, u32[]{:S(2)}) collective-permute-start(bf16[40,768]{1,0:T(8,128)(2,1)S(1)} %get-tuple-element.76), channel_id=1, source_target_pairs={{0,192},{1,201},{2,194},{3,203},{4,204},{5,197},{6,206},{7,199},{8... | collective-permute-start | bytes 184328 | tf_op jit(solution)/shard_map/ppermute | solution.py:71
  115.9 8.1 %collective-permute-start.36 = (bf16[40,768]{1,0:T(8,128)(2,1)S(1)}, bf16[40,768]{1,0:T(8,128)(2,1)S(1)}, u32[]{:S(2)}, u32[]{:S(2)}) collective-permute-start(bf16[40,768]{1,0:T(8,128)(2,1)S(1)} %get-tuple-element.77), channel_id=1, source_target_pairs={{0,128},{1,137},{2,130},{3,139},{4,140},{5,133},{6,142},{7,135},{8... | collective-permute-start | bytes 184328 | tf_op jit(solution)/shard_map/ppermute | solution.py:71
  117.8 6.2 %collective-permute-start.37 = (bf16[40,768]{1,0:T(8,128)(2,1)S(1)}, bf16[40,768]{1,0:T(8,128)(2,1)S(1)}, u32[]{:S(2)}, u32[]{:S(2)}) collective-permute-start(bf16[40,768]{1,0:T(8,128)(2,1)S(1)} %get-tuple-element.78), channel_id=1, source_target_pairs={{0,64},{1,73},{2,66},{3,75},{4,76},{5,69},{6,78},{7,71},{8,72},{9,... | collective-permute-start | bytes 184328 | tf_op jit(solution)/shard_map/ppermute | solution.py:71
  124.3 6.4 %collective-permute-start.38 = (bf16[72,768]{1,0:T(8,128)(2,1)S(1)}, bf16[72,768]{1,0:T(8,128)(2,1)S(1)}, u32[]{:S(2)}, u32[]{:S(2)}) collective-permute-start(bf16[72,768]{1,0:T(8,128)(2,1)S(1)} %get-tuple-element.80), channel_id=1, source_target_pairs={{0,56},{8,48},{16,40},{24,32},{32,24},{40,16},{48,8},{56,0},{1,57}... | collective-permute-start | bytes 331784 | tf_op jit(solution)/shard_map/ppermute | solution.py:76
  (8 other events, 80.8 us)

commit v5 on v4

--- a/solution.py
+++ b/solution.py
@@ -103,7 +103,7 @@
 
 
 def moved(shape, source_of, *blocks):
-    joined = jnp.concatenate([b[...] for b in blocks], axis=0)
+    joined = jnp.concatenate([b[...] for b in blocks], axis=0) if len(blocks) > 1 else blocks[0][...]
     row = lax.broadcasted_iota(jnp.int32, (shape[0], joined.shape[0]), 0)
     column = lax.broadcasted_iota(jnp.int32, (shape[0], joined.shape[0]), 1)
     source, valid = source_of(row)
@@ -120,15 +120,10 @@
     return half, distance, row - k * CAP, k < jnp.where(part == 2, 2, 3)
 
 
-def returning(row):
-    k = (row * 3641) >> 16
-    return k >> 2, k & 3, row - k * CAP, row >= 0
-
-
-def slots_of(ids, order, rows):
+def slots_of(ids):
     tokens = ids.shape[1]
-    slot = lax.broadcasted_iota(jnp.int32, (rows, tokens), 0)
-    half, distance, inside, valid = order(slot)
+    slot = lax.broadcasted_iota(jnp.int32, (2 * NEAR + BLOCK, tokens), 0)
+    half, distance, inside, valid = leaving(slot)
     zh, y2 = lax.axis_index("zh"), lax.axis_index("y2")
     expert = ((zh + distance) & 3) * 2 + (y2 ^ half)
     first, second = ids[0:1, :] == expert, ids[1:2, :] == expert
@@ -149,7 +144,7 @@
     fetch.start()
     fetch_tokens.start()
     fetch.wait()
-    first, second = slots_of(ids_ref[...], leaving, 2 * NEAR + BLOCK)
+    first, second = slots_of(ids_ref[...])
     picks = jnp.where(first | second, 1.0, 0.0).astype(BF16)
     fetch_tokens.wait()
     chosen = jnp.dot(picks, tokens_ref[...], preferred_element_type=F32).astype(BF16)
@@ -239,28 +234,46 @@
 
 
 def unpack_kernel(*refs):
-    terms, out_refs = refs[:-FAR], refs[-FAR:]
+    terms, out_refs = refs[:-5], refs[-5:]
     total = sum(t[...].astype(F32) for t in terms).astype(BF16)
 
     def source_of(row):
-        block, inside, _ = in_blocks(row)
-        return block * 2 * CAP + inside, inside < 2 * CAP
-
-    rows = moved((FAR * BLOCK, 0), source_of, total)
-    for k, out in enumerate(out_refs):
-        out[...] = rows[k * BLOCK : (k + 1) * BLOCK].astype(BF16)
+        part, inside, _ = in_blocks(row)
+        halves_row = row - 3 * BLOCK
+        half = jnp.where(halves_row >= CROSSED, 1, 0)
+        halves_row = halves_row - half * CROSSED
+        block = jnp.where(part == 2, 3, part)
+        near = row < 3 * BLOCK
+        source = jnp.where(near, block * 2 * CAP + inside, (4 + half) * CAP + halves_row)
+        return source, jnp.where(near, inside - 2 * CAP, halves_row - CAP) < 0
+
+    rows = moved((3 * BLOCK + 2 * CROSSED, 0), source_of, total).astype(BF16)
+    start = 0
+    for out in out_refs:
+        out[...] = rows[start : start + out.shape[0]]
+        start += out.shape[0]
+
+
+def join_kernel(keep_ref, came_ref, out_ref):
+    def source_of(row):
+        half = jnp.where(row < CAP, 0, 1)
+        return half * CROSSED + row - half * CAP, row < 2 * CAP
+
+    out_ref[...] = moved((BLOCK, 0), source_of, keep_ref, came_ref).astype(BF16)
 
 
 def unshuffle_kernel(*refs):
-    blocks, (keep_ref, send_ref) = refs[:FAR], refs[FAR:]
+    blocks, (keep_ref, send_ref) = refs[:3], refs[3:]
 
     def source_of(row):
+        half = jnp.where(row < NEAR, 0, 1)
+        row = row - half * NEAR
         k = (row * 3641) >> 16
-        return (k & 3) * BLOCK + (k >> 2) * CAP + row - k * CAP, row >= 0
-
-    rows = moved((ROWS, 0), source_of, *blocks).astype(BF16)
-    keep_ref[...] = rows[:KEPT]
-    send_ref[...] = rows[KEPT:]
+        return k * BLOCK + half * CAP + row - k * CAP, k < 3
+
+    rows = moved((2 * NEAR, 0), source_of, *blocks).astype(BF16)
+    keep_ref[...] = rows[:NEAR]
+    send_ref[...] = rows[NEAR:]
 
 
 def transposed_dot(left, right):
@@ -342,7 +355,7 @@
     return parts[0] + parts[1], parts[2] + parts[3]
 
 
-def combine_kernel(width_all, ids_ref, sums_ref, keep_ref, came_ref, out_ref):
+def combine_kernel(width_all, ids_ref, sums_ref, keep_ref, came_ref, far_ref, out_ref):
     ids = ids_ref[...]
     sums = sums_ref[...]
     experts = sums.shape[0] // 2
@@ -355,9 +368,9 @@
     ]
     gate_first = 1.0 / (1.0 + jnp.exp(logits[1] - logits[0]))
     gate_second = 1.0 / (1.0 + jnp.exp(logits[0] - logits[1]))
-    first, second = slots_of(ids, returning, ROWS)
+    first, second = slots_of(ids)
     weights = jnp.where(first, gate_first, 0.0) + jnp.where(second, gate_second, 0.0)
-    rows = jnp.concatenate([keep_ref[...], came_ref[...]], axis=0)
+    rows = jnp.concatenate([keep_ref[...], came_ref[...], far_ref[...]], axis=0)
     out_ref[...] = sum(
         lax.dot_general(w, rows, (((0,), (0,)), ((), ())), preferred_element_type=F32)
         for w in halves(weights)
@@ -632,7 +645,7 @@
     width = tokens.shape[1]
     gain = norm_gain.reshape(1, width_all)
     ids = expert_ids.T
-    kept, block = (KEPT, width), (BLOCK, width)
+    block = (BLOCK, width)
 
     keep, send, far = select(ids, tokens)
     part_sums, gain = stats(tokens, gain, router_weight.T)
@@ -697,18 +710,23 @@
         hop(added(*parts[2]), "x+", "z"),
         hop(added(*parts[3]), "xx", "yz"),
     ]
-    blocks = small(unpack_kernel, [block] * FAR, *terms)
-    back = [along_z(blocks[k], (FAR - k) % FAR) for k in range(FAR)]
-    keep, send = small(unshuffle_kernel, [kept, kept], *back)
+    crossed = (CROSSED, width)
+    stay, one, three, two, other = small(unpack_kernel, [block] * 3 + [crossed] * 2, *terms)
+    other = across_y(other)
+    one, three = along_z(one, 3), along_z(three, 1)
+    stay = along_z(stay, 0)
+    (far,) = small(join_kernel, [block], two, other)
+    far = along_z(far, 2)
+    keep, send = small(unshuffle_kernel, [(NEAR, width)] * 2, stay, one, three)
     came = across_y(send)
     return pl.pallas_call(
         partial(combine_kernel, width_all),
         out_shape=jax.ShapeDtypeStruct(tokens.shape, BF16),
-        in_specs=vmem(4),
+        in_specs=vmem(5),
         out_specs=vmem(1)[0],
         compiler_params=pltpu.CompilerParams(vmem_limit_bytes=4 << 20),
         name="combine",
-    )(ids, sums, keep, came)
+    )(ids, sums, keep, came, far)
 
 
 def solution(mesh):

time: 132 us -> 133 us (level)
  waiting for transfers between devices: 49.5 us -> 52.2 us
  starting transfers between devices: 63.5 us -> 61.8 us
    ppermute x9, waiting for transfers between devices: 6.94 us -> 12.8 us  [along_z(): return lax.ppermute(value, ('zh', 'c', 'zl', 'x'), pairs)]
    ppermute x3 -> x4, waiting for transfers between devices: 7.26 us -> 4.12 us  [across_y(): return lax.ppermute(value, ('y2', 'y1', 'c'), pairs)]
    ppermute x9, starting transfers between devices: 32.7 us -> 31 us  [along_z(): return lax.ppermute(value, ('zh', 'c', 'zl', 'x'), pairs)]
    ppermute x3 -> x4, starting transfers between devices: 3.73 us -> 3.73 us  [across_y(): return lax.ppermute(value, ('y2', 'y1', 'c'), pairs)]
  transfers between devices with their start and end apart: 39 -> 40, of which waited for: 19 -> 20; matrix products, arithmetic and copies ran while one was open for 0% -> 0% of each run, Pallas kernels for 12% -> 12%
where the time goes in v5:
time: 133 us
  starting transfers between devices  61.8 us (46%)
  waiting for transfers between devices  52.2 us (39%)
  Pallas kernels  18.6 us (14%)
    ppermute x24, waiting for transfers between devices, hop(): return lax.ppermute(value, OWNER, owner_pairs(step_core0, step_core1))  35.3 us
    ppermute x9, starting transfers between devices, along_z(): return lax.ppermute(value, ('zh', 'c', 'zl', 'x'), pairs)  31 us
    ppermute x24, starting transfers between devices, hop(): return lax.ppermute(value, OWNER, owner_pairs(step_core0, step_core1))  25.8 us
    ppermute x9, waiting for transfers between devices, along_z(): return lax.ppermute(value, ('zh', 'c', 'zl', 'x'), pairs)  12.8 us
    pallas_call x1, Pallas kernels, early_of(): pl.pallas_call(partial(early_kernel, where), out_shape=[jax.ShapeDtypeStr...  4.18 us
    ppermute x4, waiting for transfers between devices, across_y(): return lax.ppermute(value, ('y2', 'y1', 'c'), pairs)  4.12 us
    ppermute x4, starting transfers between devices, across_y(): return lax.ppermute(value, ('y2', 'y1', 'c'), pairs)  3.73 us
    pallas_call x2, Pallas kernels, down_of(): pl.pallas_call(partial(down_kernel, far, places), out_shape=[jax.ShapeDty...  3.58 us
  transfers between devices with their start and end apart: 40, of which 20 were waited for; matrix products, arithmetic and copies ran while one was open for 0% of the time, Pallas kernels for 12%

profile of v5, /device:TPU:33, one launch (start us, length us, event | category | flops | bytes accessed | tf_op | source)
XLA Modules:
  0.0 132.8 jit_solution(17219983446173318787)
XLA Ops:
  2.3 2.7 %collective-permute-start = (bf16[56,768]{1,0:T(8,128)(2,1)S(1)}, bf16[56,768]{1,0:T(8,128)(2,1)S(1)}, u32[]{:S(2)}, u32[]{:S(2)}) collective-permute-start(bf16[56,768]{1,0:T(8,128)(2,1)S(1)} %get-tuple-element.46), channel_id=1, source_target_pairs={{0,56},{8,48},{16,40},{24,32},{32,24},{40,16},{48,8},{56,0},{1,57}... | collective-permute-start | bytes 258056 | tf_op jit(solution)/shard_map/ppermute | solution.py:76
  5.0 6.4 %collective-permute-start.3 = (bf16[40,768]{1,0:T(8,128)(2,1)S(1)}, bf16[40,768]{1,0:T(8,128)(2,1)S(1)}, u32[]{:S(2)}, u32[]{:S(2)}) collective-permute-start(bf16[40,768]{1,0:T(8,128)(2,1)S(1)} %get-tuple-element.50), channel_id=1, source_target_pairs={{0,128},{1,137},{2,130},{3,139},{4,140},{5,133},{6,142},{7,135},{8... | collective-permute-start | bytes 184328 | tf_op jit(solution)/shard_map/ppermute | solution.py:71
  15.1 4.1 %collective-permute-done.5.crossed_ref = bf16[24,768]{1,0:T(8,128)(2,1)S(1)} collective-permute-done((bf16[24,768]{1,0:T(8,128)(2,1)S(1)}, bf16[24,768]{1,0:T(8,128)(2,1)S(1)}, u32[]{:S(2)}, u32[]{:S(2)}) %collective-permute-start.5) | collective-permute-done | bytes 36896 | tf_op jit(solution)/shard_map/ppermute | solution.py:76
  19.2 2.6 %collective-permute-start.1 = (bf16[48,768]{1,0:T(8,128)(2,1)S(1)}, bf16[48,768]{1,0:T(8,128)(2,1)S(1)}, u32[]{:S(2)}, u32[]{:S(2)}) collective-permute-start(bf16[48,768]{1,0:T(8,128)(2,1)S(1)} %get-tuple-element.48), channel_id=1, source_target_pairs={{0,0},{1,9},{2,2},{3,11},{4,12},{5,5},{6,14},{7,7},{8,8},{9,1},{10... | collective-permute-start | bytes 221192 | tf_op jit(solution)/shard_map/ppermute | solution.py:71
  21.8 4.0 %collective-permute-start.4 = (bf16[40,768]{1,0:T(8,128)(2,1)S(1)}, bf16[40,768]{1,0:T(8,128)(2,1)S(1)}, u32[]{:S(2)}, u32[]{:S(2)}) collective-permute-start(bf16[40,768]{1,0:T(8,128)(2,1)S(1)} %get-tuple-element.51), channel_id=1, source_target_pairs={{0,192},{1,201},{2,194},{3,203},{4,204},{5,197},{6,206},{7,199},{8... | collective-permute-start | bytes 184328 | tf_op jit(solution)/shard_map/ppermute | solution.py:71
  28.0 2.4 %collective-permute-start.9 = (bf16[152,768]{1,0:T(8,128)(2,1)S(1)}, bf16[152,768]{1,0:T(8,128)(2,1)S(1)}, u32[]{:S(2)}, u32[]{:S(2)}) collective-permute-start(bf16[152,768]{1,0:T(8,128)(2,1)S(1)} %shard_map.75.refs_0_), channel_id=1, source_target_pairs={{0,11},{8,4},{9,0},{1,13},{2,9},{10,6},{11,2},{3,15},{12,7},{4,8},... | collective-permute-start | bytes 700424 | tf_op jit(solution)/shard_map/ppermute | solution.py:58
  30.4 3.7 %collective-permute-done.8.first_ref.refs_1_ = bf16[152,768]{1,0:T(8,128)(2,1)S(1)} collective-permute-done((bf16[152,768]{1,0:T(8,128)(2,1)S(1)}, bf16[152,768]{1,0:T(8,128)(2,1)S(1)}, u32[]{:S(2)}, u32[]{:S(2)}) %collective-permute-start.8) | collective-permute-done | bytes 233504 | tf_op jit(solution)/shard_map/ppermute | solution.py:58
  34.1 1.8 %collective-permute-start.12 = (bf16[152,768]{1,0:T(8,128)(2,1)S(1)}, bf16[152,768]{1,0:T(8,128)(2,1)S(1)}, u32[]{:S(2)}, u32[]{:S(2)}) collective-permute-start(bf16[152,768]{1,0:T(8,128)(2,1)S(1)} %shard_map.75.refs_0_), channel_id=1, source_target_pairs={{0,2},{8,28},{9,11},{1,21},{2,0},{10,30},{11,9},{3,23},{12,14},{4,... | collective-permute-start | bytes 700424 | tf_op jit(solution)/shard_map/ppermute | solution.py:58
  35.9 5.2 %collective-permute-done.12.refs_3_ = bf16[152,768]{1,0:T(8,128)(2,1)S(1)} collective-permute-done((bf16[152,768]{1,0:T(8,128)(2,1)S(1)}, bf16[152,768]{1,0:T(8,128)(2,1)S(1)}, u32[]{:S(2)}, u32[]{:S(2)}) %collective-permute-start.12) | collective-permute-done | bytes 233504 | tf_op jit(solution)/shard_map/ppermute | solution.py:58
  41.2 4.3 %collective-permute-start.18 = (bf16[152,768]{1,0:T(8,128)(2,1)S(1)}, bf16[152,768]{1,0:T(8,128)(2,1)S(1)}, u32[]{:S(2)}, u32[]{:S(2)}) collective-permute-start(bf16[152,768]{1,0:T(8,128)(2,1)S(1)} %shard_map.75.refs_0_), channel_id=1, source_target_pairs={{0,12},{8,3},{9,5},{1,8},{2,14},{10,1},{11,7},{3,10},{12,0},{4,15}... | collective-permute-start | bytes 700424 | tf_op jit(solution)/shard_map/ppermute | solution.py:58
  45.5 4.0 %collective-permute-done.18.refs_1_ = bf16[152,768]{1,0:T(8,128)(2,1)S(1)} collective-permute-done((bf16[152,768]{1,0:T(8,128)(2,1)S(1)}, bf16[152,768]{1,0:T(8,128)(2,1)S(1)}, u32[]{:S(2)}, u32[]{:S(2)}) %collective-permute-start.18) | collective-permute-done | bytes 233504 | tf_op jit(solution)/shard_map/ppermute | solution.py:58
  51.4 3.9 %collective-permute-done.19.refs_2_ = bf16[152,768]{1,0:T(8,128)(2,1)S(1)} collective-permute-done((bf16[152,768]{1,0:T(8,128)(2,1)S(1)}, bf16[152,768]{1,0:T(8,128)(2,1)S(1)}, u32[]{:S(2)}, u32[]{:S(2)}) %collective-permute-start.19) | collective-permute-done | bytes 233504 | tf_op jit(solution)/shard_map/ppermute | solution.py:58
  55.3 5.0 %collective-permute-done.10.refs_6_ = bf16[2,152,768]{2,1,0:T(8,128)(2,1)S(1)} collective-permute-done((bf16[2,152,768]{2,1,0:T(8,128)(2,1)S(1)}, bf16[2,152,768]{2,1,0:T(8,128)(2,1)S(1)}, u32[]{:S(2)}, u32[]{:S(2)}) %collective-permute-start.10) | collective-permute-done | bytes 466976 | tf_op jit(solution)/shard_map/ppermute | solution.py:58
  60.3 2.9 %fetch.1 = (bf16[6144,256]{1,0:T(8,128)(2,1)S(1)}, bf16[6144,256]{1,0:T(8,128)(2,1)S(1)}) custom-call(bf16[6144,256]{1,0:T(8,128)(2,1)} %refs_0_.1, bf16[6144,256]{1,0:T(8,128)(2,1)} %refs_1_.1), custom_call_target="tpu_custom_call" | custom-call | tf_op jit(solution)/shard_map/fetch/pallas_call | solution.py:342
  65.8 4.2 %early.1 = (bf16[256,6144]{1,0:T(8,128)(2,1)S(1)}, f32[4,288,256]{2,1,0:T(8,128)S(1)}, bf16[288,6144]{1,0:T(8,128)(2,1)S(1)}, f32[288,128]{1,0:T(8,128)S(1)}, f32[16,64]{1,0:T(8,128)S(1)}) custom-call(f32[1,6144]{1,0:T(1,128)S(1)} %get-tuple-element.44.gain_ref, ...), custom_call_target="tpu_custom_call", output_to_operand_aliasing={{2}: (9, {}), {3}: (10, {}), {4}: (11, {})} | custom-call | flops 3623878656 | bytes 12582912 | tf_op jit(solution)/shard_map/early/pallas_call | solution.py:483
  70.0 2.3 %collective-permute-done.14.refs_2_ = bf16[152,768]{1,0:T(8,128)(2,1)S(1)} collective-permute-done((bf16[152,768]{1,0:T(8,128)(2,1)S(1)}, bf16[152,768]{1,0:T(8,128)(2,1)S(1)}, u32[]{:S(2)}, u32[]{:S(2)}) %collective-permute-start.14) | collective-permute-done | bytes 233504 | tf_op jit(solution)/shard_map/ppermute | solution.py:58
  72.4 2.0 %late.1 = (bf16[288,512]{1,0:T(8,128)(2,1)S(1)}, f32[16,64]{1,0:T(8,128)S(1)}, f32[4,288,256]{2,1,0:T(8,128)S(1)}) custom-call(f32[1,6144]{1,0:T(1,128)S(1)} %get-tuple-element.44.gain_ref, bf16[152,768]{1,0:T(8,128)(2,1)S(1)} %collective-permute-done.7.refs_0_, ...), custom_call_target="tpu_custom_call", output_to_operand_aliasing={{2}: (8, {})} | custom-call | flops 905969664 | bytes 2359296 | tf_op jit(solution)/shard_map/late/pallas_call | solution.py:538
  75.6 1.5 %collective-permute-start.28 = (bf16[288,768]{1,0:T(8,128)(2,1)S(1)}, bf16[288,768]{1,0:T(8,128)(2,1)S(1)}, u32[]{:S(2)}, u32[]{:S(2)}) collective-permute-start(bf16[288,768]{1,0:T(8,128)(2,1)S(1)} %get-tuple-element.72), channel_id=1, source_target_pairs={{0,24},{8,1},{9,17},{1,10},{2,26},{10,3},{11,19},{3,8},{12,20},{4,... | collective-permute-start | bytes 1327112 | tf_op jit(solution)/shard_map/ppermute | solution.py:58
  78.6 2.3 %rest.1 = (bf16[144,768]{1,0:T(8,128)(2,1)S(1)}, bf16[144,768]{1,0:T(8,128)(2,1)S(1)}, bf16[144,768]{1,0:T(8,128)(2,1)S(1)}, bf16[144,768]{1,0:T(8,128)(2,1)S(1)...) custom-call(bf16[288,512]{1,0:T(8,128)(2,1)S(1)} %get-tuple-element., ...), custom_call_target="tpu_custom_call" | custom-call | flops 1358954496 | bytes 6291456 | tf_op jit(solution)/shard_map/rest/pallas_call | solution.py:611
  81.1 2.6 %collective-permute-done.28.refs_1_ = bf16[288,768]{1,0:T(8,128)(2,1)S(1)} collective-permute-done((bf16[288,768]{1,0:T(8,128)(2,1)S(1)}, bf16[288,768]{1,0:T(8,128)(2,1)S(1)}, u32[]{:S(2)}, u32[]{:S(2)}) %collective-permute-start.28) | collective-permute-done | bytes 442400 | tf_op jit(solution)/shard_map/ppermute | solution.py:58
  86.7 2.1 %collective-permute-start.25 = (bf16[144,768]{1,0:T(8,128)(2,1)S(1)}, bf16[144,768]{1,0:T(8,128)(2,1)S(1)}, u32[]{:S(2)}, u32[]{:S(2)}) collective-permute-start(bf16[144,768]{1,0:T(8,128)(2,1)S(1)} %shard_map.78), channel_id=1, source_target_pairs={{0,24},{8,3},{9,17},{1,8},{2,26},{10,1},{11,19},{3,10},{12,20},{4,... | collective-permute-start | bytes 663560 | tf_op jit(solution)/shard_map/ppermute | solution.py:58
  89.5 1.8 %collective-permute-start.23 = (bf16[144,768]{1,0:T(8,128)(2,1)S(1)}, bf16[144,768]{1,0:T(8,128)(2,1)S(1)}, u32[]{:S(2)}, u32[]{:S(2)}) collective-permute-start(bf16[144,768]{1,0:T(8,128)(2,1)S(1)} %shard_map.77), channel_id=1, source_target_pairs={{0,24},{8,3},{9,17},{1,8},{2,26},{10,1},{11,19},{3,10},{12,20},{4,... | collective-permute-start | bytes 663560 | tf_op jit(solution)/shard_map/ppermute | solution.py:58
  92.1 2.2 %collective-permute-done.26.refs_2_ = bf16[144,768]{1,0:T(8,128)(2,1)S(1)} collective-permute-done((bf16[144,768]{1,0:T(8,128)(2,1)S(1)}, bf16[144,768]{1,0:T(8,128)(2,1)S(1)}, u32[]{:S(2)}, u32[]{:S(2)}) %collective-permute-start.26) | collective-permute-done | bytes 221216 | tf_op jit(solution)/shard_map/ppermute | solution.py:58
  94.4 3.0 %collective-permute-start.27 = (bf16[144,768]{1,0:T(8,128)(2,1)S(1)}, bf16[144,768]{1,0:T(8,128)(2,1)S(1)}, u32[]{:S(2)}, u32[]{:S(2)}) collective-permute-start(bf16[144,768]{1,0:T(8,128)(2,1)S(1)} %shard_map.79), channel_id=1, source_target_pairs={{0,11},{8,16},{9,0},{1,25},{2,9},{10,18},{11,2},{3,27},{12,7},{4,2... | collective-permute-start | bytes 663560 | tf_op jit(solution)/shard_map/ppermute | solution.py:58
  97.4 2.4 %collective-permute-done.33.refs_5_ = bf16[144,768]{1,0:T(8,128)(2,1)S(1)} collective-permute-done((bf16[144,768]{1,0:T(8,128)(2,1)S(1)}, bf16[144,768]{1,0:T(8,128)(2,1)S(1)}, u32[]{:S(2)}, u32[]{:S(2)}) %collective-permute-start.33) | collective-permute-done | bytes 221216 | tf_op jit(solution)/shard_map/ppermute | solution.py:58
  99.8 2.7 %collective-permute-done.31.refs_4_ = bf16[144,768]{1,0:T(8,128)(2,1)S(1)} collective-permute-done((bf16[144,768]{1,0:T(8,128)(2,1)S(1)}, bf16[144,768]{1,0:T(8,128)(2,1)S(1)}, u32[]{:S(2)}, u32[]{:S(2)}) %collective-permute-start.31) | collective-permute-done | bytes 221216 | tf_op jit(solution)/shard_map/ppermute | solution.py:58
  102.9 9.1 %collective-permute-start.34 = (bf16[40,768]{1,0:T(8,128)(2,1)S(1)}, bf16[40,768]{1,0:T(8,128)(2,1)S(1)}, u32[]{:S(2)}, u32[]{:S(2)}) collective-permute-start(bf16[40,768]{1,0:T(8,128)(2,1)S(1)} %get-tuple-element.76), channel_id=1, source_target_pairs={{0,0},{1,9},{2,2},{3,11},{4,12},{5,5},{6,14},{7,7},{8,8},{9,1},{10... | collective-permute-start | bytes 184328 | tf_op jit(solution)/shard_map/ppermute | solution.py:71
  112.1 3.9 %collective-permute-start.35 = (bf16[40,768]{1,0:T(8,128)(2,1)S(1)}, bf16[40,768]{1,0:T(8,128)(2,1)S(1)}, u32[]{:S(2)}, u32[]{:S(2)}) collective-permute-start(bf16[40,768]{1,0:T(8,128)(2,1)S(1)} %get-tuple-element.77), channel_id=1, source_target_pairs={{0,192},{1,201},{2,194},{3,203},{4,204},{5,197},{6,206},{7,199},{8... | collective-permute-start | bytes 184328 | tf_op jit(solution)/shard_map/ppermute | solution.py:71
  117.3 4.9 %collective-permute-done.36.refs_2_ = bf16[40,768]{1,0:T(8,128)(2,1)S(1)} collective-permute-done((bf16[40,768]{1,0:T(8,128)(2,1)S(1)}, bf16[40,768]{1,0:T(8,128)(2,1)S(1)}, u32[]{:S(2)}, u32[]{:S(2)}) %collective-permute-start.36) | collective-permute-done | bytes 61472 | tf_op jit(solution)/shard_map/ppermute | solution.py:71
  122.7 1.9 %collective-permute-start.39 = (bf16[40,768]{1,0:T(8,128)(2,1)S(1)}, bf16[40,768]{1,0:T(8,128)(2,1)S(1)}, u32[]{:S(2)}, u32[]{:S(2)}) collective-permute-start(bf16[40,768]{1,0:T(8,128)(2,1)S(1)} %shard_map.86), channel_id=1, source_target_pairs={{0,128},{1,137},{2,130},{3,139},{4,140},{5,133},{6,142},{7,135},{8... | collective-permute-start | bytes 184328 | tf_op jit(solution)/shard_map/ppermute | solution.py:71
  124.6 2.0 %collective-permute-start.20 = (f32[16,64]{1,0:T(8,128)S(1)}, f32[16,64]{1,0:T(8,128)S(1)}, u32[]{:S(2)}, u32[]{:S(2)}) collective-permute-start(f32[16,64]{1,0:T(8,128)S(1)} %get-tuple-element.60), channel_id=1, source_target_pairs={{0,0},{1,9},{2,2},{3,11},{4,12},{5,5},{6,14},{7,7},{8,8},{9,1},{10... | collective-permute-start | bytes 12296 | tf_op jit(solution)/shard_map/ppermute | solution.py:71
  127.6 4.1 %collective-permute-done.39.far_ref = bf16[40,768]{1,0:T(8,128)(2,1)S(1)} collective-permute-done((bf16[40,768]{1,0:T(8,128)(2,1)S(1)}, bf16[40,768]{1,0:T(8,128)(2,1)S(1)}, u32[]{:S(2)}, u32[]{:S(2)}) %collective-permute-start.39) | collective-permute-done | bytes 61472 | tf_op jit(solution)/shard_map/ppermute | solution.py:71
  (73 shorter events, 24.2 us)
Async XLA Ops:
  0.0 65.2 %collective-permute-start.15 = (bf16[6144,256]{1,0:T(8,128)(2,1)}, bf16[6144,256]{1,0:T(8,128)(2,1)S(1)}, u32[]{:S(2)}, u32[]{:S(2)}) collective-permute-start(bf16[6144,256]{1,0:T(8,128)(2,1)} %refs_0_.1), channel_id=1, source_target_pairs={{0,8},{8,0},{1,9},{9,1},{2,10},{10,2},{3,11},{11,3},{4,12},{12,4},... | collective-permute-start | bytes 9437192 | tf_op jit(solution)/shard_map/ppermute | solution.py:80
  0.7 65.1 %collective-permute-start.16 = (bf16[6144,256]{1,0:T(8,128)(2,1)}, bf16[6144,256]{1,0:T(8,128)(2,1)S(1)}, u32[]{:S(2)}, u32[]{:S(2)}) collective-permute-start(bf16[6144,256]{1,0:T(8,128)(2,1)} %refs_1_.1), channel_id=1, source_target_pairs={{0,8},{8,0},{1,9},{9,1},{2,10},{10,2},{3,11},{11,3},{4,12},{12,4},... | collective-permute-start | bytes 9437192 | tf_op jit(solution)/shard_map/ppermute | solution.py:80
  0.7 73.7 %collective-permute-start.21 = (bf16[256,6144]{1,0:T(8,128)(2,1)}, bf16[256,6144]{1,0:T(8,128)(2,1)S(1)}, u32[]{:S(2)}, u32[]{:S(2)}) collective-permute-start(bf16[256,6144]{1,0:T(8,128)(2,1)} %refs_7_.1), channel_id=1, source_target_pairs={{0,8},{8,0},{1,9},{9,1},{2,10},{10,2},{3,11},{11,3},{4,12},{12,4},... | collective-permute-start | bytes 9437192 | tf_op jit(solution)/shard_map/ppermute | solution.py:80
  2.3 10.3 %collective-permute-start = (bf16[56,768]{1,0:T(8,128)(2,1)S(1)}, bf16[56,768]{1,0:T(8,128)(2,1)S(1)}, u32[]{:S(2)}, u32[]{:S(2)}) collective-permute-start(bf16[56,768]{1,0:T(8,128)(2,1)S(1)} %get-tuple-element.46), channel_id=1, source_target_pairs={{0,56},{8,48},{16,40},{24,32},{32,24},{40,16},{48,8},{56,0},{1,57}... | collective-permute-start | bytes 258056 | tf_op jit(solution)/shard_map/ppermute | solution.py:76
  5.0 9.0 %collective-permute-start.3 = (bf16[40,768]{1,0:T(8,128)(2,1)S(1)}, bf16[40,768]{1,0:T(8,128)(2,1)S(1)}, u32[]{:S(2)}, u32[]{:S(2)}) collective-permute-start(bf16[40,768]{1,0:T(8,128)(2,1)S(1)} %get-tuple-element.50), channel_id=1, source_target_pairs={{0,128},{1,137},{2,130},{3,139},{4,140},{5,133},{6,142},{7,135},{8... | collective-permute-start | bytes 184328 | tf_op jit(solution)/shard_map/ppermute | solution.py:71
  12.8 9.0 %collective-permute-start.2 = (bf16[40,768]{1,0:T(8,128)(2,1)S(1)}, bf16[40,768]{1,0:T(8,128)(2,1)S(1)}, u32[]{:S(2)}, u32[]{:S(2)}) collective-permute-start(bf16[40,768]{1,0:T(8,128)(2,1)S(1)} %get-tuple-element.49), channel_id=1, source_target_pairs={{0,64},{1,73},{2,66},{3,75},{4,76},{5,69},{6,78},{7,71},{8,72},{9,... | collective-permute-start | bytes 184328 | tf_op jit(solution)/shard_map/ppermute | solution.py:71
  19.2 7.9 %collective-permute-start.1 = (bf16[48,768]{1,0:T(8,128)(2,1)S(1)}, bf16[48,768]{1,0:T(8,128)(2,1)S(1)}, u32[]{:S(2)}, u32[]{:S(2)}) collective-permute-start(bf16[48,768]{1,0:T(8,128)(2,1)S(1)} %get-tuple-element.48), channel_id=1, source_target_pairs={{0,0},{1,9},{2,2},{3,11},{4,12},{5,5},{6,14},{7,7},{8,8},{9,1},{10... | collective-permute-start | bytes 221192 | tf_op jit(solution)/shard_map/ppermute | solution.py:71
  27.3 6.8 %collective-permute-start.8 = (bf16[152,768]{1,0:T(8,128)(2,1)S(1)}, bf16[152,768]{1,0:T(8,128)(2,1)S(1)}, u32[]{:S(2)}, u32[]{:S(2)}) collective-permute-start(bf16[152,768]{1,0:T(8,128)(2,1)S(1)} %shard_map.75.refs_0_), channel_id=1, source_target_pairs={{0,9},{8,16},{9,2},{1,25},{2,11},{10,18},{11,0},{3,27},{12,5},{4,2... | collective-permute-start | bytes 700424 | tf_op jit(solution)/shard_map/ppermute | solution.py:58
  28.0 8.0 %collective-permute-start.9 = (bf16[152,768]{1,0:T(8,128)(2,1)S(1)}, bf16[152,768]{1,0:T(8,128)(2,1)S(1)}, u32[]{:S(2)}, u32[]{:S(2)}) collective-permute-start(bf16[152,768]{1,0:T(8,128)(2,1)S(1)} %shard_map.75.refs_0_), channel_id=1, source_target_pairs={{0,11},{8,4},{9,0},{1,13},{2,9},{10,6},{11,2},{3,15},{12,7},{4,8},... | collective-permute-start | bytes 700424 | tf_op jit(solution)/shard_map/ppermute | solution.py:58
  34.1 7.1 %collective-permute-start.12 = (bf16[152,768]{1,0:T(8,128)(2,1)S(1)}, bf16[152,768]{1,0:T(8,128)(2,1)S(1)}, u32[]{:S(2)}, u32[]{:S(2)}) collective-permute-start(bf16[152,768]{1,0:T(8,128)(2,1)S(1)} %shard_map.75.refs_0_), channel_id=1, source_target_pairs={{0,2},{8,28},{9,11},{1,21},{2,0},{10,30},{11,9},{3,23},{12,14},{4,... | collective-permute-start | bytes 700424 | tf_op jit(solution)/shard_map/ppermute | solution.py:58
  35.9 9.5 %collective-permute-start.6 = (bf16[152,768]{1,0:T(8,128)(2,1)S(1)}, bf16[152,768]{1,0:T(8,128)(2,1)S(1)}, u32[]{:S(2)}, u32[]{:S(2)}) collective-permute-start(bf16[152,768]{1,0:T(8,128)(2,1)S(1)} %shard_map.75.refs_0_), channel_id=1, source_target_pairs={{0,24},{8,1},{9,17},{1,10},{2,26},{10,3},{11,19},{3,8},{12,20},{4,... | collective-permute-start | bytes 700424 | tf_op jit(solution)/shard_map/ppermute | solution.py:58
  41.2 8.4 %collective-permute-start.18 = (bf16[152,768]{1,0:T(8,128)(2,1)S(1)}, bf16[152,768]{1,0:T(8,128)(2,1)S(1)}, u32[]{:S(2)}, u32[]{:S(2)}) collective-permute-start(bf16[152,768]{1,0:T(8,128)(2,1)S(1)} %shard_map.75.refs_0_), channel_id=1, source_target_pairs={{0,12},{8,3},{9,5},{1,8},{2,14},{10,1},{11,7},{3,10},{12,0},{4,15}... | collective-permute-start | bytes 700424 | tf_op jit(solution)/shard_map/ppermute | solution.py:58
  51.3 9.0 %collective-permute-start.10 = (bf16[2,152,768]{2,1,0:T(8,128)(2,1)S(1)}, bf16[2,152,768]{2,1,0:T(8,128)(2,1)S(1)}, u32[]{:S(2)}, u32[]{:S(2)}) collective-permute-start(bf16[2,152,768]{2,1,0:T(8,128)(2,1)S(1)} %shard_map.76), channel_id=1, source_target_pairs={{0,12},{8,3},{9,5},{1,8},{2,14},{10,1},{11,7},{3,10},{12,0},{4,15}... | collective-permute-start | bytes 1400840 | tf_op jit(solution)/shard_map/ppermute | solution.py:58
  55.3 8.7 %collective-permute-start.17 = (bf16[2,152,768]{2,1,0:T(8,128)(2,1)S(1)}, bf16[2,152,768]{2,1,0:T(8,128)(2,1)S(1)}, u32[]{:S(2)}, u32[]{:S(2)}) collective-permute-start(bf16[2,152,768]{2,1,0:T(8,128)(2,1)S(1)} %shard_map.76), channel_id=1, source_target_pairs={{0,24},{8,1},{9,17},{1,10},{2,26},{10,3},{11,19},{3,8},{12,20},{4,... | collective-permute-start | bytes 1400840 | tf_op jit(solution)/shard_map/ppermute | solution.py:58
  60.3 12.1 %collective-permute-start.11 = (bf16[2,152,768]{2,1,0:T(8,128)(2,1)S(1)}, bf16[2,152,768]{2,1,0:T(8,128)(2,1)S(1)}, u32[]{:S(2)}, u32[]{:S(2)}) collective-permute-start(bf16[2,152,768]{2,1,0:T(8,128)(2,1)S(1)} %collective-permute-done.10.refs_6_), channel_id=1, source_target_pairs={{0,24},{8,3},{9,17},{1,8},{2,26},{10,1},{11,19},{3,10},{12,20},{4,... | collective-permute-start | bytes 1400840 | tf_op jit(solution)/shard_map/ppermute | solution.py:58
  65.2 7.1 %collective-permute-start.14 = (bf16[152,768]{1,0:T(8,128)(2,1)S(1)}, bf16[152,768]{1,0:T(8,128)(2,1)S(1)}, u32[]{:S(2)}, u32[]{:S(2)}) collective-permute-start(bf16[152,768]{1,0:T(8,128)(2,1)S(1)} %collective-permute-done.13.refs_5_), channel_id=1, source_target_pairs={{0,12},{8,1},{9,5},{1,10},{2,14},{10,3},{11,7},{3,8},{12,0},{4,13}... | collective-permute-start | bytes 700424 | tf_op jit(solution)/shard_map/ppermute | solution.py:58
  75.6 8.1 %collective-permute-start.28 = (bf16[288,768]{1,0:T(8,128)(2,1)S(1)}, bf16[288,768]{1,0:T(8,128)(2,1)S(1)}, u32[]{:S(2)}, u32[]{:S(2)}) collective-permute-start(bf16[288,768]{1,0:T(8,128)(2,1)S(1)} %get-tuple-element.72), channel_id=1, source_target_pairs={{0,24},{8,1},{9,17},{1,10},{2,26},{10,3},{11,19},{3,8},{12,20},{4,... | collective-permute-start | bytes 1327112 | tf_op jit(solution)/shard_map/ppermute | solution.py:58
  77.2 9.5 %collective-permute-start.22 = (bf16[288,768]{1,0:T(8,128)(2,1)S(1)}, bf16[288,768]{1,0:T(8,128)(2,1)S(1)}, u32[]{:S(2)}, u32[]{:S(2)}) collective-permute-start(bf16[288,768]{1,0:T(8,128)(2,1)S(1)} %get-tuple-element.65), channel_id=1, source_target_pairs={{0,12},{8,3},{9,5},{1,8},{2,14},{10,1},{11,7},{3,10},{12,0},{4,15}... | collective-permute-start | bytes 1327112 | tf_op jit(solution)/shard_map/ppermute | solution.py:58
  80.9 8.1 %collective-permute-start.30 = (bf16[288,768]{1,0:T(8,128)(2,1)S(1)}, bf16[288,768]{1,0:T(8,128)(2,1)S(1)}, u32[]{:S(2)}, u32[]{:S(2)}) collective-permute-start(bf16[288,768]{1,0:T(8,128)(2,1)S(1)} %get-tuple-element.73), channel_id=1, source_target_pairs={{0,24},{8,3},{9,17},{1,8},{2,26},{10,1},{11,19},{3,10},{12,20},{4,... | collective-permute-start | bytes 1327112 | tf_op jit(solution)/shard_map/ppermute | solution.py:58
  84.8 7.1 %collective-permute-start.29 = (bf16[144,768]{1,0:T(8,128)(2,1)S(1)}, bf16[144,768]{1,0:T(8,128)(2,1)S(1)}, u32[]{:S(2)}, u32[]{:S(2)}) collective-permute-start(bf16[144,768]{1,0:T(8,128)(2,1)S(1)} %shard_map.80), channel_id=1, source_target_pairs={{0,12},{8,1},{9,5},{1,10},{2,14},{10,3},{11,7},{3,8},{12,0},{4,13}... | collective-permute-start | bytes 663560 | tf_op jit(solution)/shard_map/ppermute | solution.py:58
  85.8 8.5 %collective-permute-start.26 = (bf16[144,768]{1,0:T(8,128)(2,1)S(1)}, bf16[144,768]{1,0:T(8,128)(2,1)S(1)}, u32[]{:S(2)}, u32[]{:S(2)}) collective-permute-start(bf16[144,768]{1,0:T(8,128)(2,1)S(1)} %get-tuple-element.69), channel_id=1, source_target_pairs={{0,12},{8,1},{9,5},{1,10},{2,14},{10,3},{11,7},{3,8},{12,0},{4,13}... | collective-permute-start | bytes 663560 | tf_op jit(solution)/shard_map/ppermute | solution.py:58
  86.7 7.6 %collective-permute-start.25 = (bf16[144,768]{1,0:T(8,128)(2,1)S(1)}, bf16[144,768]{1,0:T(8,128)(2,1)S(1)}, u32[]{:S(2)}, u32[]{:S(2)}) collective-permute-start(bf16[144,768]{1,0:T(8,128)(2,1)S(1)} %shard_map.78), channel_id=1, source_target_pairs={{0,24},{8,3},{9,17},{1,8},{2,26},{10,1},{11,19},{3,10},{12,20},{4,... | collective-permute-start | bytes 663560 | tf_op jit(solution)/shard_map/ppermute | solution.py:58
  89.0 8.4 %collective-permute-start.24 = (bf16[144,768]{1,0:T(8,128)(2,1)S(1)}, bf16[144,768]{1,0:T(8,128)(2,1)S(1)}, u32[]{:S(2)}, u32[]{:S(2)}) collective-permute-start(bf16[144,768]{1,0:T(8,128)(2,1)S(1)} %get-tuple-element.66), channel_id=1, source_target_pairs={{0,12},{8,1},{9,5},{1,10},{2,14},{10,3},{11,7},{3,8},{12,0},{4,13}... | collective-permute-start | bytes 663560 | tf_op jit(solution)/shard_map/ppermute | solution.py:58
  89.5 7.9 %collective-permute-start.23 = (bf16[144,768]{1,0:T(8,128)(2,1)S(1)}, bf16[144,768]{1,0:T(8,128)(2,1)S(1)}, u32[]{:S(2)}, u32[]{:S(2)}) collective-permute-start(bf16[144,768]{1,0:T(8,128)(2,1)S(1)} %shard_map.77), channel_id=1, source_target_pairs={{0,24},{8,3},{9,17},{1,8},{2,26},{10,1},{11,19},{3,10},{12,20},{4,... | collective-permute-start | bytes 663560 | tf_op jit(solution)/shard_map/ppermute | solution.py:58
  91.9 7.9 %collective-permute-start.33 = (bf16[144,768]{1,0:T(8,128)(2,1)S(1)}, bf16[144,768]{1,0:T(8,128)(2,1)S(1)}, u32[]{:S(2)}, u32[]{:S(2)}) collective-permute-start(bf16[144,768]{1,0:T(8,128)(2,1)S(1)} %shard_map.83), channel_id=1, source_target_pairs={{0,2},{8,28},{9,11},{1,21},{2,0},{10,30},{11,9},{3,23},{12,14},{4,... | collective-permute-start | bytes 663560 | tf_op jit(solution)/shard_map/ppermute | solution.py:58
  94.3 8.3 %collective-permute-start.31 = (bf16[144,768]{1,0:T(8,128)(2,1)S(1)}, bf16[144,768]{1,0:T(8,128)(2,1)S(1)}, u32[]{:S(2)}, u32[]{:S(2)}) collective-permute-start(bf16[144,768]{1,0:T(8,128)(2,1)S(1)} %shard_map.81), channel_id=1, source_target_pairs={{0,9},{8,4},{9,2},{1,13},{2,11},{10,6},{11,0},{3,15},{12,5},{4,8},... | collective-permute-start | bytes 663560 | tf_op jit(solution)/shard_map/ppermute | solution.py:58
  94.4 8.2 %collective-permute-start.27 = (bf16[144,768]{1,0:T(8,128)(2,1)S(1)}, bf16[144,768]{1,0:T(8,128)(2,1)S(1)}, u32[]{:S(2)}, u32[]{:S(2)}) collective-permute-start(bf16[144,768]{1,0:T(8,128)(2,1)S(1)} %shard_map.79), channel_id=1, source_target_pairs={{0,11},{8,16},{9,0},{1,25},{2,9},{10,18},{11,2},{3,27},{12,7},{4,2... | collective-permute-start | bytes 663560 | tf_op jit(solution)/shard_map/ppermute | solution.py:58
  102.9 13.0 %collective-permute-start.34 = (bf16[40,768]{1,0:T(8,128)(2,1)S(1)}, bf16[40,768]{1,0:T(8,128)(2,1)S(1)}, u32[]{:S(2)}, u32[]{:S(2)}) collective-permute-start(bf16[40,768]{1,0:T(8,128)(2,1)S(1)} %get-tuple-element.76), channel_id=1, source_target_pairs={{0,0},{1,9},{2,2},{3,11},{4,12},{5,5},{6,14},{7,7},{8,8},{9,1},{10... | collective-permute-start | bytes 184328 | tf_op jit(solution)/shard_map/ppermute | solution.py:71
  115.9 6.3 %collective-permute-start.36 = (bf16[40,768]{1,0:T(8,128)(2,1)S(1)}, bf16[40,768]{1,0:T(8,128)(2,1)S(1)}, u32[]{:S(2)}, u32[]{:S(2)}) collective-permute-start(bf16[40,768]{1,0:T(8,128)(2,1)S(1)} %get-tuple-element.78), channel_id=1, source_target_pairs={{0,64},{1,73},{2,66},{3,75},{4,76},{5,69},{6,78},{7,71},{8,72},{9,... | collective-permute-start | bytes 184328 | tf_op jit(solution)/shard_map/ppermute | solution.py:71
  115.9 6.6 %collective-permute-start.38 = (bf16[24,768]{1,0:T(8,128)(2,1)S(1)}, bf16[24,768]{1,0:T(8,128)(2,1)S(1)}, u32[]{:S(2)}, u32[]{:S(2)}) collective-permute-start(bf16[24,768]{1,0:T(8,128)(2,1)S(1)} %get-tuple-element.82), channel_id=1, source_target_pairs={{0,56},{8,48},{16,40},{24,32},{32,24},{40,16},{48,8},{56,0},{1,57}... | collective-permute-start | bytes 110600 | tf_op jit(solution)/shard_map/ppermute | solution.py:76
  122.4 9.3 %collective-permute-start.37 = (bf16[56,768]{1,0:T(8,128)(2,1)S(1)}, bf16[56,768]{1,0:T(8,128)(2,1)S(1)}, u32[]{:S(2)}, u32[]{:S(2)}) collective-permute-start(bf16[56,768]{1,0:T(8,128)(2,1)S(1)} %get-tuple-element.80), channel_id=1, source_target_pairs={{0,56},{8,48},{16,40},{24,32},{32,24},{40,16},{48,8},{56,0},{1,57}... | collective-permute-start | bytes 258056 | tf_op jit(solution)/shard_map/ppermute | solution.py:76
  122.7 9.1 %collective-permute-start.39 = (bf16[40,768]{1,0:T(8,128)(2,1)S(1)}, bf16[40,768]{1,0:T(8,128)(2,1)S(1)}, u32[]{:S(2)}, u32[]{:S(2)}) collective-permute-start(bf16[40,768]{1,0:T(8,128)(2,1)S(1)} %shard_map.86), channel_id=1, source_target_pairs={{0,128},{1,137},{2,130},{3,139},{4,140},{5,133},{6,142},{7,135},{8... | collective-permute-start | bytes 184328 | tf_op jit(solution)/shard_map/ppermute | solution.py:71
  (9 other events, 87.1 us)

commit v6 on v5

--- a/solution.py
+++ b/solution.py
@@ -355,7 +355,7 @@
     return parts[0] + parts[1], parts[2] + parts[3]
 
 
-def combine_kernel(width_all, ids_ref, sums_ref, keep_ref, came_ref, far_ref, out_ref):
+def gates_kernel(width_all, ids_ref, sums_ref, *out_refs):
     ids = ids_ref[...]
     sums = sums_ref[...]
     experts = sums.shape[0] // 2
@@ -370,10 +370,15 @@
     gate_second = 1.0 / (1.0 + jnp.exp(logits[0] - logits[1]))
     first, second = slots_of(ids)
     weights = jnp.where(first, gate_first, 0.0) + jnp.where(second, gate_second, 0.0)
+    for out, part in zip(out_refs, halves(weights)):
+        out[...] = part
+
+
+def combine_kernel(high_ref, low_ref, keep_ref, came_ref, far_ref, out_ref):
     rows = jnp.concatenate([keep_ref[...], came_ref[...], far_ref[...]], axis=0)
     out_ref[...] = sum(
-        lax.dot_general(w, rows, (((0,), (0,)), ((), ())), preferred_element_type=F32)
-        for w in halves(weights)
+        lax.dot_general(w[...], rows, (((0,), (0,)), ((), ())), preferred_element_type=F32)
+        for w in (high_ref, low_ref)
     ).astype(BF16)
 
 
@@ -395,8 +400,8 @@
 
 CHUNK = 48
 FIRST = ((0, 0), (0, 1), (0, 2), (0, 3), (1, 0), (1, 3), (2, 1), (2, 2))
-SECOND = ((1, 1), (1, 2), (2, 0), (2, 3))
-LAST = ((3, 0), (3, 1), (3, 2), (3, 3))
+SECOND = ((1, 1), (1, 2), (2, 0), (2, 3), (3, 0))
+LAST = ((3, 1), (3, 2), (3, 3))
 
 
 def prepare(tile, gain, out_ref, row_start, column_at, squares_ref, squares_start):
@@ -719,14 +724,16 @@
     far = along_z(far, 2)
     keep, send = small(unshuffle_kernel, [(NEAR, width)] * 2, stay, one, three)
     came = across_y(send)
+    slots = (2 * NEAR + BLOCK, tokens.shape[0])
+    gates = small(partial(gates_kernel, width_all), [slots] * 2, ids, sums)
     return pl.pallas_call(
-        partial(combine_kernel, width_all),
+        combine_kernel,
         out_shape=jax.ShapeDtypeStruct(tokens.shape, BF16),
         in_specs=vmem(5),
         out_specs=vmem(1)[0],
         compiler_params=pltpu.CompilerParams(vmem_limit_bytes=4 << 20),
         name="combine",
-    )(ids, sums, keep, came, far)
+    )(*gates, keep, came, far)
 
 
 def solution(mesh):

time: 133 us -> 135 us (1.015)
  waiting for transfers between devices: 52.2 us -> 54.8 us
    ppermute x24, waiting for transfers between devices: 35.3 us -> 37.5 us  [hop(): return lax.ppermute(value, OWNER, owner_pairs(step_core0, step_core1))]
where the time goes in v6:
time: 135 us
  starting transfers between devices  61.3 us (45%)
  waiting for transfers between devices  54.8 us (41%)
  Pallas kernels  18.1 us (13%)
    ppermute x24, waiting for transfers between devices, hop(): return lax.ppermute(value, OWNER, owner_pairs(step_core0, step_core1))  37.5 us
    ppermute x9, starting transfers between devices, along_z(): return lax.ppermute(value, ('zh', 'c', 'zl', 'x'), pairs)  30.8 us
    ppermute x24, starting transfers between devices, hop(): return lax.ppermute(value, OWNER, owner_pairs(step_core0, step_core1))  25.3 us
    ppermute x9, waiting for transfers between devices, along_z(): return lax.ppermute(value, ('zh', 'c', 'zl', 'x'), pairs)  13.3 us
    pallas_call x1, Pallas kernels, early_of(): pl.pallas_call(partial(early_kernel, where), out_shape=[jax.ShapeDtypeStr...  4.27 us
    ppermute x4, waiting for transfers between devices, across_y(): return lax.ppermute(value, ('y2', 'y1', 'c'), pairs)  4.12 us
    ppermute x4, starting transfers between devices, across_y(): return lax.ppermute(value, ('y2', 'y1', 'c'), pairs)  4.05 us
    pallas_call x2, Pallas kernels, down_of(): pl.pallas_call(partial(down_kernel, far, places), out_shape=[jax.ShapeDty...  3.58 us
  transfers between devices with their start and end apart: 40, of which 20 were waited for; matrix products, arithmetic and copies ran while one was open for 0% of the time, Pallas kernels for 12%

profile of v6, /device:TPU:33, one launch (start us, length us, event | category | flops | bytes accessed | tf_op | source)
XLA Modules:
  0.0 134.5 jit_solution(2213907673827637195)
XLA Ops:
  2.3 2.7 %collective-permute-start = (bf16[56,768]{1,0:T(8,128)(2,1)S(1)}, bf16[56,768]{1,0:T(8,128)(2,1)S(1)}, u32[]{:S(2)}, u32[]{:S(2)}) collective-permute-start(bf16[56,768]{1,0:T(8,128)(2,1)S(1)} %get-tuple-element.48), channel_id=1, source_target_pairs={{0,56},{8,48},{16,40},{24,32},{32,24},{40,16},{48,8},{56,0},{1,57}... | collective-permute-start | bytes 258056 | tf_op jit(solution)/shard_map/ppermute | solution.py:76
  5.0 6.4 %collective-permute-start.3 = (bf16[40,768]{1,0:T(8,128)(2,1)S(1)}, bf16[40,768]{1,0:T(8,128)(2,1)S(1)}, u32[]{:S(2)}, u32[]{:S(2)}) collective-permute-start(bf16[40,768]{1,0:T(8,128)(2,1)S(1)} %get-tuple-element.52), channel_id=1, source_target_pairs={{0,128},{1,137},{2,130},{3,139},{4,140},{5,133},{6,142},{7,135},{8... | collective-permute-start | bytes 184328 | tf_op jit(solution)/shard_map/ppermute | solution.py:71
  15.1 4.1 %collective-permute-done.5.crossed_ref = bf16[24,768]{1,0:T(8,128)(2,1)S(1)} collective-permute-done((bf16[24,768]{1,0:T(8,128)(2,1)S(1)}, bf16[24,768]{1,0:T(8,128)(2,1)S(1)}, u32[]{:S(2)}, u32[]{:S(2)}) %collective-permute-start.5) | collective-permute-done | bytes 36896 | tf_op jit(solution)/shard_map/ppermute | solution.py:76
  19.2 2.6 %collective-permute-start.1 = (bf16[48,768]{1,0:T(8,128)(2,1)S(1)}, bf16[48,768]{1,0:T(8,128)(2,1)S(1)}, u32[]{:S(2)}, u32[]{:S(2)}) collective-permute-start(bf16[48,768]{1,0:T(8,128)(2,1)S(1)} %get-tuple-element.50), channel_id=1, source_target_pairs={{0,0},{1,9},{2,2},{3,11},{4,12},{5,5},{6,14},{7,7},{8,8},{9,1},{10... | collective-permute-start | bytes 221192 | tf_op jit(solution)/shard_map/ppermute | solution.py:71
  21.8 4.0 %collective-permute-start.4 = (bf16[40,768]{1,0:T(8,128)(2,1)S(1)}, bf16[40,768]{1,0:T(8,128)(2,1)S(1)}, u32[]{:S(2)}, u32[]{:S(2)}) collective-permute-start(bf16[40,768]{1,0:T(8,128)(2,1)S(1)} %get-tuple-element.53), channel_id=1, source_target_pairs={{0,192},{1,201},{2,194},{3,203},{4,204},{5,197},{6,206},{7,199},{8... | collective-permute-start | bytes 184328 | tf_op jit(solution)/shard_map/ppermute | solution.py:71
  28.0 2.4 %collective-permute-start.7 = (bf16[152,768]{1,0:T(8,128)(2,1)S(1)}, bf16[152,768]{1,0:T(8,128)(2,1)S(1)}, u32[]{:S(2)}, u32[]{:S(2)}) collective-permute-start(bf16[152,768]{1,0:T(8,128)(2,1)S(1)} %shard_map.75.refs_0_), channel_id=1, source_target_pairs={{0,11},{8,4},{9,0},{1,13},{2,9},{10,6},{11,2},{3,15},{12,7},{4,8},... | collective-permute-start | bytes 700424 | tf_op jit(solution)/shard_map/ppermute | solution.py:58
  30.4 3.7 %collective-permute-done.6.first_ref.refs_1_ = bf16[152,768]{1,0:T(8,128)(2,1)S(1)} collective-permute-done((bf16[152,768]{1,0:T(8,128)(2,1)S(1)}, bf16[152,768]{1,0:T(8,128)(2,1)S(1)}, u32[]{:S(2)}, u32[]{:S(2)}) %collective-permute-start.6) | collective-permute-done | bytes 233504 | tf_op jit(solution)/shard_map/ppermute | solution.py:58
  34.1 1.8 %collective-permute-start.10 = (bf16[152,768]{1,0:T(8,128)(2,1)S(1)}, bf16[152,768]{1,0:T(8,128)(2,1)S(1)}, u32[]{:S(2)}, u32[]{:S(2)}) collective-permute-start(bf16[152,768]{1,0:T(8,128)(2,1)S(1)} %shard_map.75.refs_0_), channel_id=1, source_target_pairs={{0,2},{8,28},{9,11},{1,21},{2,0},{10,30},{11,9},{3,23},{12,14},{4,... | collective-permute-start | bytes 700424 | tf_op jit(solution)/shard_map/ppermute | solution.py:58
  35.9 5.2 %collective-permute-done.10.refs_3_ = bf16[152,768]{1,0:T(8,128)(2,1)S(1)} collective-permute-done((bf16[152,768]{1,0:T(8,128)(2,1)S(1)}, bf16[152,768]{1,0:T(8,128)(2,1)S(1)}, u32[]{:S(2)}, u32[]{:S(2)}) %collective-permute-start.10) | collective-permute-done | bytes 233504 | tf_op jit(solution)/shard_map/ppermute | solution.py:58
  41.2 4.3 %collective-permute-start.16 = (bf16[152,768]{1,0:T(8,128)(2,1)S(1)}, bf16[152,768]{1,0:T(8,128)(2,1)S(1)}, u32[]{:S(2)}, u32[]{:S(2)}) collective-permute-start(bf16[152,768]{1,0:T(8,128)(2,1)S(1)} %shard_map.75.refs_0_), channel_id=1, source_target_pairs={{0,12},{8,3},{9,5},{1,8},{2,14},{10,1},{11,7},{3,10},{12,0},{4,15}... | collective-permute-start | bytes 700424 | tf_op jit(solution)/shard_map/ppermute | solution.py:58
  45.5 4.0 %collective-permute-done.16.refs_1_ = bf16[152,768]{1,0:T(8,128)(2,1)S(1)} collective-permute-done((bf16[152,768]{1,0:T(8,128)(2,1)S(1)}, bf16[152,768]{1,0:T(8,128)(2,1)S(1)}, u32[]{:S(2)}, u32[]{:S(2)}) %collective-permute-start.16) | collective-permute-done | bytes 233504 | tf_op jit(solution)/shard_map/ppermute | solution.py:58
  49.5 1.4 %collective-permute-start.17 = (bf16[152,768]{1,0:T(8,128)(2,1)S(1)}, bf16[152,768]{1,0:T(8,128)(2,1)S(1)}, u32[]{:S(2)}, u32[]{:S(2)}) collective-permute-start(bf16[152,768]{1,0:T(8,128)(2,1)S(1)} %collective-permute-done.10.refs_3_), channel_id=1, source_target_pairs={{0,12},{8,3},{9,5},{1,8},{2,14},{10,1},{11,7},{3,10},{12,0},{4,15}... | collective-permute-start | bytes 700424 | tf_op jit(solution)/shard_map/ppermute | solution.py:58
  51.3 4.0 %collective-permute-done.17.refs_2_ = bf16[152,768]{1,0:T(8,128)(2,1)S(1)} collective-permute-done((bf16[152,768]{1,0:T(8,128)(2,1)S(1)}, bf16[152,768]{1,0:T(8,128)(2,1)S(1)}, u32[]{:S(2)}, u32[]{:S(2)}) %collective-permute-start.17) | collective-permute-done | bytes 233504 | tf_op jit(solution)/shard_map/ppermute | solution.py:58
  57.8 5.8 %collective-permute-done.8.refs_6_ = bf16[2,152,768]{2,1,0:T(8,128)(2,1)S(1)} collective-permute-done((bf16[2,152,768]{2,1,0:T(8,128)(2,1)S(1)}, bf16[2,152,768]{2,1,0:T(8,128)(2,1)S(1)}, u32[]{:S(2)}, u32[]{:S(2)}) %collective-permute-start.8) | collective-permute-done | bytes 466976 | tf_op jit(solution)/shard_map/ppermute | solution.py:58
  63.6 2.9 %fetch.1 = (bf16[6144,256]{1,0:T(8,128)(2,1)S(1)}, bf16[6144,256]{1,0:T(8,128)(2,1)S(1)}) custom-call(bf16[6144,256]{1,0:T(8,128)(2,1)} %refs_0_.1, bf16[6144,256]{1,0:T(8,128)(2,1)} %refs_1_.1), custom_call_target="tpu_custom_call" | custom-call | tf_op jit(solution)/shard_map/fetch/pallas_call | solution.py:342
  68.2 4.3 %early.1 = (bf16[256,6144]{1,0:T(8,128)(2,1)S(1)}, f32[4,288,256]{2,1,0:T(8,128)S(1)}, bf16[288,6144]{1,0:T(8,128)(2,1)S(1)}, f32[288,128]{1,0:T(8,128)S(1)}, f32[16,64]{1,0:T(8,128)S(1)}) custom-call(f32[1,6144]{1,0:T(1,128)S(1)} %get-tuple-element.46.gain_ref, ...), custom_call_target="tpu_custom_call", output_to_operand_aliasing={{2}: (10, {}), {3}: (11, {}), {4}: (12, {})} | custom-call | flops 3623878656 | bytes 12582912 | tf_op jit(solution)/shard_map/early/pallas_call | solution.py:488
  73.1 1.5 %late.1 = (bf16[288,512]{1,0:T(8,128)(2,1)S(1)}, f32[16,64]{1,0:T(8,128)S(1)}, f32[4,288,256]{2,1,0:T(8,128)S(1)}) custom-call(f32[1,6144]{1,0:T(1,128)S(1)} %get-tuple-element.46.gain_ref, bf16[2,152,768]{2,1,0:T(8,128)(2,1)S(1)} %collective-permute-done.9.refs_0_, ...), custom_call_target="tpu_custom_call", output_to_operand_aliasing={{2}: (7, {})} | custom-call | flops 905969664 | bytes 2359296 | tf_op jit(solution)/shard_map/late/pallas_call | solution.py:543
  75.9 1.5 %collective-permute-start.28 = (bf16[288,768]{1,0:T(8,128)(2,1)S(1)}, bf16[288,768]{1,0:T(8,128)(2,1)S(1)}, u32[]{:S(2)}, u32[]{:S(2)}) collective-permute-start(bf16[288,768]{1,0:T(8,128)(2,1)S(1)} %get-tuple-element.76), channel_id=1, source_target_pairs={{0,24},{8,1},{9,17},{1,10},{2,26},{10,3},{11,19},{3,8},{12,20},{4,... | collective-permute-start | bytes 1327112 | tf_op jit(solution)/shard_map/ppermute | solution.py:58
  78.6 2.3 %rest.1 = (bf16[144,768]{1,0:T(8,128)(2,1)S(1)}, bf16[144,768]{1,0:T(8,128)(2,1)S(1)}, bf16[144,768]{1,0:T(8,128)(2,1)S(1)}, bf16[144,768]{1,0:T(8,128)(2,1)S(1)...) custom-call(bf16[288,512]{1,0:T(8,128)(2,1)S(1)} %get-tuple-element., ...), custom_call_target="tpu_custom_call" | custom-call | flops 1358954496 | bytes 6291456 | tf_op jit(solution)/shard_map/rest/pallas_call | solution.py:616
  81.1 2.9 %collective-permute-done.28.refs_1_ = bf16[288,768]{1,0:T(8,128)(2,1)S(1)} collective-permute-done((bf16[288,768]{1,0:T(8,128)(2,1)S(1)}, bf16[288,768]{1,0:T(8,128)(2,1)S(1)}, u32[]{:S(2)}, u32[]{:S(2)}) %collective-permute-start.28) | collective-permute-done | bytes 442400 | tf_op jit(solution)/shard_map/ppermute | solution.py:58
  86.7 2.3 %collective-permute-start.25 = (bf16[144,768]{1,0:T(8,128)(2,1)S(1)}, bf16[144,768]{1,0:T(8,128)(2,1)S(1)}, u32[]{:S(2)}, u32[]{:S(2)}) collective-permute-start(bf16[144,768]{1,0:T(8,128)(2,1)S(1)} %shard_map.79), channel_id=1, source_target_pairs={{0,24},{8,3},{9,17},{1,8},{2,26},{10,1},{11,19},{3,10},{12,20},{4,... | collective-permute-start | bytes 663560 | tf_op jit(solution)/shard_map/ppermute | solution.py:58
  89.8 1.5 %collective-permute-start.23 = (bf16[144,768]{1,0:T(8,128)(2,1)S(1)}, bf16[144,768]{1,0:T(8,128)(2,1)S(1)}, u32[]{:S(2)}, u32[]{:S(2)}) collective-permute-start(bf16[144,768]{1,0:T(8,128)(2,1)S(1)} %shard_map.78), channel_id=1, source_target_pairs={{0,24},{8,3},{9,17},{1,8},{2,26},{10,1},{11,19},{3,10},{12,20},{4,... | collective-permute-start | bytes 663560 | tf_op jit(solution)/shard_map/ppermute | solution.py:58
  92.3 2.3 %collective-permute-done.26.refs_2_ = bf16[144,768]{1,0:T(8,128)(2,1)S(1)} collective-permute-done((bf16[144,768]{1,0:T(8,128)(2,1)S(1)}, bf16[144,768]{1,0:T(8,128)(2,1)S(1)}, u32[]{:S(2)}, u32[]{:S(2)}) %collective-permute-start.26) | collective-permute-done | bytes 221216 | tf_op jit(solution)/shard_map/ppermute | solution.py:58
  94.6 3.0 %collective-permute-start.27 = (bf16[144,768]{1,0:T(8,128)(2,1)S(1)}, bf16[144,768]{1,0:T(8,128)(2,1)S(1)}, u32[]{:S(2)}, u32[]{:S(2)}) collective-permute-start(bf16[144,768]{1,0:T(8,128)(2,1)S(1)} %shard_map.80), channel_id=1, source_target_pairs={{0,11},{8,16},{9,0},{1,25},{2,9},{10,18},{11,2},{3,27},{12,7},{4,2... | collective-permute-start | bytes 663560 | tf_op jit(solution)/shard_map/ppermute | solution.py:58
  97.7 3.2 %collective-permute-done.33.refs_5_ = bf16[144,768]{1,0:T(8,128)(2,1)S(1)} collective-permute-done((bf16[144,768]{1,0:T(8,128)(2,1)S(1)}, bf16[144,768]{1,0:T(8,128)(2,1)S(1)}, u32[]{:S(2)}, u32[]{:S(2)}) %collective-permute-start.33) | collective-permute-done | bytes 221216 | tf_op jit(solution)/shard_map/ppermute | solution.py:58
  100.8 2.9 %collective-permute-done.31.refs_4_ = bf16[144,768]{1,0:T(8,128)(2,1)S(1)} collective-permute-done((bf16[144,768]{1,0:T(8,128)(2,1)S(1)}, bf16[144,768]{1,0:T(8,128)(2,1)S(1)}, u32[]{:S(2)}, u32[]{:S(2)}) %collective-permute-start.31) | collective-permute-done | bytes 221216 | tf_op jit(solution)/shard_map/ppermute | solution.py:58
  104.1 9.5 %collective-permute-start.34 = (bf16[40,768]{1,0:T(8,128)(2,1)S(1)}, bf16[40,768]{1,0:T(8,128)(2,1)S(1)}, u32[]{:S(2)}, u32[]{:S(2)}) collective-permute-start(bf16[40,768]{1,0:T(8,128)(2,1)S(1)} %get-tuple-element.80), channel_id=1, source_target_pairs={{0,0},{1,9},{2,2},{3,11},{4,12},{5,5},{6,14},{7,7},{8,8},{9,1},{10... | collective-permute-start | bytes 184328 | tf_op jit(solution)/shard_map/ppermute | solution.py:71
  113.6 3.8 %collective-permute-start.35 = (bf16[40,768]{1,0:T(8,128)(2,1)S(1)}, bf16[40,768]{1,0:T(8,128)(2,1)S(1)}, u32[]{:S(2)}, u32[]{:S(2)}) collective-permute-start(bf16[40,768]{1,0:T(8,128)(2,1)S(1)} %get-tuple-element.81), channel_id=1, source_target_pairs={{0,192},{1,201},{2,194},{3,203},{4,204},{5,197},{6,206},{7,199},{8... | collective-permute-start | bytes 184328 | tf_op jit(solution)/shard_map/ppermute | solution.py:71
  117.4 1.6 %collective-permute-done.35.refs_1_ = bf16[40,768]{1,0:T(8,128)(2,1)S(1)} collective-permute-done((bf16[40,768]{1,0:T(8,128)(2,1)S(1)}, bf16[40,768]{1,0:T(8,128)(2,1)S(1)}, u32[]{:S(2)}, u32[]{:S(2)}) %collective-permute-start.35) | collective-permute-done | bytes 61472 | tf_op jit(solution)/shard_map/ppermute | solution.py:71
  119.0 5.3 %collective-permute-done.36.refs_2_ = bf16[40,768]{1,0:T(8,128)(2,1)S(1)} collective-permute-done((bf16[40,768]{1,0:T(8,128)(2,1)S(1)}, bf16[40,768]{1,0:T(8,128)(2,1)S(1)}, u32[]{:S(2)}, u32[]{:S(2)}) %collective-permute-start.36) | collective-permute-done | bytes 61472 | tf_op jit(solution)/shard_map/ppermute | solution.py:71
  126.5 1.9 %collective-permute-start.20 = (f32[16,64]{1,0:T(8,128)S(1)}, f32[16,64]{1,0:T(8,128)S(1)}, u32[]{:S(2)}, u32[]{:S(2)}) collective-permute-start(f32[16,64]{1,0:T(8,128)S(1)} %get-tuple-element.62), channel_id=1, source_target_pairs={{0,0},{1,9},{2,2},{3,11},{4,12},{5,5},{6,14},{7,7},{8,8},{9,1},{10... | collective-permute-start | bytes 12296 | tf_op jit(solution)/shard_map/ppermute | solution.py:71
  129.8 3.9 %collective-permute-done.39.far_ref = bf16[40,768]{1,0:T(8,128)(2,1)S(1)} collective-permute-done((bf16[40,768]{1,0:T(8,128)(2,1)S(1)}, bf16[40,768]{1,0:T(8,128)(2,1)S(1)}, u32[]{:S(2)}, u32[]{:S(2)}) %collective-permute-start.39) | collective-permute-done | bytes 61472 | tf_op jit(solution)/shard_map/ppermute | solution.py:71
  (74 shorter events, 25.0 us)
Async XLA Ops:
  0.0 68.2 %collective-permute-start.13 = (bf16[6144,256]{1,0:T(8,128)(2,1)}, bf16[6144,256]{1,0:T(8,128)(2,1)S(1)}, u32[]{:S(2)}, u32[]{:S(2)}) collective-permute-start(bf16[6144,256]{1,0:T(8,128)(2,1)} %refs_0_.1), channel_id=1, source_target_pairs={{0,8},{8,0},{1,9},{9,1},{2,10},{10,2},{3,11},{11,3},{4,12},{12,4},... | collective-permute-start | bytes 9437192 | tf_op jit(solution)/shard_map/ppermute | solution.py:80
  0.7 67.5 %collective-permute-start.14 = (bf16[6144,256]{1,0:T(8,128)(2,1)}, bf16[6144,256]{1,0:T(8,128)(2,1)S(1)}, u32[]{:S(2)}, u32[]{:S(2)}) collective-permute-start(bf16[6144,256]{1,0:T(8,128)(2,1)} %refs_1_.1), channel_id=1, source_target_pairs={{0,8},{8,0},{1,9},{9,1},{2,10},{10,2},{3,11},{11,3},{4,12},{12,4},... | collective-permute-start | bytes 9437192 | tf_op jit(solution)/shard_map/ppermute | solution.py:80
  0.7 74.0 %collective-permute-start.21 = (bf16[256,6144]{1,0:T(8,128)(2,1)}, bf16[256,6144]{1,0:T(8,128)(2,1)S(1)}, u32[]{:S(2)}, u32[]{:S(2)}) collective-permute-start(bf16[256,6144]{1,0:T(8,128)(2,1)} %refs_8_.1), channel_id=1, source_target_pairs={{0,8},{8,0},{1,9},{9,1},{2,10},{10,2},{3,11},{11,3},{4,12},{12,4},... | collective-permute-start | bytes 9437192 | tf_op jit(solution)/shard_map/ppermute | solution.py:80
  2.3 10.3 %collective-permute-start = (bf16[56,768]{1,0:T(8,128)(2,1)S(1)}, bf16[56,768]{1,0:T(8,128)(2,1)S(1)}, u32[]{:S(2)}, u32[]{:S(2)}) collective-permute-start(bf16[56,768]{1,0:T(8,128)(2,1)S(1)} %get-tuple-element.48), channel_id=1, source_target_pairs={{0,56},{8,48},{16,40},{24,32},{32,24},{40,16},{48,8},{56,0},{1,57}... | collective-permute-start | bytes 258056 | tf_op jit(solution)/shard_map/ppermute | solution.py:76
  5.0 9.0 %collective-permute-start.3 = (bf16[40,768]{1,0:T(8,128)(2,1)S(1)}, bf16[40,768]{1,0:T(8,128)(2,1)S(1)}, u32[]{:S(2)}, u32[]{:S(2)}) collective-permute-start(bf16[40,768]{1,0:T(8,128)(2,1)S(1)} %get-tuple-element.52), channel_id=1, source_target_pairs={{0,128},{1,137},{2,130},{3,139},{4,140},{5,133},{6,142},{7,135},{8... | collective-permute-start | bytes 184328 | tf_op jit(solution)/shard_map/ppermute | solution.py:71
  12.8 9.0 %collective-permute-start.2 = (bf16[40,768]{1,0:T(8,128)(2,1)S(1)}, bf16[40,768]{1,0:T(8,128)(2,1)S(1)}, u32[]{:S(2)}, u32[]{:S(2)}) collective-permute-start(bf16[40,768]{1,0:T(8,128)(2,1)S(1)} %get-tuple-element.51), channel_id=1, source_target_pairs={{0,64},{1,73},{2,66},{3,75},{4,76},{5,69},{6,78},{7,71},{8,72},{9,... | collective-permute-start | bytes 184328 | tf_op jit(solution)/shard_map/ppermute | solution.py:71
  19.2 7.9 %collective-permute-start.1 = (bf16[48,768]{1,0:T(8,128)(2,1)S(1)}, bf16[48,768]{1,0:T(8,128)(2,1)S(1)}, u32[]{:S(2)}, u32[]{:S(2)}) collective-permute-start(bf16[48,768]{1,0:T(8,128)(2,1)S(1)} %get-tuple-element.50), channel_id=1, source_target_pairs={{0,0},{1,9},{2,2},{3,11},{4,12},{5,5},{6,14},{7,7},{8,8},{9,1},{10... | collective-permute-start | bytes 221192 | tf_op jit(solution)/shard_map/ppermute | solution.py:71
  27.3 6.8 %collective-permute-start.6 = (bf16[152,768]{1,0:T(8,128)(2,1)S(1)}, bf16[152,768]{1,0:T(8,128)(2,1)S(1)}, u32[]{:S(2)}, u32[]{:S(2)}) collective-permute-start(bf16[152,768]{1,0:T(8,128)(2,1)S(1)} %shard_map.75.refs_0_), channel_id=1, source_target_pairs={{0,9},{8,16},{9,2},{1,25},{2,11},{10,18},{11,0},{3,27},{12,5},{4,2... | collective-permute-start | bytes 700424 | tf_op jit(solution)/shard_map/ppermute | solution.py:58
  28.0 8.0 %collective-permute-start.7 = (bf16[152,768]{1,0:T(8,128)(2,1)S(1)}, bf16[152,768]{1,0:T(8,128)(2,1)S(1)}, u32[]{:S(2)}, u32[]{:S(2)}) collective-permute-start(bf16[152,768]{1,0:T(8,128)(2,1)S(1)} %shard_map.75.refs_0_), channel_id=1, source_target_pairs={{0,11},{8,4},{9,0},{1,13},{2,9},{10,6},{11,2},{3,15},{12,7},{4,8},... | collective-permute-start | bytes 700424 | tf_op jit(solution)/shard_map/ppermute | solution.py:58
  34.1 7.1 %collective-permute-start.10 = (bf16[152,768]{1,0:T(8,128)(2,1)S(1)}, bf16[152,768]{1,0:T(8,128)(2,1)S(1)}, u32[]{:S(2)}, u32[]{:S(2)}) collective-permute-start(bf16[152,768]{1,0:T(8,128)(2,1)S(1)} %shard_map.75.refs_0_), channel_id=1, source_target_pairs={{0,2},{8,28},{9,11},{1,21},{2,0},{10,30},{11,9},{3,23},{12,14},{4,... | collective-permute-start | bytes 700424 | tf_op jit(solution)/shard_map/ppermute | solution.py:58
  35.9 9.5 %collective-permute-start.18 = (bf16[152,768]{1,0:T(8,128)(2,1)S(1)}, bf16[152,768]{1,0:T(8,128)(2,1)S(1)}, u32[]{:S(2)}, u32[]{:S(2)}) collective-permute-start(bf16[152,768]{1,0:T(8,128)(2,1)S(1)} %shard_map.75.refs_0_), channel_id=1, source_target_pairs={{0,24},{8,1},{9,17},{1,10},{2,26},{10,3},{11,19},{3,8},{12,20},{4,... | collective-permute-start | bytes 700424 | tf_op jit(solution)/shard_map/ppermute | solution.py:58
  41.2 8.4 %collective-permute-start.16 = (bf16[152,768]{1,0:T(8,128)(2,1)S(1)}, bf16[152,768]{1,0:T(8,128)(2,1)S(1)}, u32[]{:S(2)}, u32[]{:S(2)}) collective-permute-start(bf16[152,768]{1,0:T(8,128)(2,1)S(1)} %shard_map.75.refs_0_), channel_id=1, source_target_pairs={{0,12},{8,3},{9,5},{1,8},{2,14},{10,1},{11,7},{3,10},{12,0},{4,15}... | collective-permute-start | bytes 700424 | tf_op jit(solution)/shard_map/ppermute | solution.py:58
  51.3 6.5 %collective-permute-start.19 = (bf16[152,768]{1,0:T(8,128)(2,1)S(1)}, bf16[152,768]{1,0:T(8,128)(2,1)S(1)}, u32[]{:S(2)}, u32[]{:S(2)}) collective-permute-start(bf16[152,768]{1,0:T(8,128)(2,1)S(1)} %collective-permute-done.18.refs_4_), channel_id=1, source_target_pairs={{0,12},{8,1},{9,5},{1,10},{2,14},{10,3},{11,7},{3,8},{12,0},{4,13}... | collective-permute-start | bytes 700424 | tf_op jit(solution)/shard_map/ppermute | solution.py:58
  55.3 8.3 %collective-permute-start.8 = (bf16[2,152,768]{2,1,0:T(8,128)(2,1)S(1)}, bf16[2,152,768]{2,1,0:T(8,128)(2,1)S(1)}, u32[]{:S(2)}, u32[]{:S(2)}) collective-permute-start(bf16[2,152,768]{2,1,0:T(8,128)(2,1)S(1)} %shard_map.76), channel_id=1, source_target_pairs={{0,12},{8,3},{9,5},{1,8},{2,14},{10,1},{11,7},{3,10},{12,0},{4,15}... | collective-permute-start | bytes 1400840 | tf_op jit(solution)/shard_map/ppermute | solution.py:58
  57.8 9.5 %collective-permute-start.15 = (bf16[2,152,768]{2,1,0:T(8,128)(2,1)S(1)}, bf16[2,152,768]{2,1,0:T(8,128)(2,1)S(1)}, u32[]{:S(2)}, u32[]{:S(2)}) collective-permute-start(bf16[2,152,768]{2,1,0:T(8,128)(2,1)S(1)} %shard_map.76), channel_id=1, source_target_pairs={{0,24},{8,1},{9,17},{1,10},{2,26},{10,3},{11,19},{3,8},{12,20},{4,... | collective-permute-start | bytes 1400840 | tf_op jit(solution)/shard_map/ppermute | solution.py:58
  63.6 9.6 %collective-permute-start.9 = (bf16[2,152,768]{2,1,0:T(8,128)(2,1)S(1)}, bf16[2,152,768]{2,1,0:T(8,128)(2,1)S(1)}, u32[]{:S(2)}, u32[]{:S(2)}) collective-permute-start(bf16[2,152,768]{2,1,0:T(8,128)(2,1)S(1)} %collective-permute-done.8.refs_6_), channel_id=1, source_target_pairs={{0,24},{8,3},{9,17},{1,8},{2,26},{10,1},{11,19},{3,10},{12,20},{4,... | collective-permute-start | bytes 1400840 | tf_op jit(solution)/shard_map/ppermute | solution.py:58
  75.9 8.1 %collective-permute-start.28 = (bf16[288,768]{1,0:T(8,128)(2,1)S(1)}, bf16[288,768]{1,0:T(8,128)(2,1)S(1)}, u32[]{:S(2)}, u32[]{:S(2)}) collective-permute-start(bf16[288,768]{1,0:T(8,128)(2,1)S(1)} %get-tuple-element.76), channel_id=1, source_target_pairs={{0,24},{8,1},{9,17},{1,10},{2,26},{10,3},{11,19},{3,8},{12,20},{4,... | collective-permute-start | bytes 1327112 | tf_op jit(solution)/shard_map/ppermute | solution.py:58
  77.4 9.2 %collective-permute-start.22 = (bf16[288,768]{1,0:T(8,128)(2,1)S(1)}, bf16[288,768]{1,0:T(8,128)(2,1)S(1)}, u32[]{:S(2)}, u32[]{:S(2)}) collective-permute-start(bf16[288,768]{1,0:T(8,128)(2,1)S(1)} %get-tuple-element.69), channel_id=1, source_target_pairs={{0,12},{8,3},{9,5},{1,8},{2,14},{10,1},{11,7},{3,10},{12,0},{4,15}... | collective-permute-start | bytes 1327112 | tf_op jit(solution)/shard_map/ppermute | solution.py:58
  80.9 8.1 %collective-permute-start.30 = (bf16[288,768]{1,0:T(8,128)(2,1)S(1)}, bf16[288,768]{1,0:T(8,128)(2,1)S(1)}, u32[]{:S(2)}, u32[]{:S(2)}) collective-permute-start(bf16[288,768]{1,0:T(8,128)(2,1)S(1)} %get-tuple-element.77), channel_id=1, source_target_pairs={{0,24},{8,3},{9,17},{1,8},{2,26},{10,1},{11,19},{3,10},{12,20},{4,... | collective-permute-start | bytes 1327112 | tf_op jit(solution)/shard_map/ppermute | solution.py:58
  84.8 7.4 %collective-permute-start.29 = (bf16[144,768]{1,0:T(8,128)(2,1)S(1)}, bf16[144,768]{1,0:T(8,128)(2,1)S(1)}, u32[]{:S(2)}, u32[]{:S(2)}) collective-permute-start(bf16[144,768]{1,0:T(8,128)(2,1)S(1)} %shard_map.81), channel_id=1, source_target_pairs={{0,12},{8,1},{9,5},{1,10},{2,14},{10,3},{11,7},{3,8},{12,0},{4,13}... | collective-permute-start | bytes 663560 | tf_op jit(solution)/shard_map/ppermute | solution.py:58
  86.0 8.5 %collective-permute-start.26 = (bf16[144,768]{1,0:T(8,128)(2,1)S(1)}, bf16[144,768]{1,0:T(8,128)(2,1)S(1)}, u32[]{:S(2)}, u32[]{:S(2)}) collective-permute-start(bf16[144,768]{1,0:T(8,128)(2,1)S(1)} %get-tuple-element.73), channel_id=1, source_target_pairs={{0,12},{8,1},{9,5},{1,10},{2,14},{10,3},{11,7},{3,8},{12,0},{4,13}... | collective-permute-start | bytes 663560 | tf_op jit(solution)/shard_map/ppermute | solution.py:58
  86.7 7.9 %collective-permute-start.25 = (bf16[144,768]{1,0:T(8,128)(2,1)S(1)}, bf16[144,768]{1,0:T(8,128)(2,1)S(1)}, u32[]{:S(2)}, u32[]{:S(2)}) collective-permute-start(bf16[144,768]{1,0:T(8,128)(2,1)S(1)} %shard_map.79), channel_id=1, source_target_pairs={{0,24},{8,3},{9,17},{1,8},{2,26},{10,1},{11,19},{3,10},{12,20},{4,... | collective-permute-start | bytes 663560 | tf_op jit(solution)/shard_map/ppermute | solution.py:58
  89.1 8.6 %collective-permute-start.24 = (bf16[144,768]{1,0:T(8,128)(2,1)S(1)}, bf16[144,768]{1,0:T(8,128)(2,1)S(1)}, u32[]{:S(2)}, u32[]{:S(2)}) collective-permute-start(bf16[144,768]{1,0:T(8,128)(2,1)S(1)} %get-tuple-element.70), channel_id=1, source_target_pairs={{0,12},{8,1},{9,5},{1,10},{2,14},{10,3},{11,7},{3,8},{12,0},{4,13}... | collective-permute-start | bytes 663560 | tf_op jit(solution)/shard_map/ppermute | solution.py:58
  89.8 7.9 %collective-permute-start.23 = (bf16[144,768]{1,0:T(8,128)(2,1)S(1)}, bf16[144,768]{1,0:T(8,128)(2,1)S(1)}, u32[]{:S(2)}, u32[]{:S(2)}) collective-permute-start(bf16[144,768]{1,0:T(8,128)(2,1)S(1)} %shard_map.78), channel_id=1, source_target_pairs={{0,24},{8,3},{9,17},{1,8},{2,26},{10,1},{11,19},{3,10},{12,20},{4,... | collective-permute-start | bytes 663560 | tf_op jit(solution)/shard_map/ppermute | solution.py:58
  92.2 8.7 %collective-permute-start.33 = (bf16[144,768]{1,0:T(8,128)(2,1)S(1)}, bf16[144,768]{1,0:T(8,128)(2,1)S(1)}, u32[]{:S(2)}, u32[]{:S(2)}) collective-permute-start(bf16[144,768]{1,0:T(8,128)(2,1)S(1)} %shard_map.84), channel_id=1, source_target_pairs={{0,2},{8,28},{9,11},{1,21},{2,0},{10,30},{11,9},{3,23},{12,14},{4,... | collective-permute-start | bytes 663560 | tf_op jit(solution)/shard_map/ppermute | solution.py:58
  94.6 9.2 %collective-permute-start.31 = (bf16[144,768]{1,0:T(8,128)(2,1)S(1)}, bf16[144,768]{1,0:T(8,128)(2,1)S(1)}, u32[]{:S(2)}, u32[]{:S(2)}) collective-permute-start(bf16[144,768]{1,0:T(8,128)(2,1)S(1)} %shard_map.82), channel_id=1, source_target_pairs={{0,9},{8,4},{9,2},{1,13},{2,11},{10,6},{11,0},{3,15},{12,5},{4,8},... | collective-permute-start | bytes 663560 | tf_op jit(solution)/shard_map/ppermute | solution.py:58
  94.6 9.1 %collective-permute-start.27 = (bf16[144,768]{1,0:T(8,128)(2,1)S(1)}, bf16[144,768]{1,0:T(8,128)(2,1)S(1)}, u32[]{:S(2)}, u32[]{:S(2)}) collective-permute-start(bf16[144,768]{1,0:T(8,128)(2,1)S(1)} %shard_map.80), channel_id=1, source_target_pairs={{0,11},{8,16},{9,0},{1,25},{2,9},{10,18},{11,2},{3,27},{12,7},{4,2... | collective-permute-start | bytes 663560 | tf_op jit(solution)/shard_map/ppermute | solution.py:58
  104.1 13.3 %collective-permute-start.34 = (bf16[40,768]{1,0:T(8,128)(2,1)S(1)}, bf16[40,768]{1,0:T(8,128)(2,1)S(1)}, u32[]{:S(2)}, u32[]{:S(2)}) collective-permute-start(bf16[40,768]{1,0:T(8,128)(2,1)S(1)} %get-tuple-element.80), channel_id=1, source_target_pairs={{0,0},{1,9},{2,2},{3,11},{4,12},{5,5},{6,14},{7,7},{8,8},{9,1},{10... | collective-permute-start | bytes 184328 | tf_op jit(solution)/shard_map/ppermute | solution.py:71
  117.4 7.0 %collective-permute-start.36 = (bf16[40,768]{1,0:T(8,128)(2,1)S(1)}, bf16[40,768]{1,0:T(8,128)(2,1)S(1)}, u32[]{:S(2)}, u32[]{:S(2)}) collective-permute-start(bf16[40,768]{1,0:T(8,128)(2,1)S(1)} %get-tuple-element.82), channel_id=1, source_target_pairs={{0,64},{1,73},{2,66},{3,75},{4,76},{5,69},{6,78},{7,71},{8,72},{9,... | collective-permute-start | bytes 184328 | tf_op jit(solution)/shard_map/ppermute | solution.py:71
  117.4 7.6 %collective-permute-start.38 = (bf16[24,768]{1,0:T(8,128)(2,1)S(1)}, bf16[24,768]{1,0:T(8,128)(2,1)S(1)}, u32[]{:S(2)}, u32[]{:S(2)}) collective-permute-start(bf16[24,768]{1,0:T(8,128)(2,1)S(1)} %get-tuple-element.86), channel_id=1, source_target_pairs={{0,56},{8,48},{16,40},{24,32},{32,24},{40,16},{48,8},{56,0},{1,57}... | collective-permute-start | bytes 110600 | tf_op jit(solution)/shard_map/ppermute | solution.py:76
  124.6 9.0 %collective-permute-start.37 = (bf16[56,768]{1,0:T(8,128)(2,1)S(1)}, bf16[56,768]{1,0:T(8,128)(2,1)S(1)}, u32[]{:S(2)}, u32[]{:S(2)}) collective-permute-start(bf16[56,768]{1,0:T(8,128)(2,1)S(1)} %get-tuple-element.84), channel_id=1, source_target_pairs={{0,56},{8,48},{16,40},{24,32},{32,24},{40,16},{48,8},{56,0},{1,57}... | collective-permute-start | bytes 258056 | tf_op jit(solution)/shard_map/ppermute | solution.py:76
  125.1 8.5 %collective-permute-start.39 = (bf16[40,768]{1,0:T(8,128)(2,1)S(1)}, bf16[40,768]{1,0:T(8,128)(2,1)S(1)}, u32[]{:S(2)}, u32[]{:S(2)}) collective-permute-start(bf16[40,768]{1,0:T(8,128)(2,1)S(1)} %shard_map.87), channel_id=1, source_target_pairs={{0,128},{1,137},{2,130},{3,139},{4,140},{5,133},{6,142},{7,135},{8... | collective-permute-start | bytes 184328 | tf_op jit(solution)/shard_map/ppermute | solution.py:71
  (9 other events, 84.9 us)
